TPU v7x, 32 devices: a whole 2x2x4 slice. The times are simulated.
32 devices in a mesh: ma: 8 (over z, x), freq: 4 (over y, core).
Axes of the slice: x: 2, y: 2, z: 4, core: 2. Of those that a mesh axis runs over, the one named last changes fastest.
Arguments:
- visibilities: bfloat16 [16, 192, 16, 2, 512], P('ma', None, 'freq')
- eigenmodes: bfloat16 [16, 16, 2, 512, 256], P('ma', 'freq'), may hold values from -0.375 to 0.375
- retained: int32 [16], P('ma'), may hold values from 1 to 256
Outputs:
- coefficients: bfloat16 [16, 2, 192, 256], P('ma')
- filtered: bfloat16 [16, 192, 16, 2, 512], P('ma', None, 'freq')
All inputs are finite; a program needn't handle non-finite values.
Results may differ from a plain program's by a relative error of at most 0.0049.
Values may be sent and summed in bfloat16 or wider, within the bound.
No kernel may reach another device: no remote copies, remote signals or barrier semaphores. Data moves between devices by JAX's collectives and lax.ppermute only.
A program may use at most 128 MiB of HBM per device.

v0:
```python
import jax
import jax.numpy as jnp
from jax import lax
from jax.sharding import PartitionSpec as P


def per_device(visibilities, eigenmodes, retained):
    local_modes, samples, local_freqs, _, base = visibilities.shape
    kmax = eigenmodes.shape[-1]
    width = local_freqs * 2 * base
    flat = visibilities.reshape(local_modes, samples, width)
    swapped = jnp.stack(
        [visibilities[:, :, :, 1, :], -visibilities[:, :, :, 0, :]], axis=3
    ).reshape(local_modes, samples, width)
    matrix = eigenmodes.reshape(local_modes, width, kmax)
    part_re = jnp.einsum("msc,mck->msk", flat, matrix, preferred_element_type=jnp.float32)
    part_im = jnp.einsum("msc,mck->msk", swapped, matrix, preferred_element_type=jnp.float32)
    proj_re, proj_im = lax.psum((part_re, part_im), "freq")
    columns = proj_re.shape[2]
    ranks = jnp.arange(columns, dtype=jnp.int32)
    keep = (ranks[None, :] < retained[:, None]).astype(jnp.float32)
    power = jnp.sum(keep[:, None, :] * (proj_re * proj_re + proj_im * proj_im), axis=(0, 1))
    count = jnp.float32(samples) * jnp.sum(keep, axis=0)
    keep, power, count = (keep, power, count)
    power, count = lax.psum((power, count), "ma")
    scale = 1.0 / jnp.sqrt(power / jnp.maximum(count, 1.0) + 1e-06)
    gain = keep * scale[None, :]
    coef_re = (proj_re * gain[:, None, :]).astype(jnp.bfloat16)
    coef_im = (proj_im * gain[:, None, :]).astype(jnp.bfloat16)
    first = jnp.einsum("msk,mck->msc", coef_re, matrix, preferred_element_type=jnp.float32).reshape(
        local_modes, samples, local_freqs, 2, base
    )
    second = jnp.einsum(
        "msk,mck->msc", coef_im, matrix, preferred_element_type=jnp.float32
    ).reshape(local_modes, samples, local_freqs, 2, base)
    out_re = first[:, :, :, 0, :] - second[:, :, :, 1, :]
    out_im = second[:, :, :, 0, :] + first[:, :, :, 1, :]
    filtered = jnp.stack([out_re, out_im], axis=3).astype(jnp.bfloat16)
    coefficients = jnp.stack([coef_re, coef_im], axis=1)
    return (coefficients, filtered)


def solution(mesh):
    return jax.shard_map(
        per_device,
        mesh=mesh,
        in_specs=(P("ma", None, "freq", None, None), P("ma", "freq", None, None, None), P("ma")),
        out_specs=(P("ma", None, None, None), P("ma", None, "freq", None, None)),
        check_vma=False,
    )
```

profile of v0, /device:TPU:0, one launch (start us, length us, event | category | flops | bytes accessed | tf_op | source)
XLA Modules:
  0.0 165.1 jit_solution(11623645128931911182)
XLA Ops:
  7.2 0.0 copy-start.2
  7.2 0.0 all-reduce.4.cloned.1.call-start
  7.2 6.3 %reshape.62 = bf16[2,192,4096]{2,1,0:T(8,128)(2,1)} reshape(bf16[2,192,4,2,512]{4,3,2,1,0:T(2,128)(2,1)} %param.3) | data formatting | bytes 6291456 | tf_op jit(solution)/shard_map/reshape | solution.py:11
  13.5 0.0 copy-done.2
  13.5 5.8 %fusion.9 = (bf16[2,192,4,1,512]{4,3,2,1,0:T(2,128)(2,1)S(1)}, bf16[2,192,4,1,512]{4,3,2,1,0:T(2,128)(2,1)S(1)}) fusion(bf16[2,192,4,2,512]{4,3,2,1,0:T(2,128)(2,1)S(1)} %copy-done.2), kind=kLoop, calls=%fused_computation.22 | loop fusion | flops 786432 | bytes 6291456 | tf_op jit(solution)/shard_map/slice | solution.py:13
  19.3 8.0 %pad_maximum_fusion = bf16[2,192,4,2,512]{4,3,2,1,0:T(2,128)(2,1)} fusion(bf16[2,192,4,1,512]{4,3,2,1,0:T(2,128)(2,1)S(1)} %get-tuple-element.11, bf16[2,192,4,1,512]{4,3,2,1,0:T(2,128)(2,1)S(1)} %get-tuple-element.10), kind=kLoop, calls=%fused_computation.4 | loop fusion | flops 6291456 | bytes 6291456 | tf_op jit(solution)/shard_map/stack | solution.py:12
  27.3 6.3 %reshape.64 = bf16[2,192,4096]{2,1,0:T(8,128)(2,1)} reshape(bf16[2,192,4,2,512]{4,3,2,1,0:T(2,128)(2,1)} %pad_maximum_fusion) | data formatting | bytes 6291456 | tf_op jit(solution)/shard_map/reshape | solution.py:14
  33.6 0.0 copy-done.3
  33.6 4.1 %fusion.10 = f32[2,192,256]{2,1,0:T(8,128)} fusion(bf16[2,192,4096]{2,1,0:T(8,128)(2,1)S(1)} %copy-done.3, bf16[2,4096,256]{2,1,0:T(8,128)(2,1)} %bitcast.11), kind=kOutput, calls=%fused_computation.23 | convolution fusion | flops 805306368 | bytes 7733248 | tf_op jit(solution)/shard_map/msc,mck->msk/dot_general | solution.py:16
  37.7 0.0 copy-done
  37.7 0.5 copy-done.4
  38.2 1.7 %fusion.11 = f32[2,192,256]{2,1,0:T(8,128)} fusion(bf16[2,192,4096]{2,1,0:T(8,128)(2,1)S(1)} %copy-done.4, bf16[2,4096,256]{2,1,0:T(8,128)(2,1)S(1)} %bitcast.13), kind=kOutput, calls=%fused_computation.24 | convolution fusion | flops 805306368 | bytes 7733248 | tf_op jit(solution)/shard_map/msc,mck->msk/dot_general | solution.py:17
  39.9 0.0 all-reduce.4.cloned.1.call-update
  39.9 0.0 copy-done.6
  39.9 0.1 fusion.8
  40.0 0.1 fusion.7
  40.1 37.8 %all-reduce.4.cloned.1.call-done = (f32[2,192,256]{2,1,0:T(8,128)}, f32[2,192,256]{2,1,0:T(8,128)}) async-done(((f32[2,192,256]{2,1,0:T(8,128)}, f32[2,192,256]{2,1,0:T(8,128)}), (f32[2,192,256]{2,1,0:T(8,128)}, f32[2,192,256]{2,1,0:T(8,128)})) %all-reduce.4.cloned.1.call-update) | async-done | bytes 786448 | tf_op jit(solution)/shard_map/psum | solution.py:18
  77.9 1.2 multiply_reduce_fusion
  79.1 21.5 %all-reduce = (f32[256]{0:T(256)S(1)}, f32[256]{0:T(256)S(1)}) all-reduce(f32[256]{0:T(256)S(1)} %multiply_reduce_fusion, f32[256]{0:T(256)S(1)} %broadcast_multiply_fusion), channel_id=1, replica_groups=mesh['ma'=8,'freq'=4] {'ma'}, use_global_device_ids=true, to_apply=%region_3.0 | all-reduce | flops 512 | bytes 4096 | tf_op jit(solution)/shard_map/psum | solution.py:25
  100.6 0.1 fusion.6
  100.7 1.2 fusion.3
  101.9 0.0 copy-start.1
  101.9 0.0 copy-start.5
  101.9 6.6 %fusion.4 = f32[2,192,4096]{2,1,0:T(8,128)} fusion(bf16[2,4096,256]{2,1,0:T(8,128)(2,1)} %bitcast.12, f32[2,192,256]{2,1,0:T(8,128)} %get-tuple-element.6, f32[2,256]{1,0:T(2,128)S(1)} %fusion.6), kind=kOutput, calls=%fused_computation.13 | convolution fusion | flops 805502976 | bytes 10881024 | tf_op jit(solution)/shard_map/msk,mck->msc/dot_general | solution.py:33
  108.5 0.0 copy-done.1
  108.5 0.0 copy-done.5
  108.5 4.1 %fusion.2 = f32[2,192,4096]{2,1,0:T(8,128)} fusion(bf16[2,4096,256]{2,1,0:T(8,128)(2,1)S(1)} %bitcast.14, f32[2,192,256]{2,1,0:T(8,128)S(1)} %copy-done.5, f32[2,256]{1,0:T(2,128)S(1)} %fusion.6), kind=kOutput, calls=%fused_computation.11 | convolution fusion | flops 805502976 | bytes 10881024 | tf_op jit(solution)/shard_map/msk,mck->msc/dot_general | solution.py:30
  112.7 0.8 copy.5
  113.5 9.2 %reshape.66 = f32[2,192,4,2,512]{4,3,2,1,0:T(2,128)} reshape(f32[2,192,4096]{2,1,0:T(8,128)} %fusion.4) | data formatting | bytes 12582912 | tf_op jit(solution)/shard_map/reshape | solution.py:35
  122.6 9.2 %reshape.65 = f32[2,192,4,2,512]{4,3,2,1,0:T(2,128)} reshape(f32[2,192,4096]{2,1,0:T(8,128)} %fusion.2) | data formatting | bytes 12582912 | tf_op jit(solution)/shard_map/reshape | solution.py:30
  131.8 18.4 %fusion.1 = (bf16[2,192,4,1,512]{4,3,2,1,0:T(2,128)(2,1)S(1)}, bf16[2,192,4,1,512]{4,3,2,1,0:T(2,128)(2,1)S(1)}) fusion(f32[2,192,4,2,512]{4,3,2,1,0:T(2,128)} %reshape.66, f32[2,192,4,2,512]{4,3,2,1,0:T(2,128)} %reshape.65), kind=kLoop, calls=%fused_computation.3 | loop fusion | flops 3145728 | bytes 15728640 | tf_op jit(solution)/shard_map/convert
  150.2 8.0 %pad_maximum_fusion.1 = bf16[2,192,4,2,512]{4,3,2,1,0:T(2,128)(2,1)} fusion(bf16[2,192,4,1,512]{4,3,2,1,0:T(2,128)(2,1)S(1)} %get-tuple-element.9, bf16[2,192,4,1,512]{4,3,2,1,0:T(2,128)(2,1)S(1)} %get-tuple-element.8), kind=kLoop, calls=%fused_computation.5 | loop fusion | flops 6291456 | bytes 6291456 | tf_op jit(solution)/shard_map/stack | solution.py:38
  (7 shorter events, 0.1 us)
Async XLA Ops:
  7.2 6.3 %copy-start.2 = (bf16[2,192,4,2,512]{4,3,2,1,0:T(2,128)(2,1)S(1)}, bf16[2,192,4,2,512]{4,3,2,1,0:T(2,128)(2,1)}, u32[]{:S(2)}) copy-start(bf16[2,192,4,2,512]{4,3,2,1,0:T(2,128)(2,1)} %param.3) | copy-start | bytes 9437188
  7.2 70.7 %all-reduce.4.cloned.1.call-start = ((), (), s32[]{:S(2)}) async-start(), calls=%async_computation | async-start | bytes 1572864 | tf_op jit(solution)/shard_map/psum | solution.py:18
  27.3 6.3 %copy-start.3 = (bf16[2,192,4096]{2,1,0:T(8,128)(2,1)S(1)}, bf16[2,192,4096]{2,1,0:T(8,128)(2,1)}, u32[]{:S(2)}) copy-start(bf16[2,192,4096]{2,1,0:T(8,128)(2,1)} %reshape.62) | copy-start | bytes 9437188
  33.6 4.1 %copy-start = (bf16[2,4,2,512,256]{4,3,2,1,0:T(8,128)(2,1)S(1)}, bf16[2,4,2,512,256]{4,3,2,1,0:T(8,128)(2,1)}, u32[]{:S(2)}) copy-start(bf16[2,4,2,512,256]{4,3,2,1,0:T(8,128)(2,1)} %param.4) | copy-start | bytes 12582916
  33.6 4.6 %copy-start.4 = (bf16[2,192,4096]{2,1,0:T(8,128)(2,1)S(1)}, bf16[2,192,4096]{2,1,0:T(8,128)(2,1)}, u32[]{:S(2)}) copy-start(bf16[2,192,4096]{2,1,0:T(8,128)(2,1)} %reshape.64) | copy-start | bytes 9437188
  38.2 1.8 %copy-start.6 = (s32[2]{0:T(128)S(1)}, s32[2]{0:T(128)}, u32[]{:S(2)}) copy-start(s32[2]{0:T(128)} %param.5) | copy-start | bytes 28
  101.9 6.7 %copy-start.1 = (bf16[2,4,2,512,256]{4,3,2,1,0:T(8,128)(2,1)S(1)}, bf16[2,4,2,512,256]{4,3,2,1,0:T(8,128)(2,1)}, u32[]{:S(2)}) copy-start(bf16[2,4,2,512,256]{4,3,2,1,0:T(8,128)(2,1)} %param.4) | copy-start | bytes 12582916
  101.9 6.7 %copy-start.5 = (f32[2,192,256]{2,1,0:T(8,128)S(1)}, f32[2,192,256]{2,1,0:T(8,128)}, u32[]{:S(2)}) copy-start(f32[2,192,256]{2,1,0:T(8,128)} %get-tuple-element.7) | copy-start | bytes 1179652
Sparse Core Ops, SparseCore 0:
  40.0 37.7 all-reduce.3
where the time goes:
time: 166 us; the launch traced here: 165 us
  other arithmetic  42.9 us (26%)
  waiting for transfers between devices  37.8 us (23%)
  local copies, waits for them, and re-layouts  32.2 us (19%)
  blocking collectives  21.5 us (13%)
  matrix products  16.5 us (10%)
  between operations  14.1 us (8%)
    psum x1, waiting for transfers between devices, per_device(): proj_re, proj_im = lax.psum((part_re, part_im), 'freq')  37.8 us
    psum x1, blocking collectives, per_device(): power, count = lax.psum((power, count), 'ma')  21.5 us
    another operation x1, other arithmetic  18.4 us
    reshape x1, local copies, waits for them, and re-layouts, per_device(): jnp.einsum('msk,mck->msc', coef_re, matrix, preferred_element_type=jnp.fl...  9.18 us
    reshape x1, local copies, waits for them, and re-layouts, per_device(): second = jnp.einsum('msk,mck->msc', coef_im, matrix, preferred_element_ty...  9.16 us
    another operation x1, other arithmetic, per_device(): jnp.stack([visibilities[:, :, :, 1, :], -visibilities[:, :, :, 0, :]], ax...  8.05 us
    another operation x1, other arithmetic, per_device(): filtered = jnp.stack([out_re, out_im], axis=3).astype(jnp.bfloat16)  8.05 us
    dot_general x1, matrix products, per_device(): jnp.einsum('msk,mck->msc', coef_im, matrix, preferred_element_type=jnp.fl...  6.64 us
  transfers between devices with their start and end apart: 1, of which 1 were waited for; matrix products, arithmetic and copies ran while one was open for 0% of the time, Pallas kernels for 0%

commit v1 on v0

v1 whole, which is shorter than its diff:
```python
import functools

import jax
import jax.numpy as jnp
from jax import lax
from jax.experimental import pallas as pl
from jax.experimental.pallas import tpu as pltpu
from jax.sharding import PartitionSpec as P

F32 = jnp.float32
BF16 = jnp.bfloat16


def times_i(x):
    up = pltpu.roll(x, x.shape[0] - 1, 0)
    down = pltpu.roll(x, 1, 0)
    even = (lax.broadcasted_iota(jnp.int32, x.shape, 0) & 1) == 0
    return jnp.where(even, -up, down)


def project_kernel(mode_ref, v_ref, e_ref, out_ref, acc):
    f = pl.program_id(0)
    samples, base = v_ref.shape[1], v_ref.shape[-1]
    rows = v_ref[0, :, 0].reshape(2 * samples, base)
    by_re = jnp.dot(rows, e_ref[0, 0, 0], preferred_element_type=F32)
    by_im = jnp.dot(rows, e_ref[0, 0, 1], preferred_element_type=F32)

    @pl.when(f == 0)
    def _():
        acc[0] = by_re
        acc[1] = by_im

    @pl.when(f > 0)
    def _():
        acc[0] += by_re
        acc[1] += by_im

    @pl.when(f == pl.num_programs(0) - 1)
    def _():
        out_ref[...] = (acc[0] - times_i(acc[1])).astype(out_ref.dtype)


def project(mode, v, e, dtype):
    _, samples, freqs, _, base = v.shape
    kmax = e.shape[-1]
    return pl.pallas_call(
        project_kernel,
        grid_spec=pltpu.PrefetchScalarGridSpec(
            num_scalar_prefetch=1,
            grid=(freqs,),
            in_specs=[
                pl.BlockSpec((1, samples, 1, 2, base), lambda f, mode: (mode[0], 0, f, 0, 0)),
                pl.BlockSpec((1, 1, 2, base, kmax), lambda f, mode: (mode[0], f, 0, 0, 0)),
            ],
            out_specs=pl.BlockSpec((2 * samples, kmax), lambda f, mode: (0, 0)),
            scratch_shapes=[pltpu.VMEM((2, 2 * samples, kmax), F32)],
        ),
        out_shape=jax.ShapeDtypeStruct((2 * samples, kmax), dtype),
        name="project",
        cost_estimate=pl.CostEstimate(
            flops=8 * samples * freqs * base * kmax,
            bytes_accessed=4 * (samples * freqs * base + freqs * base * kmax),
            transcendentals=0,
        ),
    )(mode, v, e)


def power_kernel(mode_ref, retained_ref, mine_ref, theirs_ref, total_ref, stats_ref):
    total = mine_ref[...].astype(F32) + theirs_ref[...].astype(F32)
    total_ref[...] = total.astype(total_ref.dtype)
    kmax = total.shape[1]
    keep = lax.broadcasted_iota(jnp.int32, (1, kmax), 1) < retained_ref[mode_ref[0]]
    keep = keep.astype(F32)
    power = keep * jnp.sum(total * total, axis=0, keepdims=True)
    stats = jnp.concatenate([power, keep], axis=0)
    stats_ref[...] = jnp.broadcast_to(stats[None], stats_ref.shape)


def power_of(mode, retained, mine, theirs, peers):
    rows, kmax = mine.shape
    return pl.pallas_call(
        power_kernel,
        grid_spec=pltpu.PrefetchScalarGridSpec(
            num_scalar_prefetch=2,
            grid=(1,),
            in_specs=[pl.BlockSpec((rows, kmax), lambda i, a, b: (0, 0))] * 2,
            out_specs=[
                pl.BlockSpec((rows, kmax), lambda i, a, b: (0, 0)),
                pl.BlockSpec((peers, 2, kmax), lambda i, a, b: (0, 0, 0)),
            ],
        ),
        out_shape=[
            jax.ShapeDtypeStruct((rows, kmax), BF16),
            jax.ShapeDtypeStruct((peers, 2, kmax), F32),
        ],
        name="power",
    )(mode, retained, mine, theirs)


def back_kernel(first_ref, retained_ref, copies, stats_ref, mine_ref, other_ref, e_ref, coef_ref, out_ref, pair, flat):
    m, f = pl.program_id(0), pl.program_id(1)
    rows, kmax = mine_ref.shape
    samples = rows // 2

    def prepare(proj_ref):
        stats = jnp.sum(stats_ref[...], axis=0) * F32(1.0 / copies)
        power, count = stats[0:1], F32(samples) * stats[1:2]
        scale = 1.0 / jnp.sqrt(power / jnp.maximum(count, 1.0) + 1e-06)
        keep = lax.broadcasted_iota(jnp.int32, (1, kmax), 1) < retained_ref[m]
        gain = keep.astype(F32) * scale
        coef = proj_ref[...].astype(F32) * gain
        lanes = flat.shape[2]
        for i in range(flat.shape[0]):
            flat[i] = coef[:, i * lanes : (i + 1) * lanes]
            for part in range(2):
                every = flat[i, pl.ds(part, samples, stride=2), :]
                coef_ref[0, part, :, i * lanes : (i + 1) * lanes] = every.astype(BF16)
        pair[:, :kmax] = coef.astype(BF16)
        pair[:, kmax:] = times_i(coef).astype(BF16)

    @pl.when((f == 0) & (m == first_ref[0]))
    def _():
        prepare(mine_ref)

    @pl.when((f == 0) & (m != first_ref[0]))
    def _():
        prepare(other_ref)

    contract = (((1,), (1,)), ((), ()))
    out = lax.dot_general(pair[:, :kmax], e_ref[0, 0, 0], contract, preferred_element_type=F32)
    out += lax.dot_general(pair[:, kmax:], e_ref[0, 0, 1], contract, preferred_element_type=F32)
    out_ref[0, :, 0] = out.astype(BF16).reshape(samples, 2, out.shape[1])


def back(first, retained, copies, stats, mine, other, e):
    rows, kmax = mine.shape
    modes, freqs, _, base, _ = e.shape
    samples = rows // 2
    whole = lambda *shape: pl.BlockSpec(shape, lambda m, f, a, b: (0,) * len(shape))
    return pl.pallas_call(
        lambda first_ref, retained_ref, *refs: back_kernel(first_ref, retained_ref, copies, *refs),
        grid_spec=pltpu.PrefetchScalarGridSpec(
            num_scalar_prefetch=2,
            grid=(modes, freqs),
            in_specs=[
                whole(*stats.shape),
                whole(rows, kmax),
                whole(rows, kmax),
                pl.BlockSpec((1, 1, 2, base, kmax), lambda m, f, a, b: (m, f, 0, 0, 0)),
            ],
            out_specs=[
                pl.BlockSpec((1, 2, samples, kmax), lambda m, f, a, b: (m, 0, 0, 0)),
                pl.BlockSpec((1, samples, 1, 2, base), lambda m, f, a, b: (m, 0, f, 0, 0)),
            ],
            scratch_shapes=[pltpu.VMEM((rows, 2 * kmax), BF16), pltpu.VMEM((kmax // 128, rows, 128), F32)],
        ),
        out_shape=[
            jax.ShapeDtypeStruct((modes, 2, samples, kmax), BF16),
            jax.ShapeDtypeStruct((modes, samples, freqs, 2, base), BF16),
        ],
        name="back",
    )(first, retained, stats, mine, other, e)


def per_device(visibilities, eigenmodes, retained):
    freq_size, ma_size = lax.axis_size("freq"), lax.axis_size("ma")
    place = lax.axis_index("freq")

    def swap(x, bit):
        return lax.ppermute(x, "freq", [(i, i ^ bit) for i in range(freq_size)])

    kept = (place & 1).astype(jnp.int32).reshape(1)
    given = 1 - kept
    received = swap(project(given, visibilities, eigenmodes, BF16), 1)
    total = (project(kept, visibilities, eigenmodes, F32) + received.astype(F32)).astype(BF16)
    bit = 2
    while 2 * bit < freq_size:
        total = (total.astype(F32) + swap(total, bit).astype(F32)).astype(BF16)
        bit *= 2
    theirs = swap(total, bit)
    peers = ma_size * freq_size
    mine, stats = power_of(kept, retained, total, theirs, peers)
    other = swap(mine, 1)
    stats = lax.all_to_all(stats, ("ma", "freq"), 0, 0, tiled=True)
    coefficients, filtered = back(kept, retained, freq_size // 2, stats, mine, other, eigenmodes)
    return coefficients, filtered


def solution(mesh):
    return jax.shard_map(
        per_device,
        mesh=mesh,
        in_specs=(P("ma", None, "freq", None, None), P("ma", "freq", None, None, None), P("ma")),
        out_specs=(P("ma", None, None, None), P("ma", None, "freq", None, None)),
        check_vma=False,
    )
```

time: 166 us -> 46.7 us (0.28)
  other arithmetic: 42.9 us -> 1.04 us
  waiting for transfers between devices: 37.8 us -> 5.57 us
  local copies, waits for them, and re-layouts: 32.2 us -> 1.37 us
  Pallas kernels: 0 us -> 20.7 us
  matrix products: 16.5 us -> 0 us
  between operations: 14.1 us -> 0.65 us
  blocking collectives: 21.5 us -> 13.7 us
  starting transfers between devices: 0.04 us -> 3.07 us
    psum x1 -> x0, waiting for transfers between devices: 37.8 us -> none  [per_device(): proj_re, proj_im = lax.psum((part_re, part_im), 'freq')]
    another operation x5 -> x0, other arithmetic: 35.7 us -> none
    reshape x4 -> x0, local copies, waits for them, and re-layouts: 30.9 us -> none  [the longest x1 9.18 us: per_device(): jnp.einsum('msk,mck->msc', coef_re, matrix, preferred_element_type=jnp.fl...]
    psum x1 -> x0, blocking collectives: 21.5 us -> none  [per_device(): power, count = lax.psum((power, count), 'ma')]
    pallas_call x0 -> x4, Pallas kernels: none -> 20.7 us  [the longest x2 9.19 us: project(): pl.pallas_call(project_kernel, grid_spec=pltpu.PrefetchScalarGridSpec(num...]
    dot_general x4 -> x0, matrix products: 16.5 us -> none  [the longest x1 6.64 us: per_device(): jnp.einsum('msk,mck->msc', coef_im, matrix, preferred_element_type=jnp.fl...]
    all_to_all x0 -> x1, blocking collectives: none -> 13.7 us  [per_device(): stats = lax.all_to_all(stats, ('ma', 'freq'), 0, 0, tiled=True)]
    slice x1 -> x0, other arithmetic: 5.76 us -> none  [per_device(): visibilities[:, :, :, 1, :]]
  transfers between devices with their start and end apart: 1 -> 3, of which waited for: 1 -> 1; matrix products, arithmetic and copies ran while one was open for 0% -> 0% of each run, Pallas kernels for 0% -> 10%
where the time goes in v1:
time: 46.7 us; the launch traced here: 46.2 us
  Pallas kernels  20.7 us (44%)
  blocking collectives  13.7 us (29%)
  waiting for transfers between devices  5.57 us (12%)
  starting transfers between devices  3.07 us (7%)
  local copies, waits for them, and re-layouts  1.37 us (3%)
  other arithmetic  1.04 us (2%)
  between operations  0.65 us (1%)
    all_to_all x1, blocking collectives, per_device(): stats = lax.all_to_all(stats, ('ma', 'freq'), 0, 0, tiled=True)  13.7 us
    pallas_call x2, Pallas kernels, project(): pl.pallas_call(project_kernel, grid_spec=pltpu.PrefetchScalarGridSpec(num...  9.19 us
    pallas_call x1, Pallas kernels, back(): pl.pallas_call(lambda first_ref, retained_ref, *refs: back_kernel(first_r...  9.09 us
    ppermute x3, waiting for transfers between devices, swap(): return lax.ppermute(x, 'freq', [(i, i ^ bit) for i in range(freq_size)])  5.57 us
    ppermute x3, starting transfers between devices, swap(): return lax.ppermute(x, 'freq', [(i, i ^ bit) for i in range(freq_size)])  3.07 us
    pallas_call x1, Pallas kernels, power_of(): pl.pallas_call(power_kernel, grid_spec=pltpu.PrefetchScalarGridSpec(num_s...  2.46 us
    unnamed x6, local copies, waits for them, and re-layouts  1.37 us
    convert_element_type x1, other arithmetic, per_device(): (project(kept, visibilities, eigenmodes, F32) + received.astype(F32)).ast...  1.04 us
  transfers between devices with their start and end apart: 3, of which 1 were waited for; matrix products, arithmetic and copies ran while one was open for 0% of the time, Pallas kernels for 10%

profile of v1, /device:TPU:0, one launch (start us, length us, event | category | flops | bytes accessed | tf_op | source)
XLA Modules:
  0.0 46.2 jit_solution(13695356778289421209)
XLA Ops:
  0.6 4.6 %project.3 = bf16[384,256]{1,0:T(8,128)(2,1)} custom-call(s32[1]{0:T(128)S(6)} %sub.3.mode_ref, bf16[2,192,4,2,512]{4,3,2,1,0:T(2,128)(2,1)} %v_ref.3, bf16[2,4,2,512,256]{4,3,2,1,0:T(8,128)(2,1)} %refs_3_.1), custom_call_target="tpu_custom_call" | custom-call | flops 805306368 | bytes 3670016 | tf_op jit(solution)/shard_map/project/pallas_call | solution.py:46
  5.2 0.5 %collective-permute-start = (bf16[384,256]{1,0:T(8,128)(2,1)}, bf16[384,256]{1,0:T(8,128)(2,1)S(1)}, u32[]{:S(2)}, u32[]{:S(2)}) collective-permute-start(bf16[384,256]{1,0:T(8,128)(2,1)} %project.3), channel_id=1, source_target_pairs={{0,1},{1,0},{2,3},{3,2},{4,5},{5,4},{6,7},{7,6},{8,9},{9,8},{10,11... | collective-permute-start | bytes 589832 | tf_op jit(solution)/shard_map/ppermute | solution.py:170
  5.7 4.6 %project.2 = f32[384,256]{1,0:T(8,128)} custom-call(s32[1]{0:T(128)} %bitcast.mode_ref.first_ref, bf16[2,192,4,2,512]{4,3,2,1,0:T(2,128)(2,1)} %v_ref.3, bf16[2,4,2,512,256]{4,3,2,1,0:T(8,128)(2,1)} %refs_3_.1), custom_call_target="tpu_custom_call" | custom-call | flops 805306368 | bytes 3670016 | tf_op jit(solution)/shard_map/project/pallas_call | solution.py:46
  10.3 0.0 collective-permute-done
  10.3 1.0 %add_convert_fusion.mine_ref = bf16[384,256]{1,0:T(8,128)(2,1)S(1)} fusion(f32[384,256]{1,0:T(8,128)} %project.2, bf16[384,256]{1,0:T(8,128)(2,1)S(1)} %collective-permute-done), kind=kLoop, calls=%fused_computation | loop fusion | flops 294912 | bytes 786432 | tf_op jit(solution)/shard_map/convert_element_type | solution.py:175
  11.4 0.0 copy-start
  11.4 2.6 %collective-permute-start.1 = (bf16[384,256]{1,0:T(8,128)(2,1)S(1)}, bf16[384,256]{1,0:T(8,128)(2,1)S(1)}, u32[]{:S(2)}, u32[]{:S(2)}) collective-permute-start(bf16[384,256]{1,0:T(8,128)(2,1)S(1)} %add_convert_fusion.mine_ref), channel_id=1, source_target_pairs={{0,2},{1,3},{2,0},{3,1},{4,6},{5,7},{6,4},{7,5},{8,10},{9,11},{10,... | collective-permute-start | bytes 589832 | tf_op jit(solution)/shard_map/ppermute | solution.py:170
  13.9 5.6 %collective-permute-done.1.theirs_ref = bf16[384,256]{1,0:T(8,128)(2,1)S(1)} collective-permute-done((bf16[384,256]{1,0:T(8,128)(2,1)S(1)}, bf16[384,256]{1,0:T(8,128)(2,1)S(1)}, u32[]{:S(2)}, u32[]{:S(2)}) %collective-permute-start.1) | collective-permute-done | bytes 196640 | tf_op jit(solution)/shard_map/ppermute | solution.py:170
  19.5 0.0 copy-done
  19.5 0.0 copy-start.2
  19.5 0.7 %copy-done.2 = bf16[384,256]{1,0:T(8,128)(2,1)} copy-done((bf16[384,256]{1,0:T(8,128)(2,1)}, bf16[384,256]{1,0:T(8,128)(2,1)S(1)}, u32[]{:S(2)}) %copy-start.2) | copy-done | bytes 196632
  20.2 2.5 %power.1 = (bf16[384,256]{1,0:T(8,128)(2,1)}, f32[32,2,256]{2,1,0:T(2,128)}) custom-call(s32[1]{0:T(128)} %bitcast.mode_ref.first_ref, s32[2]{0:T(128)} %retained_ref.3, bf16[384,256]{1,0:T(8,128)(2,1)} %copy-done, bf16[384,256]{1,0:T(8,128)(2,1)} %copy-done.2), custom_call_target="tpu_custom_call" | custom-call | tf_op jit(solution)/shard_map/power/pallas_call | solution.py:81
  22.7 0.0 collective-permute-start.2
  22.7 13.7 %all_to_all.5.refs_0_ = f32[32,2,256]{2,1,0:T(2,128)} all-to-all(f32[32,2,256]{2,1,0:T(2,128)} %get-tuple-element.4), channel_id=1, replica_groups=mesh['ma'=8,'freq'=4] {'ma','freq'}, dimensions={0} | all-to-all | bytes 131072 | tf_op jit(solution)/shard_map/all_to_all | solution.py:184
  36.4 0.0 collective-permute-done.2.refs_2_
  36.4 0.0 copy-start.1
  36.4 0.7 %copy-done.1 = bf16[384,256]{1,0:T(8,128)(2,1)} copy-done((bf16[384,256]{1,0:T(8,128)(2,1)}, bf16[384,256]{1,0:T(8,128)(2,1)S(1)}, u32[]{:S(2)}) %copy-start.1) | copy-done | bytes 196632
  37.1 9.1 %back.1 = (bf16[2,2,192,256]{3,2,1,0:T(8,128)(2,1)}, bf16[2,192,4,2,512]{4,3,2,1,0:T(2,128)(2,1)}) custom-call(s32[1]{0:T(128)} %bitcast.mode_ref.first_ref, s32[2]{0:T(128)} %retained_ref.3, f32[32,2,256]{2,1,0:T(2,128)} %all_to_all.5.refs_0_, bf16[384,256]{1,0:T(8,128)(2,1)} %get-tuple-element.5.refs_1_, bf16[384,256]{1,0:T(8,128)(2,1)} %copy-done.1, ...), custom_call_target="tpu_custom_call" | custom-call | tf_op jit(solution)/shard_map/back/pallas_call | solution.py:140
Async XLA Ops:
  5.2 5.1 %collective-permute-start = (bf16[384,256]{1,0:T(8,128)(2,1)}, bf16[384,256]{1,0:T(8,128)(2,1)S(1)}, u32[]{:S(2)}, u32[]{:S(2)}) collective-permute-start(bf16[384,256]{1,0:T(8,128)(2,1)} %project.3), channel_id=1, source_target_pairs={{0,1},{1,0},{2,3},{3,2},{4,5},{5,4},{6,7},{7,6},{8,9},{9,8},{10,11... | collective-permute-start | bytes 589832 | tf_op jit(solution)/shard_map/ppermute | solution.py:170
  11.4 8.2 %copy-start = (bf16[384,256]{1,0:T(8,128)(2,1)}, bf16[384,256]{1,0:T(8,128)(2,1)S(1)}, u32[]{:S(2)}) copy-start(bf16[384,256]{1,0:T(8,128)(2,1)S(1)} %add_convert_fusion.mine_ref) | copy-start | bytes 589828
  11.4 8.1 %collective-permute-start.1 = (bf16[384,256]{1,0:T(8,128)(2,1)S(1)}, bf16[384,256]{1,0:T(8,128)(2,1)S(1)}, u32[]{:S(2)}, u32[]{:S(2)}) collective-permute-start(bf16[384,256]{1,0:T(8,128)(2,1)S(1)} %add_convert_fusion.mine_ref), channel_id=1, source_target_pairs={{0,2},{1,3},{2,0},{3,1},{4,6},{5,7},{6,4},{7,5},{8,10},{9,11},{10,... | collective-permute-start | bytes 589832 | tf_op jit(solution)/shard_map/ppermute | solution.py:170
  19.5 0.7 %copy-start.2 = (bf16[384,256]{1,0:T(8,128)(2,1)}, bf16[384,256]{1,0:T(8,128)(2,1)S(1)}, u32[]{:S(2)}) copy-start(bf16[384,256]{1,0:T(8,128)(2,1)S(1)} %collective-permute-done.1.theirs_ref) | copy-start | bytes 589828
  22.7 13.7 %collective-permute-start.2 = (bf16[384,256]{1,0:T(8,128)(2,1)}, bf16[384,256]{1,0:T(8,128)(2,1)S(1)}, u32[]{:S(2)}, u32[]{:S(2)}) collective-permute-start(bf16[384,256]{1,0:T(8,128)(2,1)} %get-tuple-element.5.refs_1_), channel_id=1, source_target_pairs={{0,1},{1,0},{2,3},{3,2},{4,5},{5,4},{6,7},{7,6},{8,9},{9,8},{10,11... | collective-permute-start | bytes 589832 | tf_op jit(solution)/shard_map/ppermute | solution.py:170
  36.4 0.7 %copy-start.1 = (bf16[384,256]{1,0:T(8,128)(2,1)}, bf16[384,256]{1,0:T(8,128)(2,1)S(1)}, u32[]{:S(2)}) copy-start(bf16[384,256]{1,0:T(8,128)(2,1)S(1)} %collective-permute-done.2.refs_2_) | copy-start | bytes 589828

commit v2 on v0

v2 whole, which is shorter than its diff:
```python
import functools

import jax
import jax.numpy as jnp
from jax import lax
from jax.experimental import pallas as pl
from jax.experimental.pallas import tpu as pltpu
from jax.sharding import PartitionSpec as P

F32 = jnp.float32
BF16 = jnp.bfloat16
VMEM = pl.BlockSpec(memory_space=pltpu.VMEM)
SMEM = pl.BlockSpec(memory_space=pltpu.SMEM)
HBM = pl.BlockSpec(memory_space=pltpu.HBM)
MIB = 1 << 20


def limit(vmem):
    return pltpu.CompilerParams(vmem_limit_bytes=vmem)


def times_i(x):
    up = pltpu.roll(x, x.shape[0] - 1, 0)
    down = pltpu.roll(x, 1, 0)
    even = (lax.broadcasted_iota(jnp.int32, x.shape, 0) & 1) == 0
    return jnp.where(even, -up, down)


def project_kernel(first_ref, v_hbm, e_hbm, given_ref, kept_ref, e_ref, v_buf, acc, v_sem, e_sem):
    modes, freqs, samples, _, base = v_buf.shape
    rows = 2 * samples
    half = modes // 2
    mode = [lax.rem(first_ref[0] + j, modes) for j in range(modes)]
    copies = []
    for j in range(modes):
        for f in range(freqs):
            e_copy = pltpu.make_async_copy(e_hbm.at[mode[j], f], e_ref.at[mode[j], f], e_sem.at[j, f])
            v_copy = pltpu.make_async_copy(v_hbm.at[mode[j], :, f], v_buf.at[j, f], v_sem.at[j, f])
            e_copy.start()
            v_copy.start()
            copies.append((e_copy, v_copy))
    for j in range(modes):
        for f in range(freqs):
            for copy in copies[j * freqs + f]:
                copy.wait()
            x = v_buf[j, f].reshape(rows, base)
            by_re = jnp.dot(x, e_ref[mode[j], f, 0], preferred_element_type=F32)
            by_im = jnp.dot(x, e_ref[mode[j], f, 1], preferred_element_type=F32)
            if f > 0:
                by_re += acc[0]
                by_im += acc[1]
            if f < freqs - 1:
                acc[0] = by_re
                acc[1] = by_im
            else:
                out_ref = given_ref if j < half else kept_ref
                out = by_re - times_i(by_im)
                out_ref[pl.ds(j % half * rows, rows), :] = out.astype(out_ref.dtype)


def project(first, v, e):
    modes, samples, freqs, _, base = v.shape
    kmax = e.shape[-1]
    rows = modes // 2 * 2 * samples
    return pl.pallas_call(
        project_kernel,
        in_specs=[SMEM, HBM, HBM],
        out_specs=[VMEM, VMEM, VMEM],
        out_shape=[
            jax.ShapeDtypeStruct((rows, kmax), BF16),
            jax.ShapeDtypeStruct((rows, kmax), F32),
            jax.ShapeDtypeStruct(e.shape, e.dtype),
        ],
        scratch_shapes=[
            pltpu.VMEM((modes, freqs, samples, 2, base), v.dtype),
            pltpu.VMEM((2, 2 * samples, kmax), F32),
            pltpu.SemaphoreType.DMA((modes, freqs)),
            pltpu.SemaphoreType.DMA((modes, freqs)),
        ],
        name="project",
        compiler_params=limit(MIB * 16),
    )(first, pltpu.with_memory_space_constraint(v, pltpu.HBM), pltpu.with_memory_space_constraint(e, pltpu.HBM))


def power_kernel(first_ref, retained_ref, mine_ref, theirs_ref, total_ref, stats_ref):
    modes = retained_ref.shape[0]
    half = modes // 2
    kmax = mine_ref.shape[1]
    rows = mine_ref.shape[0] // half
    stats = jnp.zeros((2, kmax), F32)
    for j in range(half):
        at = pl.ds(j * rows, rows)
        total = mine_ref[at, :].astype(F32) + theirs_ref[at, :].astype(F32)
        total_ref[at, :] = total.astype(total_ref.dtype)
        keep = lax.broadcasted_iota(jnp.int32, (1, kmax), 1) < retained_ref[lax.rem(first_ref[0] + j, modes)]
        keep = keep.astype(F32)
        power = keep * jnp.sum(total * total, axis=0, keepdims=True)
        stats += jnp.concatenate([power, keep], axis=0)
    stats_ref[...] = jnp.broadcast_to(stats[None], stats_ref.shape)


def power_of(first, retained, mine, theirs, peers):
    rows, kmax = mine.shape
    return pl.pallas_call(
        power_kernel,
        in_specs=[SMEM, SMEM, VMEM, VMEM],
        out_specs=[VMEM, VMEM],
        out_shape=[
            jax.ShapeDtypeStruct((rows, kmax), BF16),
            jax.ShapeDtypeStruct((peers, 2, kmax), F32),
        ],
        name="power",
        compiler_params=limit(MIB * 4),
    )(first, retained, mine, theirs)


def back_kernel(
    copies, first_ref, retained_ref, stats_ref, mine_ref, other_ref, e_ref, coef_hbm, out_hbm, pair, flat, coef_buf, out_buf, coef_sem, out_sem
):
    modes, freqs, samples, _, base = out_buf.shape
    kmax = mine_ref.shape[1]
    rows = 2 * samples
    half = modes // 2
    lanes = flat.shape[2]
    stats = jnp.sum(stats_ref[...], axis=0) * F32(1.0 / copies)
    power, count = stats[0:1], F32(samples) * stats[1:2]
    scale = 1.0 / jnp.sqrt(power / jnp.maximum(count, 1.0) + 1e-06)
    contract = (((1,), (1,)), ((), ()))
    pending = []
    for j in range(modes):
        mode = lax.rem(first_ref[0] + j, modes)
        proj_ref = mine_ref if j < half else other_ref
        keep = lax.broadcasted_iota(jnp.int32, (1, kmax), 1) < retained_ref[mode]
        gain = keep.astype(F32) * scale
        coef = proj_ref[pl.ds(j % half * rows, rows), :].astype(F32) * gain
        pair[:, :kmax] = coef.astype(BF16)
        pair[:, kmax:] = times_i(coef).astype(BF16)
        for i in range(kmax // lanes):
            flat[i] = coef[:, i * lanes : (i + 1) * lanes]
            for part in range(2):
                every = flat[i, pl.ds(part, samples, stride=2), :]
                coef_buf[j, part, :, i * lanes : (i + 1) * lanes] = every.astype(BF16)
        copy = pltpu.make_async_copy(coef_buf.at[j], coef_hbm.at[mode], coef_sem.at[j])
        copy.start()
        pending.append(copy)
        for f in range(freqs):
            out = lax.dot_general(pair[:, :kmax], e_ref[mode, f, 0], contract, preferred_element_type=F32)
            out += lax.dot_general(pair[:, kmax:], e_ref[mode, f, 1], contract, preferred_element_type=F32)
            out_buf[j, f] = out.astype(BF16).reshape(samples, 2, base)
            copy = pltpu.make_async_copy(out_buf.at[j, f], out_hbm.at[mode, :, f], out_sem.at[j, f])
            copy.start()
            pending.append(copy)
    for copy in pending:
        copy.wait()


def back(first, retained, copies, stats, mine, other, e):
    kmax = mine.shape[1]
    modes, freqs, _, base, _ = e.shape
    samples = mine.shape[0] // modes
    return pl.pallas_call(
        functools.partial(back_kernel, copies),
        in_specs=[SMEM, SMEM, VMEM, VMEM, VMEM, VMEM],
        out_specs=[HBM, HBM],
        out_shape=[
            jax.ShapeDtypeStruct((modes, 2, samples, kmax), BF16),
            jax.ShapeDtypeStruct((modes, samples, freqs, 2, base), BF16),
        ],
        scratch_shapes=[
            pltpu.VMEM((2 * samples, 2 * kmax), BF16),
            pltpu.VMEM((kmax // 128, 2 * samples, 128), F32),
            pltpu.VMEM((modes, 2, samples, kmax), BF16),
            pltpu.VMEM((modes, freqs, samples, 2, base), BF16),
            pltpu.SemaphoreType.DMA((modes,)),
            pltpu.SemaphoreType.DMA((modes, freqs)),
        ],
        name="back",
        compiler_params=limit(MIB * 16),
    )(first, retained, stats, mine, other, e)


def per_device(visibilities, eigenmodes, retained):
    freq_size, ma_size = lax.axis_size("freq"), lax.axis_size("ma")
    half = visibilities.shape[0] // 2
    side = (lax.axis_index("freq") & 1).astype(jnp.int32).reshape(1)

    def swap(x, bit):
        return lax.ppermute(x, "freq", [(i, i ^ bit) for i in range(freq_size)])

    first_kept, first_given = side * half, (1 - side) * half
    given, kept, e_vmem = project(first_given, visibilities, eigenmodes)
    total = (kept + swap(given, 1).astype(F32)).astype(BF16)
    bit = 2
    while 2 * bit < freq_size:
        total = (total.astype(F32) + swap(total, bit).astype(F32)).astype(BF16)
        bit *= 2
    mine, stats = power_of(first_kept, retained, total, swap(total, bit), ma_size * freq_size)
    other = swap(mine, 1)
    stats = lax.all_to_all(stats, ("ma", "freq"), 0, 0, tiled=True)
    coefficients, filtered = back(first_kept, retained, freq_size // 2, stats, mine, other, e_vmem)
    return coefficients, filtered


def solution(mesh):
    return jax.shard_map(
        per_device,
        mesh=mesh,
        in_specs=(P("ma", None, "freq", None, None), P("ma", "freq", None, None, None), P("ma")),
        out_specs=(P("ma", None, None, None), P("ma", None, "freq", None, None)),
        check_vma=False,
    )
```

time: 166 us -> 31.9 us (0.19)
  other arithmetic: 42.9 us -> 0.05 us
  local copies, waits for them, and re-layouts: 32.2 us -> 0.01 us
  waiting for transfers between devices: 37.8 us -> 6.28 us
  matrix products: 16.5 us -> 0 us
  between operations: 14.1 us -> 0.67 us
  blocking collectives: 21.5 us -> 13.4 us
  Pallas kernels: 0 us -> 7.75 us
  starting transfers between devices: 0.04 us -> 3.57 us
    psum x1 -> x0, waiting for transfers between devices: 37.8 us -> none  [per_device(): proj_re, proj_im = lax.psum((part_re, part_im), 'freq')]
    another operation x5 -> x0, other arithmetic: 35.7 us -> none
    reshape x4 -> x0, local copies, waits for them, and re-layouts: 30.9 us -> none  [the longest x1 9.18 us: per_device(): jnp.einsum('msk,mck->msc', coef_re, matrix, preferred_element_type=jnp.fl...]
    psum x1 -> x0, blocking collectives: 21.5 us -> none  [per_device(): power, count = lax.psum((power, count), 'ma')]
    dot_general x4 -> x0, matrix products: 16.5 us -> none  [the longest x1 6.64 us: per_device(): jnp.einsum('msk,mck->msc', coef_im, matrix, preferred_element_type=jnp.fl...]
    all_to_all x0 -> x1, blocking collectives: none -> 13.4 us  [per_device(): stats = lax.all_to_all(stats, ('ma', 'freq'), 0, 0, tiled=True)]
    pallas_call x0 -> x3, Pallas kernels: none -> 7.75 us  [the longest x1 3.73 us: project(): pl.pallas_call(project_kernel, in_specs=[SMEM, HBM, HBM], out_specs=[VMEM...]
    ppermute x0 -> x3, waiting for transfers between devices: none -> 6.28 us  [swap(): return lax.ppermute(x, 'freq', [(i, i ^ bit) for i in range(freq_size)])]
  transfers between devices with their start and end apart: 1 -> 3, of which waited for: 1 -> 2; matrix products, arithmetic and copies ran while one was open for 0% -> 0% of each run, Pallas kernels for 0% -> 0%
where the time goes in v2:
time: 31.9 us; the launch traced here: 31.7 us
  blocking collectives  13.4 us (42%)
  Pallas kernels  7.75 us (24%)
  waiting for transfers between devices  6.28 us (20%)
  starting transfers between devices  3.57 us (11%)
  between operations  0.67 us (2%)
    all_to_all x1, blocking collectives, per_device(): stats = lax.all_to_all(stats, ('ma', 'freq'), 0, 0, tiled=True)  13.4 us
    ppermute x3, waiting for transfers between devices, swap(): return lax.ppermute(x, 'freq', [(i, i ^ bit) for i in range(freq_size)])  6.28 us
    pallas_call x1, Pallas kernels, project(): pl.pallas_call(project_kernel, in_specs=[SMEM, HBM, HBM], out_specs=[VMEM...  3.73 us
    ppermute x3, starting transfers between devices, swap(): return lax.ppermute(x, 'freq', [(i, i ^ bit) for i in range(freq_size)])  3.57 us
    pallas_call x1, Pallas kernels, back(): pl.pallas_call(functools.partial(back_kernel, copies), in_specs=[SMEM, SM...  3.37 us
    pallas_call x1, Pallas kernels, power_of(): pl.pallas_call(power_kernel, in_specs=[SMEM, SMEM, VMEM, VMEM], out_specs...  0.65 us
  transfers between devices with their start and end apart: 3, of which 2 were waited for; matrix products, arithmetic and copies ran while one was open for 0% of the time, Pallas kernels for 0%

profile of v2, /device:TPU:0, one launch (start us, length us, event | category | flops | bytes accessed | tf_op | source)
XLA Modules:
  0.0 31.7 jit_solution(4108832655329203174)
XLA Ops:
  0.6 0.0 copy-start
  0.6 3.7 %project.1 = (bf16[384,256]{1,0:T(8,128)(2,1)S(1)}, f32[384,256]{1,0:T(8,128)S(1)}, bf16[2,4,2,512,256]{4,3,2,1,0:T(8,128)(2,1)S(1)}) custom-call(s32[1]{0:T(128)S(6)} %sub.3.first_ref, bf16[2,192,4,2,512]{4,3,2,1,0:T(2,128)(2,1)} %v_hbm.1, bf16[2,4,2,512,256]{4,3,2,1,0:T(8,128)(2,1)} %e_hbm.1), custom_call_target="tpu_custom_call" | custom-call | tf_op jit(solution)/shard_map/project/pallas_call | solution.py:65
  4.4 0.6 %collective-permute-start = (bf16[384,256]{1,0:T(8,128)(2,1)S(1)}, bf16[384,256]{1,0:T(8,128)(2,1)S(1)}, u32[]{:S(2)}, u32[]{:S(2)}) collective-permute-start(bf16[384,256]{1,0:T(8,128)(2,1)S(1)} %get-tuple-element.8), channel_id=1, source_target_pairs={{0,1},{1,0},{2,3},{3,2},{4,5},{5,4},{6,7},{7,6},{8,9},{9,8},{10,11... | collective-permute-start | bytes 589832 | tf_op jit(solution)/shard_map/ppermute | solution.py:188
  4.9 1.1 %collective-permute-done = bf16[384,256]{1,0:T(8,128)(2,1)S(1)} collective-permute-done((bf16[384,256]{1,0:T(8,128)(2,1)S(1)}, bf16[384,256]{1,0:T(8,128)(2,1)S(1)}, u32[]{:S(2)}, u32[]{:S(2)}) %collective-permute-start) | collective-permute-done | bytes 196640 | tf_op jit(solution)/shard_map/ppermute | solution.py:188
  6.1 2.9 %collective-permute-start.1 = (bf16[384,256]{1,0:T(8,128)(2,1)S(1)}, bf16[384,256]{1,0:T(8,128)(2,1)S(1)}, u32[]{:S(2)}, u32[]{:S(2)}) collective-permute-start(bf16[384,256]{1,0:T(8,128)(2,1)S(1)} %add_convert_fusion.mine_ref), channel_id=1, source_target_pairs={{0,2},{1,3},{2,0},{3,1},{4,6},{5,7},{6,4},{7,5},{8,10},{9,11},{10,... | collective-permute-start | bytes 589832 | tf_op jit(solution)/shard_map/ppermute | solution.py:188
  9.0 5.2 %collective-permute-done.1.theirs_ref = bf16[384,256]{1,0:T(8,128)(2,1)S(1)} collective-permute-done((bf16[384,256]{1,0:T(8,128)(2,1)S(1)}, bf16[384,256]{1,0:T(8,128)(2,1)S(1)}, u32[]{:S(2)}, u32[]{:S(2)}) %collective-permute-start.1) | collective-permute-done | bytes 196640 | tf_op jit(solution)/shard_map/ppermute | solution.py:188
  14.2 0.0 copy-done
  14.2 0.6 %power.1 = (bf16[384,256]{1,0:T(8,128)(2,1)S(1)}, f32[32,2,256]{2,1,0:T(2,128)S(1)}) custom-call(s32[1]{0:T(128)} %bitcast.first_ref, s32[2]{0:T(128)S(1)} %copy-done, bf16[384,256]{1,0:T(8,128)(2,1)S(1)} %add_convert_fusion.mine_ref, bf16[384,256]{1,0:T(8,128)(2,1)S(1)} %collective-permute-done.1.theirs_ref), custom_call_target="tpu_custom_call" | custom-call | tf_op jit(solution)/shard_map/power/pallas_call | solution.py:104
  14.9 0.1 collective-permute-start.2
  14.9 13.4 %all_to_all.5.stats_ref = f32[32,2,256]{2,1,0:T(2,128)S(1)} all-to-all(f32[32,2,256]{2,1,0:T(2,128)S(1)} %get-tuple-element.9), channel_id=1, replica_groups=mesh['ma'=8,'freq'=4] {'ma','freq'}, dimensions={0} | all-to-all | bytes 131072 | tf_op jit(solution)/shard_map/all_to_all | solution.py:199
  28.3 0.0 collective-permute-done.2.other_ref
  28.3 3.4 %back.1 = (bf16[2,2,192,256]{3,2,1,0:T(8,128)(2,1)}, bf16[2,192,4,2,512]{4,3,2,1,0:T(2,128)(2,1)}) custom-call(s32[1]{0:T(128)} %bitcast.first_ref, s32[2]{0:T(128)S(1)} %copy-done, f32[32,2,256]{2,1,0:T(2,128)S(1)} %all_to_all.5.stats_ref, bf16[384,256]{1,0:T(8,128)(2,1)S(1)} %get-tuple-element.10.mine_ref, ...), custom_call_target="tpu_custom_call" | custom-call | tf_op jit(solution)/shard_map/back/pallas_call | solution.py:161
  (1 shorter events, 0.0 us)
Async XLA Ops:
  0.6 13.6 %copy-start = (s32[2]{0:T(128)S(1)}, s32[2]{0:T(128)}, u32[]{:S(2)}) copy-start(s32[2]{0:T(128)} %retained_ref.3) | copy-start | bytes 28
  4.4 1.6 %collective-permute-start = (bf16[384,256]{1,0:T(8,128)(2,1)S(1)}, bf16[384,256]{1,0:T(8,128)(2,1)S(1)}, u32[]{:S(2)}, u32[]{:S(2)}) collective-permute-start(bf16[384,256]{1,0:T(8,128)(2,1)S(1)} %get-tuple-element.8), channel_id=1, source_target_pairs={{0,1},{1,0},{2,3},{3,2},{4,5},{5,4},{6,7},{7,6},{8,9},{9,8},{10,11... | collective-permute-start | bytes 589832 | tf_op jit(solution)/shard_map/ppermute | solution.py:188
  6.1 8.1 %collective-permute-start.1 = (bf16[384,256]{1,0:T(8,128)(2,1)S(1)}, bf16[384,256]{1,0:T(8,128)(2,1)S(1)}, u32[]{:S(2)}, u32[]{:S(2)}) collective-permute-start(bf16[384,256]{1,0:T(8,128)(2,1)S(1)} %add_convert_fusion.mine_ref), channel_id=1, source_target_pairs={{0,2},{1,3},{2,0},{3,1},{4,6},{5,7},{6,4},{7,5},{8,10},{9,11},{10,... | collective-permute-start | bytes 589832 | tf_op jit(solution)/shard_map/ppermute | solution.py:188
  14.9 13.5 %collective-permute-start.2 = (bf16[384,256]{1,0:T(8,128)(2,1)S(1)}, bf16[384,256]{1,0:T(8,128)(2,1)S(1)}, u32[]{:S(2)}, u32[]{:S(2)}) collective-permute-start(bf16[384,256]{1,0:T(8,128)(2,1)S(1)} %get-tuple-element.10.mine_ref), channel_id=1, source_target_pairs={{0,1},{1,0},{2,3},{3,2},{4,5},{5,4},{6,7},{7,6},{8,9},{9,8},{10,11... | collective-permute-start | bytes 589832 | tf_op jit(solution)/shard_map/ppermute | solution.py:188

commit v3 on v2

v3 whole, which is shorter than its diff:
```python
import functools

import jax
import jax.numpy as jnp
from jax import lax
from jax.experimental import pallas as pl
from jax.experimental.pallas import tpu as pltpu
from jax.sharding import PartitionSpec as P

F32 = jnp.float32
BF16 = jnp.bfloat16
VMEM = pl.BlockSpec(memory_space=pltpu.VMEM)
SMEM = pl.BlockSpec(memory_space=pltpu.SMEM)
HBM = pl.BlockSpec(memory_space=pltpu.HBM)
MIB = 1 << 20


def limit(vmem):
    return pltpu.CompilerParams(vmem_limit_bytes=vmem)


def cost(flops, *arrays):
    moved = sum(a.size * a.dtype.itemsize for a in arrays)
    return pl.CostEstimate(flops=flops, bytes_accessed=moved, transcendentals=0)


def times_i(x):
    up = pltpu.roll(x, x.shape[0] - 1, 0)
    down = pltpu.roll(x, 1, 0)
    even = (lax.broadcasted_iota(jnp.int32, x.shape, 0) & 1) == 0
    return jnp.where(even, -up, down)


def project_kernel(place_ref, v_hbm, e_hbm, given_ref, kept_ref, e_kept, e_given, v_buf, acc, v_sem, e_sem):
    modes, freqs, samples, _, base = v_buf.shape
    rows = 2 * samples
    half = modes // 2
    first, later = (1 - place_ref[0]) * half, place_ref[1]
    mode = [lax.rem(first + j, modes) for j in range(modes)]
    e_of = [e_given.at[j] for j in range(half)] + [e_kept.at[j] for j in range(half)]
    copies = []
    for j in range(modes):
        for f in range(freqs):
            e_copy = pltpu.make_async_copy(e_hbm.at[mode[j], f], e_of[j].at[f], e_sem.at[j, f])
            v_copy = pltpu.make_async_copy(v_hbm.at[mode[j], :, f], v_buf.at[j, f], v_sem.at[j, f])
            e_copy.start()
            v_copy.start()
            copies.append((e_copy, v_copy))
    for j in range(modes):
        for f in range(freqs):
            for copy in copies[j * freqs + f]:
                copy.wait()
            x = v_buf[j, f].reshape(rows, base)
            by_re = jnp.dot(x, e_of[j][f, 0], preferred_element_type=F32)
            by_im = jnp.dot(x, e_of[j][f, 1], preferred_element_type=F32)
            if f > 0:
                by_re += acc[0]
                by_im += acc[1]
            if f < freqs - 1:
                acc[0] = by_re
                acc[1] = by_im
            else:
                out_ref = given_ref if j < half else kept_ref
                out = (by_re - times_i(by_im)).astype(out_ref.dtype)
                out_ref[1 - later, j % half] = out[:samples]
                out_ref[later, j % half] = out[samples:]


def project(place, v, e):
    modes, samples, freqs, _, base = v.shape
    kmax = e.shape[-1]
    shape = (2, modes // 2, samples, kmax)
    return pl.pallas_call(
        project_kernel,
        in_specs=[SMEM, HBM, HBM],
        out_specs=[VMEM, VMEM, VMEM],
        out_shape=[
            jax.ShapeDtypeStruct(shape, BF16),
            jax.ShapeDtypeStruct(shape, F32),
            jax.ShapeDtypeStruct((modes // 2,) + e.shape[1:], e.dtype),
        ],
        scratch_shapes=[
            pltpu.VMEM((modes // 2,) + e.shape[1:], e.dtype),
            pltpu.VMEM((modes, freqs, samples, 2, base), v.dtype),
            pltpu.VMEM((2, 2 * samples, kmax), F32),
            pltpu.SemaphoreType.DMA((modes, freqs)),
            pltpu.SemaphoreType.DMA((modes, freqs)),
        ],
        name="project",
        cost_estimate=cost(8 * modes * samples * freqs * base * kmax, v, e),
        compiler_params=limit(MIB * 16),
    )(place, pltpu.with_memory_space_constraint(v, pltpu.HBM), pltpu.with_memory_space_constraint(e, pltpu.HBM))


def power_kernel(place_ref, retained_ref, mine_ref, theirs_ref, total_ref, stats_ref):
    half, _, kmax = mine_ref.shape
    power, kept = jnp.zeros((1, kmax), F32), jnp.zeros((1, kmax), F32)
    for j in range(half):
        total = mine_ref[j] + theirs_ref[j].astype(F32)
        total_ref[j] = total.astype(total_ref.dtype)
        keep = lax.broadcasted_iota(jnp.int32, (1, kmax), 1) < retained_ref[place_ref[0] * half + j]
        keep = keep.astype(F32)
        power += keep * jnp.sum(total * total, axis=0, keepdims=True)
        kept += keep
    stats = jnp.concatenate([power, kept], axis=0)
    stats_ref[...] = jnp.broadcast_to(stats[None], stats_ref.shape)


def power_of(place, retained, mine, theirs, peers):
    kmax = mine.shape[-1]
    return pl.pallas_call(
        power_kernel,
        in_specs=[SMEM, SMEM, VMEM, VMEM],
        out_specs=[VMEM, VMEM],
        out_shape=[
            jax.ShapeDtypeStruct(mine.shape, BF16),
            jax.ShapeDtypeStruct((peers, 2, kmax), F32),
        ],
        name="power",
        compiler_params=limit(MIB * 4),
    )(place, retained, mine, theirs)


def back_kernel(
    freq_size, place_ref, retained_ref, stats_ref, q0_ref, q1_ref, q2_ref, q3_ref, e_kept, e_hbm, coef_hbm, out_hbm, e_other, pair, flat, coef_buf, out_buf, e_sem, coef_sem, out_sem
):
    modes, freqs, samples, _, base = out_buf.shape
    kmax = q0_ref.shape[-1]
    half = modes // 2
    lanes = flat.shape[2]
    mode = [lax.rem(place_ref[0] * half + j, modes) for j in range(modes)]
    fetches = []
    for j in range(half):
        for f in range(freqs):
            fetch = pltpu.make_async_copy(e_hbm.at[mode[half + j], f], e_other.at[j, f], e_sem.at[j, f])
            fetch.start()
            fetches.append(fetch)
    stats = jnp.sum(stats_ref[...], axis=0)
    power = stats[0:1] * F32(4 / freq_size)
    count = F32(samples) * stats[1:2] * F32(2 / freq_size)
    scale = 1.0 / jnp.sqrt(power / jnp.maximum(count, 1.0) + 1e-06)
    contract = (((1,), (1,)), ((), ()))
    pending = []
    for j in range(modes):
        keep = lax.broadcasted_iota(jnp.int32, (1, kmax), 1) < retained_ref[mode[j]]
        gain = keep.astype(F32) * scale
        parts = (q0_ref, q2_ref) if j < half else (q1_ref, q3_ref)
        for part, side in zip(parts, (place_ref[1], 1 - place_ref[1])):
            coef = part[j % half].astype(F32) * gain
            at = pl.ds(pl.multiple_of(side * samples, samples), samples)
            pair[at, :kmax] = coef.astype(BF16)
            pair[at, kmax:] = times_i(coef).astype(BF16)
            for i in range(kmax // lanes):
                flat[i, at, :] = coef[:, i * lanes : (i + 1) * lanes]
        for i in range(kmax // lanes):
            for c in range(2):
                every = flat[i, pl.ds(c, samples, stride=2), :]
                coef_buf[j, c, :, i * lanes : (i + 1) * lanes] = every.astype(BF16)
        copy = pltpu.make_async_copy(coef_buf.at[j], coef_hbm.at[mode[j]], coef_sem.at[j])
        copy.start()
        pending.append(copy)
        for f in range(freqs):
            if j >= half:
                fetches[(j - half) * freqs + f].wait()
            e_ref = e_kept.at[j, f] if j < half else e_other.at[j - half, f]
            out = lax.dot_general(pair[:, :kmax], e_ref[0], contract, preferred_element_type=F32)
            out += lax.dot_general(pair[:, kmax:], e_ref[1], contract, preferred_element_type=F32)
            out_buf[j, f] = out.astype(BF16).reshape(samples, 2, base)
            copy = pltpu.make_async_copy(out_buf.at[j, f], out_hbm.at[mode[j], :, f], out_sem.at[j, f])
            copy.start()
            pending.append(copy)
    for copy in pending:
        copy.wait()


def back(place, retained, freq_size, stats, quarters, e_kept, e):
    modes, freqs, _, base, kmax = e.shape
    samples = quarters[0].shape[1]
    return pl.pallas_call(
        functools.partial(back_kernel, freq_size),
        in_specs=[SMEM, SMEM] + [VMEM] * 6 + [HBM],
        out_specs=[HBM, HBM],
        out_shape=[
            jax.ShapeDtypeStruct((modes, 2, samples, kmax), BF16),
            jax.ShapeDtypeStruct((modes, samples, freqs, 2, base), BF16),
        ],
        scratch_shapes=[
            pltpu.VMEM(e_kept.shape, e.dtype),
            pltpu.VMEM((2 * samples, 2 * kmax), BF16),
            pltpu.VMEM((kmax // 128, 2 * samples, 128), F32),
            pltpu.VMEM((modes, 2, samples, kmax), BF16),
            pltpu.VMEM((modes, freqs, samples, 2, base), BF16),
            pltpu.SemaphoreType.DMA(e_kept.shape[:2]),
            pltpu.SemaphoreType.DMA((modes,)),
            pltpu.SemaphoreType.DMA((modes, freqs)),
        ],
        name="back",
        cost_estimate=cost(8 * modes * samples * freqs * base * kmax, e, e),
        compiler_params=limit(MIB * 16),
    )(place, retained, stats, *quarters, e_kept, pltpu.with_memory_space_constraint(e, pltpu.HBM))


def per_device(visibilities, eigenmodes, retained):
    freq_size, ma_size = lax.axis_size("freq"), lax.axis_size("ma")
    index = lax.axis_index("freq").astype(jnp.int32)
    place = jnp.stack([index & 1, (index >> 1) & 1])

    def swap(x, bits):
        return lax.ppermute(x, "freq", [(i, i ^ bits) for i in range(freq_size)])

    given, kept, e_kept = project(place, visibilities, eigenmodes)
    total = kept + swap(given, 1).astype(F32)
    leaves, mine = total[0].astype(BF16), total[1]
    theirs = swap(leaves, 2)
    bit = 4
    while bit < freq_size:
        mine = mine + theirs.astype(F32)
        theirs = swap(mine.astype(BF16), bit)
        bit *= 2
    quarter, stats = power_of(place, retained, mine, theirs, ma_size * freq_size)
    stats = lax.all_to_all(stats, ("ma", "freq"), 0, 0, tiled=True)
    quarters = [quarter] + [swap(quarter, bits) for bits in (1, 2, 3)]
    return tuple(back(place, retained, freq_size, stats, quarters, e_kept, eigenmodes))


def solution(mesh):
    return jax.shard_map(
        per_device,
        mesh=mesh,
        in_specs=(P("ma", None, "freq", None, None), P("ma", "freq", None, None, None), P("ma")),
        out_specs=(P("ma", None, None, None), P("ma", None, "freq", None, None)),
        check_vma=False,
    )
```

time: 31.9 us -> 33.4 us (1.047)
  blocking collectives: 13.4 us -> 0 us
  starting transfers between devices: 3.57 us -> 11.5 us
  waiting for transfers between devices: 6.28 us -> 10.1 us
  Pallas kernels: 7.75 us -> 10.8 us
    all_to_all x1 -> x0, blocking collectives: 13.4 us -> none  [per_device(): stats = lax.all_to_all(stats, ('ma', 'freq'), 0, 0, tiled=True)]
    all_to_all x0 -> x1, starting transfers between devices: none -> 6.08 us  [per_device(): stats = lax.all_to_all(stats, ('ma', 'freq'), 0, 0, tiled=True)]
    ppermute x3 -> x5, waiting for transfers between devices: 6.28 us -> 10.1 us  [swap(): return lax.ppermute(x, 'freq', [(i, i ^ bits) for i in range(freq_size)])]
    pallas_call x1, Pallas kernels: 3.37 us -> 5.27 us  [back(): pl.pallas_call(functools.partial(back_kernel, freq_size), in_specs=[SMEM,...]
    ppermute x3 -> x5, starting transfers between devices: 3.57 us -> 5.45 us  [swap(): return lax.ppermute(x, 'freq', [(i, i ^ bits) for i in range(freq_size)])]
    pallas_call x1, Pallas kernels: 0.65 us -> 1.24 us  [power_of(): pl.pallas_call(power_kernel, in_specs=[SMEM, SMEM, VMEM, VMEM], out_specs...]
    pallas_call x1, Pallas kernels: 3.73 us -> 4.27 us  [project(): pl.pallas_call(project_kernel, in_specs=[SMEM, HBM, HBM], out_specs=[VMEM...]
  transfers between devices with their start and end apart: 3 -> 6, of which waited for: 2 -> 4; matrix products, arithmetic and copies ran while one was open for 0% -> 0% of each run, Pallas kernels for 0% -> 0%
where the time goes in v3:
time: 33.4 us; the launch traced here: 33.2 us
  starting transfers between devices  11.5 us (34%)
  Pallas kernels  10.8 us (32%)
  waiting for transfers between devices  10.1 us (30%)
  between operations  0.67 us (2%)
    ppermute x5, waiting for transfers between devices, swap(): return lax.ppermute(x, 'freq', [(i, i ^ bits) for i in range(freq_size)])  10.1 us
    all_to_all x1, starting transfers between devices, per_device(): stats = lax.all_to_all(stats, ('ma', 'freq'), 0, 0, tiled=True)  6.08 us
    ppermute x5, starting transfers between devices, swap(): return lax.ppermute(x, 'freq', [(i, i ^ bits) for i in range(freq_size)])  5.45 us
    pallas_call x1, Pallas kernels, back(): pl.pallas_call(functools.partial(back_kernel, freq_size), in_specs=[SMEM,...  5.27 us
    pallas_call x1, Pallas kernels, project(): pl.pallas_call(project_kernel, in_specs=[SMEM, HBM, HBM], out_specs=[VMEM...  4.27 us
    pallas_call x1, Pallas kernels, power_of(): pl.pallas_call(power_kernel, in_specs=[SMEM, SMEM, VMEM, VMEM], out_specs...  1.24 us
  transfers between devices with their start and end apart: 6, of which 4 were waited for; matrix products, arithmetic and copies ran while one was open for 0% of the time, Pallas kernels for 0%

profile of v3, /device:TPU:0, one launch (start us, length us, event | category | flops | bytes accessed | tf_op | source)
XLA Modules:
  0.0 33.2 jit_solution(3092160081806627460)
XLA Ops:
  0.6 0.1 pad_add_fusion.place_ref
  0.7 0.0 copy-start
  0.7 4.3 %project.1 = (bf16[2,1,192,256]{3,2,1,0:T(8,128)(2,1)S(1)}, f32[2,1,192,256]{3,2,1,0:T(8,128)S(1)}, bf16[1,4,2,512,256]{4,3,2,1,0:T(8,128)(2,1)S(1)}) custom-call(s32[2]{0:T(128)S(1)} %pad_add_fusion.place_ref, bf16[2,192,4,2,512]{4,3,2,1,0:T(2,128)(2,1)} %v_hbm.1, bf16[2,4,2,512,256]{4,3,2,1,0:T(8,128)(2,1)} %e_hbm.3), custom_call_target="tpu_custom_call" | custom-call | flops 1610612736 | bytes 7340032 | tf_op jit(solution)/shard_map/project/pallas_call | solution.py:73
  5.0 0.6 %collective-permute-start = (bf16[2,1,192,256]{3,2,1,0:T(8,128)(2,1)S(1)}, bf16[2,1,192,256]{3,2,1,0:T(8,128)(2,1)S(1)}, u32[]{:S(2)}, u32[]{:S(2)}) collective-permute-start(bf16[2,1,192,256]{3,2,1,0:T(8,128)(2,1)S(1)} %get-tuple-element.8), channel_id=1, source_target_pairs={{0,1},{1,0},{2,3},{3,2},{4,5},{5,4},{6,7},{7,6},{8,9},{9,8},{10,11... | collective-permute-start | bytes 589832 | tf_op jit(solution)/shard_map/ppermute | solution.py:209
  5.6 1.1 %collective-permute-done = bf16[2,1,192,256]{3,2,1,0:T(8,128)(2,1)S(1)} collective-permute-done((bf16[2,1,192,256]{3,2,1,0:T(8,128)(2,1)S(1)}, bf16[2,1,192,256]{3,2,1,0:T(8,128)(2,1)S(1)}, u32[]{:S(2)}, u32[]{:S(2)}) %collective-permute-start) | collective-permute-done | bytes 196640 | tf_op jit(solution)/shard_map/ppermute | solution.py:209
  6.7 2.9 %collective-permute-start.1 = (bf16[1,192,256]{2,1,0:T(8,128)(2,1)S(1)}, bf16[1,192,256]{2,1,0:T(8,128)(2,1)S(1)}, u32[]{:S(2)}, u32[]{:S(2)}) collective-permute-start(bf16[1,192,256]{2,1,0:T(8,128)(2,1)S(1)} %fusion), channel_id=1, source_target_pairs={{0,2},{1,3},{2,0},{3,1},{4,6},{5,7},{6,4},{7,5},{8,10},{9,11},{10,... | collective-permute-start | bytes 294920 | tf_op jit(solution)/shard_map/ppermute | solution.py:209
  9.6 3.1 %collective-permute-done.1.theirs_ref = bf16[1,192,256]{2,1,0:T(8,128)(2,1)S(1)} collective-permute-done((bf16[1,192,256]{2,1,0:T(8,128)(2,1)S(1)}, bf16[1,192,256]{2,1,0:T(8,128)(2,1)S(1)}, u32[]{:S(2)}, u32[]{:S(2)}) %collective-permute-start.1) | collective-permute-done | bytes 98336 | tf_op jit(solution)/shard_map/ppermute | solution.py:209
  12.7 0.0 copy-done
  12.7 1.2 %power.1 = (bf16[1,192,256]{2,1,0:T(8,128)(2,1)S(1)}, f32[32,2,256]{2,1,0:T(2,128)}) custom-call(s32[2]{0:T(128)S(1)} %pad_add_fusion.place_ref, s32[2]{0:T(128)S(1)} %copy-done, f32[1,192,256]{2,1,0:T(8,128)S(1)} %slice_bitcast_fusion.mine_ref, bf16[1,192,256]{2,1,0:T(8,128)(2,1)S(1)} %collective-permute-done.1.theirs_ref), custom_call_target="tpu_custom_call" | custom-call | tf_op jit(solution)/shard_map/power/pallas_call | solution.py:111
  14.0 6.1 %all-to-all-start = ((f32[32,2,256]{2,1,0:T(2,128)}), f32[32,2,256]{2,1,0:T(2,128)S(1)}, u32[]{:S(2)}, u32[]{:S(2)}) async-start(f32[32,2,256]{2,1,0:T(2,128)} %get-tuple-element.9), calls=%async_computation | async-start | bytes 131072 | tf_op jit(solution)/shard_map/all_to_all | solution.py:221
  20.0 1.6 %collective-permute-start.4 = (bf16[1,192,256]{2,1,0:T(8,128)(2,1)S(1)}, bf16[1,192,256]{2,1,0:T(8,128)(2,1)S(1)}, u32[]{:S(2)}, u32[]{:S(2)}) collective-permute-start(bf16[1,192,256]{2,1,0:T(8,128)(2,1)S(1)} %get-tuple-element.10.q0_ref), channel_id=1, source_target_pairs={{0,3},{1,2},{2,1},{3,0},{4,7},{5,6},{6,5},{7,4},{8,11},{9,10},{10,... | collective-permute-start | bytes 294920 | tf_op jit(solution)/shard_map/ppermute | solution.py:209
  21.6 0.4 %collective-permute-start.3 = (bf16[1,192,256]{2,1,0:T(8,128)(2,1)S(1)}, bf16[1,192,256]{2,1,0:T(8,128)(2,1)S(1)}, u32[]{:S(2)}, u32[]{:S(2)}) collective-permute-start(bf16[1,192,256]{2,1,0:T(8,128)(2,1)S(1)} %get-tuple-element.10.q0_ref), channel_id=1, source_target_pairs={{0,2},{1,3},{2,0},{3,1},{4,6},{5,7},{6,4},{7,5},{8,10},{9,11},{10,... | collective-permute-start | bytes 294920 | tf_op jit(solution)/shard_map/ppermute | solution.py:209
  22.0 0.0 collective-permute-start.2
  22.0 3.1 %collective-permute-done.4.q3_ref = bf16[1,192,256]{2,1,0:T(8,128)(2,1)S(1)} collective-permute-done((bf16[1,192,256]{2,1,0:T(8,128)(2,1)S(1)}, bf16[1,192,256]{2,1,0:T(8,128)(2,1)S(1)}, u32[]{:S(2)}, u32[]{:S(2)}) %collective-permute-start.4) | collective-permute-done | bytes 98336 | tf_op jit(solution)/shard_map/ppermute | solution.py:209
  25.1 2.9 %collective-permute-done.3.q2_ref = bf16[1,192,256]{2,1,0:T(8,128)(2,1)S(1)} collective-permute-done((bf16[1,192,256]{2,1,0:T(8,128)(2,1)S(1)}, bf16[1,192,256]{2,1,0:T(8,128)(2,1)S(1)}, u32[]{:S(2)}, u32[]{:S(2)}) %collective-permute-start.3) | collective-permute-done | bytes 98336 | tf_op jit(solution)/shard_map/ppermute | solution.py:209
  28.0 0.0 collective-permute-done.2.q1_ref
  28.0 0.0 all-to-all-done.stats_ref
  28.0 5.3 %back.1 = (bf16[2,2,192,256]{3,2,1,0:T(8,128)(2,1)}, bf16[2,192,4,2,512]{4,3,2,1,0:T(2,128)(2,1)}) custom-call(s32[2]{0:T(128)S(1)} %pad_add_fusion.place_ref, s32[2]{0:T(128)S(1)} %copy-done, f32[32,2,256]{2,1,0:T(2,128)S(1)} %all-to-all-done.stats_ref, bf16[1,192,256]{2,1,0:T(8,128)(2,1)S(1)} %get-tuple-element.10.q0_ref, ...), custom_call_target="tpu_custom_call" | custom-call | flops 1610612736 | bytes 8388608 | tf_op jit(solution)/shard_map/back/pallas_call | solution.py:179
  (3 shorter events, 0.1 us)
Async XLA Ops:
  0.7 12.0 %copy-start = (s32[2]{0:T(128)S(1)}, s32[2]{0:T(128)}, u32[]{:S(2)}) copy-start(s32[2]{0:T(128)} %retained_ref.3) | copy-start | bytes 28
  5.0 1.6 %collective-permute-start = (bf16[2,1,192,256]{3,2,1,0:T(8,128)(2,1)S(1)}, bf16[2,1,192,256]{3,2,1,0:T(8,128)(2,1)S(1)}, u32[]{:S(2)}, u32[]{:S(2)}) collective-permute-start(bf16[2,1,192,256]{3,2,1,0:T(8,128)(2,1)S(1)} %get-tuple-element.8), channel_id=1, source_target_pairs={{0,1},{1,0},{2,3},{3,2},{4,5},{5,4},{6,7},{7,6},{8,9},{9,8},{10,11... | collective-permute-start | bytes 589832 | tf_op jit(solution)/shard_map/ppermute | solution.py:209
  6.7 6.0 %collective-permute-start.1 = (bf16[1,192,256]{2,1,0:T(8,128)(2,1)S(1)}, bf16[1,192,256]{2,1,0:T(8,128)(2,1)S(1)}, u32[]{:S(2)}, u32[]{:S(2)}) collective-permute-start(bf16[1,192,256]{2,1,0:T(8,128)(2,1)S(1)} %fusion), channel_id=1, source_target_pairs={{0,2},{1,3},{2,0},{3,1},{4,6},{5,7},{6,4},{7,5},{8,10},{9,11},{10,... | collective-permute-start | bytes 294920 | tf_op jit(solution)/shard_map/ppermute | solution.py:209
  14.0 14.0 %all-to-all-start = ((f32[32,2,256]{2,1,0:T(2,128)}), f32[32,2,256]{2,1,0:T(2,128)S(1)}, u32[]{:S(2)}, u32[]{:S(2)}) async-start(f32[32,2,256]{2,1,0:T(2,128)} %get-tuple-element.9), calls=%async_computation | async-start | bytes 131072 | tf_op jit(solution)/shard_map/all_to_all | solution.py:221
  20.0 5.1 %collective-permute-start.4 = (bf16[1,192,256]{2,1,0:T(8,128)(2,1)S(1)}, bf16[1,192,256]{2,1,0:T(8,128)(2,1)S(1)}, u32[]{:S(2)}, u32[]{:S(2)}) collective-permute-start(bf16[1,192,256]{2,1,0:T(8,128)(2,1)S(1)} %get-tuple-element.10.q0_ref), channel_id=1, source_target_pairs={{0,3},{1,2},{2,1},{3,0},{4,7},{5,6},{6,5},{7,4},{8,11},{9,10},{10,... | collective-permute-start | bytes 294920 | tf_op jit(solution)/shard_map/ppermute | solution.py:209
  21.6 6.4 %collective-permute-start.3 = (bf16[1,192,256]{2,1,0:T(8,128)(2,1)S(1)}, bf16[1,192,256]{2,1,0:T(8,128)(2,1)S(1)}, u32[]{:S(2)}, u32[]{:S(2)}) collective-permute-start(bf16[1,192,256]{2,1,0:T(8,128)(2,1)S(1)} %get-tuple-element.10.q0_ref), channel_id=1, source_target_pairs={{0,2},{1,3},{2,0},{3,1},{4,6},{5,7},{6,4},{7,5},{8,10},{9,11},{10,... | collective-permute-start | bytes 294920 | tf_op jit(solution)/shard_map/ppermute | solution.py:209
  22.0 6.0 %collective-permute-start.2 = (bf16[1,192,256]{2,1,0:T(8,128)(2,1)S(1)}, bf16[1,192,256]{2,1,0:T(8,128)(2,1)S(1)}, u32[]{:S(2)}, u32[]{:S(2)}) collective-permute-start(bf16[1,192,256]{2,1,0:T(8,128)(2,1)S(1)} %get-tuple-element.10.q0_ref), channel_id=1, source_target_pairs={{0,1},{1,0},{2,3},{3,2},{4,5},{5,4},{6,7},{7,6},{8,9},{9,8},{10,11... | collective-permute-start | bytes 294920 | tf_op jit(solution)/shard_map/ppermute | solution.py:209

commit v4 on v2

--- a/solution.py
+++ b/solution.py
@@ -9,14 +9,18 @@
 
 F32 = jnp.float32
 BF16 = jnp.bfloat16
+TOTAL = F32
 VMEM = pl.BlockSpec(memory_space=pltpu.VMEM)
-SMEM = pl.BlockSpec(memory_space=pltpu.SMEM)
 HBM = pl.BlockSpec(memory_space=pltpu.HBM)
 MIB = 1 << 20
 
 
 def limit(vmem):
     return pltpu.CompilerParams(vmem_limit_bytes=vmem)
+
+
+def side():
+    return (lax.axis_index("freq") & 1).astype(jnp.int32)
 
 
 def times_i(x):
@@ -26,11 +30,11 @@
     return jnp.where(even, -up, down)
 
 
-def project_kernel(first_ref, v_hbm, e_hbm, given_ref, kept_ref, e_ref, v_buf, acc, v_sem, e_sem):
+def project_kernel(v_hbm, e_hbm, given_ref, kept_ref, e_ref, v_buf, acc, v_sem, e_sem):
     modes, freqs, samples, _, base = v_buf.shape
     rows = 2 * samples
     half = modes // 2
-    mode = [lax.rem(first_ref[0] + j, modes) for j in range(modes)]
+    mode = [lax.rem((1 - side()) * half + j, modes) for j in range(modes)]
     copies = []
     for j in range(modes):
         for f in range(freqs):
@@ -58,13 +62,13 @@
                 out_ref[pl.ds(j % half * rows, rows), :] = out.astype(out_ref.dtype)
 
 
-def project(first, v, e):
+def project(v, e):
     modes, samples, freqs, _, base = v.shape
     kmax = e.shape[-1]
     rows = modes // 2 * 2 * samples
     return pl.pallas_call(
         project_kernel,
-        in_specs=[SMEM, HBM, HBM],
+        in_specs=[HBM, HBM],
         out_specs=[VMEM, VMEM, VMEM],
         out_shape=[
             jax.ShapeDtypeStruct((rows, kmax), BF16),
@@ -79,12 +83,11 @@
         ],
         name="project",
         compiler_params=limit(MIB * 16),
-    )(first, pltpu.with_memory_space_constraint(v, pltpu.HBM), pltpu.with_memory_space_constraint(e, pltpu.HBM))
-
-
-def power_kernel(first_ref, retained_ref, mine_ref, theirs_ref, total_ref, stats_ref):
-    modes = retained_ref.shape[0]
-    half = modes // 2
+    )(pltpu.with_memory_space_constraint(v, pltpu.HBM), pltpu.with_memory_space_constraint(e, pltpu.HBM))
+
+
+def power_kernel(keep_ref, mine_ref, theirs_ref, total_ref, stats_ref):
+    half = keep_ref.shape[0] // 2
     kmax = mine_ref.shape[1]
     rows = mine_ref.shape[0] // half
     stats = jnp.zeros((2, kmax), F32)
@@ -92,30 +95,29 @@
         at = pl.ds(j * rows, rows)
         total = mine_ref[at, :].astype(F32) + theirs_ref[at, :].astype(F32)
         total_ref[at, :] = total.astype(total_ref.dtype)
-        keep = lax.broadcasted_iota(jnp.int32, (1, kmax), 1) < retained_ref[lax.rem(first_ref[0] + j, modes)]
-        keep = keep.astype(F32)
+        keep = jnp.where(side() == 0, keep_ref[j : j + 1], keep_ref[half + j : half + j + 1])
         power = keep * jnp.sum(total * total, axis=0, keepdims=True)
         stats += jnp.concatenate([power, keep], axis=0)
     stats_ref[...] = jnp.broadcast_to(stats[None], stats_ref.shape)
 
 
-def power_of(first, retained, mine, theirs, peers):
+def power_of(keep, mine, theirs, peers):
     rows, kmax = mine.shape
     return pl.pallas_call(
         power_kernel,
-        in_specs=[SMEM, SMEM, VMEM, VMEM],
+        in_specs=[VMEM, VMEM, VMEM],
         out_specs=[VMEM, VMEM],
         out_shape=[
-            jax.ShapeDtypeStruct((rows, kmax), BF16),
+            jax.ShapeDtypeStruct((rows, kmax), TOTAL),
             jax.ShapeDtypeStruct((peers, 2, kmax), F32),
         ],
         name="power",
         compiler_params=limit(MIB * 4),
-    )(first, retained, mine, theirs)
+    )(keep, mine, theirs)
 
 
 def back_kernel(
-    copies, first_ref, retained_ref, stats_ref, mine_ref, other_ref, e_ref, coef_hbm, out_hbm, pair, flat, coef_buf, out_buf, coef_sem, out_sem
+    copies, keep_ref, stats_ref, mine_ref, other_ref, e_ref, coef_hbm, out_hbm, pair, flat, coef_buf, out_buf, coef_sem, out_sem
 ):
     modes, freqs, samples, _, base = out_buf.shape
     kmax = mine_ref.shape[1]
@@ -128,10 +130,10 @@
     contract = (((1,), (1,)), ((), ()))
     pending = []
     for j in range(modes):
-        mode = lax.rem(first_ref[0] + j, modes)
+        mode = lax.rem(side() * half + j, modes)
         proj_ref = mine_ref if j < half else other_ref
-        keep = lax.broadcasted_iota(jnp.int32, (1, kmax), 1) < retained_ref[mode]
-        gain = keep.astype(F32) * scale
+        other = (j + half) % modes
+        gain = jnp.where(side() == 0, keep_ref[j : j + 1], keep_ref[other : other + 1]) * scale
         coef = proj_ref[pl.ds(j % half * rows, rows), :].astype(F32) * gain
         pair[:, :kmax] = coef.astype(BF16)
         pair[:, kmax:] = times_i(coef).astype(BF16)
@@ -154,13 +156,13 @@
         copy.wait()
 
 
-def back(first, retained, copies, stats, mine, other, e):
+def back(keep, copies, stats, mine, other, e):
     kmax = mine.shape[1]
     modes, freqs, _, base, _ = e.shape
     samples = mine.shape[0] // modes
     return pl.pallas_call(
         functools.partial(back_kernel, copies),
-        in_specs=[SMEM, SMEM, VMEM, VMEM, VMEM, VMEM],
+        in_specs=[VMEM] * 5,
         out_specs=[HBM, HBM],
         out_shape=[
             jax.ShapeDtypeStruct((modes, 2, samples, kmax), BF16),
@@ -176,28 +178,27 @@
         ],
         name="back",
         compiler_params=limit(MIB * 16),
-    )(first, retained, stats, mine, other, e)
+    )(keep, stats, mine, other, e)
 
 
 def per_device(visibilities, eigenmodes, retained):
     freq_size, ma_size = lax.axis_size("freq"), lax.axis_size("ma")
-    half = visibilities.shape[0] // 2
-    side = (lax.axis_index("freq") & 1).astype(jnp.int32).reshape(1)
+    ranks = jnp.arange(eigenmodes.shape[-1], dtype=jnp.int32)
+    keep = (ranks[None, :] < retained[:, None]).astype(F32)
 
     def swap(x, bit):
         return lax.ppermute(x, "freq", [(i, i ^ bit) for i in range(freq_size)])
 
-    first_kept, first_given = side * half, (1 - side) * half
-    given, kept, e_vmem = project(first_given, visibilities, eigenmodes)
+    given, kept, e_vmem = project(visibilities, eigenmodes)
     total = (kept + swap(given, 1).astype(F32)).astype(BF16)
     bit = 2
     while 2 * bit < freq_size:
         total = (total.astype(F32) + swap(total, bit).astype(F32)).astype(BF16)
         bit *= 2
-    mine, stats = power_of(first_kept, retained, total, swap(total, bit), ma_size * freq_size)
+    mine, stats = power_of(keep, total, swap(total, bit), ma_size * freq_size)
     other = swap(mine, 1)
     stats = lax.all_to_all(stats, ("ma", "freq"), 0, 0, tiled=True)
-    coefficients, filtered = back(first_kept, retained, freq_size // 2, stats, mine, other, e_vmem)
+    coefficients, filtered = back(keep, freq_size // 2, stats, mine, other, e_vmem)
     return coefficients, filtered
 
 

time: 31.9 us -> 30.7 us (0.962)
  Pallas kernels: 7.75 us -> 6.62 us
    pallas_call x3, Pallas kernels: 7.75 us -> 6.62 us  [the longest x1 3.74 us: project(): pl.pallas_call(project_kernel, in_specs=[HBM, HBM], out_specs=[VMEM, VMEM...]
where the time goes in v4:
time: 30.7 us; the launch traced here: 30.6 us
  blocking collectives  13.4 us (44%)
  Pallas kernels  6.62 us (22%)
  waiting for transfers between devices  6.2 us (20%)
  starting transfers between devices  3.57 us (12%)
  between operations  0.66 us (2%)
    all_to_all x1, blocking collectives, per_device(): stats = lax.all_to_all(stats, ('ma', 'freq'), 0, 0, tiled=True)  13.4 us
    ppermute x3, waiting for transfers between devices, swap(): return lax.ppermute(x, 'freq', [(i, i ^ bit) for i in range(freq_size)])  6.2 us
    pallas_call x1, Pallas kernels, project(): pl.pallas_call(project_kernel, in_specs=[HBM, HBM], out_specs=[VMEM, VMEM...  3.74 us
    ppermute x3, starting transfers between devices, swap(): return lax.ppermute(x, 'freq', [(i, i ^ bit) for i in range(freq_size)])  3.57 us
    pallas_call x1, Pallas kernels, back(): pl.pallas_call(functools.partial(back_kernel, copies), in_specs=[VMEM] *...  2.79 us
  transfers between devices with their start and end apart: 3, of which 2 were waited for; matrix products, arithmetic and copies ran while one was open for 0% of the time, Pallas kernels for 0%

profile of v4, /device:TPU:0, one launch (start us, length us, event | category | flops | bytes accessed | tf_op | source)
XLA Modules:
  0.0 30.6 jit_solution(16745239308840045104)
XLA Ops:
  0.6 0.0 copy-start
  0.6 3.7 %project.1 = (bf16[384,256]{1,0:T(8,128)(2,1)S(1)}, f32[384,256]{1,0:T(8,128)S(1)}, bf16[2,4,2,512,256]{4,3,2,1,0:T(8,128)(2,1)S(1)}) custom-call(bf16[2,192,4,2,512]{4,3,2,1,0:T(2,128)(2,1)} %v_hbm.1, bf16[2,4,2,512,256]{4,3,2,1,0:T(8,128)(2,1)} %e_hbm.1), custom_call_target="tpu_custom_call" | custom-call | tf_op jit(solution)/shard_map/project/pallas_call | solution.py:69
  4.4 0.6 %collective-permute-start = (bf16[384,256]{1,0:T(8,128)(2,1)S(1)}, bf16[384,256]{1,0:T(8,128)(2,1)S(1)}, u32[]{:S(2)}, u32[]{:S(2)}) collective-permute-start(bf16[384,256]{1,0:T(8,128)(2,1)S(1)} %get-tuple-element.8), channel_id=1, source_target_pairs={{0,1},{1,0},{2,3},{3,2},{4,5},{5,4},{6,7},{7,6},{8,9},{9,8},{10,11... | collective-permute-start | bytes 589832 | tf_op jit(solution)/shard_map/ppermute | solution.py:190
  4.9 1.1 %collective-permute-done = bf16[384,256]{1,0:T(8,128)(2,1)S(1)} collective-permute-done((bf16[384,256]{1,0:T(8,128)(2,1)S(1)}, bf16[384,256]{1,0:T(8,128)(2,1)S(1)}, u32[]{:S(2)}, u32[]{:S(2)}) %collective-permute-start) | collective-permute-done | bytes 196640 | tf_op jit(solution)/shard_map/ppermute | solution.py:190
  6.0 0.1 add_convert_fusion.mine_ref
  6.1 2.9 %collective-permute-start.1 = (bf16[384,256]{1,0:T(8,128)(2,1)S(1)}, bf16[384,256]{1,0:T(8,128)(2,1)S(1)}, u32[]{:S(2)}, u32[]{:S(2)}) collective-permute-start(bf16[384,256]{1,0:T(8,128)(2,1)S(1)} %add_convert_fusion.mine_ref), channel_id=1, source_target_pairs={{0,2},{1,3},{2,0},{3,1},{4,6},{5,7},{6,4},{7,5},{8,10},{9,11},{10,... | collective-permute-start | bytes 589832 | tf_op jit(solution)/shard_map/ppermute | solution.py:190
  9.0 0.0 copy-done
  9.0 0.1 compare_convert_fusion.keep_ref
  9.1 5.1 %collective-permute-done.1.theirs_ref = bf16[384,256]{1,0:T(8,128)(2,1)S(1)} collective-permute-done((bf16[384,256]{1,0:T(8,128)(2,1)S(1)}, bf16[384,256]{1,0:T(8,128)(2,1)S(1)}, u32[]{:S(2)}, u32[]{:S(2)}) %collective-permute-start.1) | collective-permute-done | bytes 196640 | tf_op jit(solution)/shard_map/ppermute | solution.py:190
  14.2 0.1 power.1
  14.3 0.1 collective-permute-start.2
  14.4 13.4 %all_to_all.5.stats_ref = f32[32,2,256]{2,1,0:T(2,128)S(1)} all-to-all(f32[32,2,256]{2,1,0:T(2,128)S(1)} %get-tuple-element.9), channel_id=1, replica_groups=mesh['ma'=8,'freq'=4] {'ma','freq'}, dimensions={0} | all-to-all | bytes 131072 | tf_op jit(solution)/shard_map/all_to_all | solution.py:200
  27.8 0.0 collective-permute-done.2.other_ref
  27.8 2.8 %back.1 = (bf16[2,2,192,256]{3,2,1,0:T(8,128)(2,1)}, bf16[2,192,4,2,512]{4,3,2,1,0:T(2,128)(2,1)}) custom-call(f32[2,256]{1,0:T(2,128)S(1)} %compare_convert_fusion.keep_ref, f32[32,2,256]{2,1,0:T(2,128)S(1)} %all_to_all.5.stats_ref, f32[384,256]{1,0:T(8,128)S(1)} %get-tuple-element.10.mine_ref, f32[384,256]{1,0:T(8,128)S(1)} %collective-permute-done.2.other_ref, ...), custom_call_target="tpu_custom_call" | custom-call | tf_op jit(solution)/shard_map/back/pallas_call | solution.py:163
Async XLA Ops:
  0.6 8.4 %copy-start = (s32[2]{0:T(128)S(1)}, s32[2]{0:T(128)}, u32[]{:S(2)}) copy-start(s32[2]{0:T(128)} %param.5) | copy-start | bytes 28
  4.4 1.6 %collective-permute-start = (bf16[384,256]{1,0:T(8,128)(2,1)S(1)}, bf16[384,256]{1,0:T(8,128)(2,1)S(1)}, u32[]{:S(2)}, u32[]{:S(2)}) collective-permute-start(bf16[384,256]{1,0:T(8,128)(2,1)S(1)} %get-tuple-element.8), channel_id=1, source_target_pairs={{0,1},{1,0},{2,3},{3,2},{4,5},{5,4},{6,7},{7,6},{8,9},{9,8},{10,11... | collective-permute-start | bytes 589832 | tf_op jit(solution)/shard_map/ppermute | solution.py:190
  6.1 8.1 %collective-permute-start.1 = (bf16[384,256]{1,0:T(8,128)(2,1)S(1)}, bf16[384,256]{1,0:T(8,128)(2,1)S(1)}, u32[]{:S(2)}, u32[]{:S(2)}) collective-permute-start(bf16[384,256]{1,0:T(8,128)(2,1)S(1)} %add_convert_fusion.mine_ref), channel_id=1, source_target_pairs={{0,2},{1,3},{2,0},{3,1},{4,6},{5,7},{6,4},{7,5},{8,10},{9,11},{10,... | collective-permute-start | bytes 589832 | tf_op jit(solution)/shard_map/ppermute | solution.py:190
  14.3 13.5 %collective-permute-start.2 = (f32[384,256]{1,0:T(8,128)S(1)}, f32[384,256]{1,0:T(8,128)S(1)}, u32[]{:S(2)}, u32[]{:S(2)}) collective-permute-start(f32[384,256]{1,0:T(8,128)S(1)} %get-tuple-element.10.mine_ref), channel_id=1, source_target_pairs={{0,1},{1,0},{2,3},{3,2},{4,5},{5,4},{6,7},{7,6},{8,9},{9,8},{10,11... | collective-permute-start | bytes 1179656 | tf_op jit(solution)/shard_map/ppermute | solution.py:190

commit v5 on v4

v5 whole, which is shorter than its diff:
```python
import functools

import jax
import jax.numpy as jnp
from jax import lax
from jax.experimental import pallas as pl
from jax.experimental.pallas import tpu as pltpu
from jax.sharding import PartitionSpec as P

F32 = jnp.float32
BF16 = jnp.bfloat16
VMEM = pl.BlockSpec(memory_space=pltpu.VMEM)
HBM = pl.BlockSpec(memory_space=pltpu.HBM)
MIB = 1 << 20


def limit(vmem):
    return pltpu.CompilerParams(vmem_limit_bytes=vmem)


def cost(flops, *arrays):
    moved = sum(a.size * a.dtype.itemsize for a in arrays)
    return pl.CostEstimate(flops=flops, bytes_accessed=moved, transcendentals=0)


def side():
    return (lax.axis_index("freq") & 1).astype(jnp.int32)


def times_i(x):
    up = pltpu.roll(x, x.shape[0] - 1, 0)
    down = pltpu.roll(x, 1, 0)
    even = (lax.broadcasted_iota(jnp.int32, x.shape, 0) & 1) == 0
    return jnp.where(even, -up, down)


def finish(j, by_re, by_im, give_ref, keep_ref):
    out = by_re - times_i(by_im)
    half = out.shape[0] // 2
    low, high = out[:half], out[half:]
    give_ref[j] = jnp.where(side() == 0, high, low).astype(give_ref.dtype)
    keep_ref[j] = jnp.where(side() == 0, low, high).astype(keep_ref.dtype)


def project_kernel(v_hbm, e_hbm, give_ref, keep_ref, part_ref, v_last, e_ref, v_buf, acc, v_sem, e_sem):
    modes, freqs = v_sem.shape
    samples, _, base = v_buf.shape[2:]
    half = modes // 2
    copies = []
    for m in range(modes):
        for f in range(freqs):
            late = m >= half and f == freqs - 1
            v_to = v_last.at[m - half] if late else v_buf.at[m, f]
            e_copy = pltpu.make_async_copy(e_hbm.at[m, f], e_ref.at[m, f], e_sem.at[m, f])
            v_copy = pltpu.make_async_copy(v_hbm.at[m, :, f], v_to, v_sem.at[m, f])
            e_copy.start()
            v_copy.start()
            copies.append((e_copy, v_copy))
    for m in range(modes):
        for f in range(freqs):
            for copy in copies[m * freqs + f]:
                copy.wait()
            if m >= half and f == freqs - 1:
                continue
            x = v_buf[m, f].reshape(2 * samples, base)
            by_re = jnp.dot(x, e_ref[m, f, 0], preferred_element_type=F32)
            by_im = jnp.dot(x, e_ref[m, f, 1], preferred_element_type=F32)
            sums = part_ref.at[m - half] if m >= half else acc
            if f > 0:
                by_re += sums[0]
                by_im += sums[1]
            if m >= half or f < freqs - 1:
                sums[0] = by_re
                sums[1] = by_im
            else:
                finish(m, by_re, by_im, give_ref, keep_ref)


def project(v, e):
    modes, samples, freqs, _, base = v.shape
    kmax = e.shape[-1]
    half = modes // 2
    return pl.pallas_call(
        project_kernel,
        in_specs=[HBM, HBM],
        out_specs=[VMEM] * 5,
        out_shape=[
            jax.ShapeDtypeStruct((half, samples, kmax), BF16),
            jax.ShapeDtypeStruct((half, samples, kmax), F32),
            jax.ShapeDtypeStruct((half, 2, 2 * samples, kmax), F32),
            jax.ShapeDtypeStruct((half, samples, 2, base), v.dtype),
            jax.ShapeDtypeStruct(e.shape, e.dtype),
        ],
        scratch_shapes=[
            pltpu.VMEM((modes, freqs, samples, 2, base), v.dtype),
            pltpu.VMEM((2, 2 * samples, kmax), F32),
            pltpu.SemaphoreType.DMA((modes, freqs)),
            pltpu.SemaphoreType.DMA((modes, freqs)),
        ],
        name="project",
        compiler_params=limit(MIB * 16),
        cost_estimate=cost(8 * modes * samples * freqs * base * kmax, v, e),
    )(pltpu.with_memory_space_constraint(v, pltpu.HBM), pltpu.with_memory_space_constraint(e, pltpu.HBM))


def rest_kernel(part_ref, v_ref, e_ref, give_ref, keep_ref):
    modes, freqs = e_ref.shape[:2]
    half, samples, _, base = v_ref.shape
    for j in range(half):
        x = v_ref[j].reshape(2 * samples, base)
        by_re = part_ref[j, 0] + jnp.dot(x, e_ref[half + j, freqs - 1, 0], preferred_element_type=F32)
        by_im = part_ref[j, 1] + jnp.dot(x, e_ref[half + j, freqs - 1, 1], preferred_element_type=F32)
        finish(j, by_re, by_im, give_ref, keep_ref)


def rest(part, v, e):
    half, samples, _, base = v.shape
    kmax = e.shape[-1]
    return pl.pallas_call(
        rest_kernel,
        in_specs=[VMEM] * 3,
        out_specs=[VMEM] * 2,
        out_shape=[
            jax.ShapeDtypeStruct((half, samples, kmax), BF16),
            jax.ShapeDtypeStruct((half, samples, kmax), F32),
        ],
        name="rest",
        compiler_params=limit(MIB * 4),
        cost_estimate=cost(8 * half * samples * base * kmax, v),
    )(part, v, e)


def power_kernel(keep_ref, a_ref, a_their_ref, b_ref, b_their_ref, total_ref, stats_ref):
    half, _, kmax = a_ref.shape
    stats = jnp.zeros((2, kmax), F32)
    for m in range(2 * half):
        mine, theirs = (a_ref, a_their_ref) if m < half else (b_ref, b_their_ref)
        total = mine[m % half].astype(F32) + theirs[m % half].astype(F32)
        total_ref[m] = total
        keep = keep_ref[m : m + 1]
        power = keep * jnp.sum(total * total, axis=0, keepdims=True)
        stats += jnp.concatenate([power, keep], axis=0)
    stats_ref[...] = jnp.broadcast_to(stats[None], stats_ref.shape)


def power_of(keep, pairs, peers):
    half, rows, kmax = pairs[0].shape
    return pl.pallas_call(
        power_kernel,
        in_specs=[VMEM] * 5,
        out_specs=[VMEM] * 2,
        out_shape=[
            jax.ShapeDtypeStruct((2 * half, rows, kmax), F32),
            jax.ShapeDtypeStruct((peers, 2, kmax), F32),
        ],
        name="power",
        compiler_params=limit(MIB * 4),
    )(keep, *pairs)


def back_kernel(
    freq_size, keep_ref, stats_ref, mine_ref, other_ref, e_ref, coef_hbm, out_hbm, pair, flat, coef_buf, out_buf, coef_sem, out_sem
):
    modes, freqs, samples, _, base = out_buf.shape
    kmax = mine_ref.shape[-1]
    lanes = flat.shape[2]
    stats = jnp.sum(stats_ref[...], axis=0)
    power, count = stats[0:1] * F32(2 / freq_size), F32(samples) * (stats[1:2] * F32(1 / freq_size))
    scale = 1.0 / jnp.sqrt(power / jnp.maximum(count, 1.0) + 1e-06)
    contract = (((1,), (1,)), ((), ()))
    pending = []

    def send(src, dst, sem):
        copy = pltpu.make_async_copy(src, dst, sem)
        copy.start()
        pending.append(copy)

    for m in range(modes):
        gain = keep_ref[m : m + 1] * scale
        mine, other = mine_ref[m] * gain, other_ref[m] * gain
        for h in range(2):
            coef = jnp.where(side() == h, mine, other)
            at = slice(h * samples, (h + 1) * samples)
            pair[at, :kmax] = coef.astype(BF16)
            pair[at, kmax:] = times_i(coef).astype(BF16)
            for i in range(kmax // lanes):
                flat[i, at, :] = coef[:, i * lanes : (i + 1) * lanes]
        for f in range(freqs):
            out = lax.dot_general(pair[:, :kmax], e_ref[m, f, 0], contract, preferred_element_type=F32)
            out += lax.dot_general(pair[:, kmax:], e_ref[m, f, 1], contract, preferred_element_type=F32)
            out_buf[m, f] = out.astype(BF16).reshape(samples, 2, base)
            if f == 0:
                for i in range(kmax // lanes):
                    for part in range(2):
                        every = flat[i, pl.ds(part, samples, stride=2), :]
                        coef_buf[m, part, :, i * lanes : (i + 1) * lanes] = every.astype(BF16)
                send(coef_buf.at[m], coef_hbm.at[m], coef_sem.at[m])
            send(out_buf.at[m, f], out_hbm.at[m, :, f], out_sem.at[m, f])
    for copy in pending:
        copy.wait()


def back(keep, freq_size, stats, mine, other, e):
    modes, freqs, _, base, kmax = e.shape
    samples = mine.shape[1]
    return pl.pallas_call(
        functools.partial(back_kernel, freq_size),
        in_specs=[VMEM] * 5,
        out_specs=[HBM, HBM],
        out_shape=[
            jax.ShapeDtypeStruct((modes, 2, samples, kmax), BF16),
            jax.ShapeDtypeStruct((modes, samples, freqs, 2, base), BF16),
        ],
        scratch_shapes=[
            pltpu.VMEM((2 * samples, 2 * kmax), BF16),
            pltpu.VMEM((kmax // 128, 2 * samples, 128), F32),
            pltpu.VMEM((modes, 2, samples, kmax), BF16),
            pltpu.VMEM((modes, freqs, samples, 2, base), BF16),
            pltpu.SemaphoreType.DMA((modes,)),
            pltpu.SemaphoreType.DMA((modes, freqs)),
        ],
        name="back",
        compiler_params=limit(MIB * 16),
    )(keep, stats, mine, other, e)


def per_device(visibilities, eigenmodes, retained):
    freq_size, ma_size = lax.axis_size("freq"), lax.axis_size("ma")
    ranks = jnp.arange(eigenmodes.shape[-1], dtype=jnp.int32)
    keep = (ranks[None, :] < retained[:, None]).astype(F32)

    def swap(x, bit):
        return lax.ppermute(x, "freq", [(i, i ^ bit) for i in range(freq_size)])

    give_a, keep_a, part, v_last, e_vmem = project(visibilities, eigenmodes)
    give_b, keep_b = rest(part, v_last, e_vmem)
    pairs = []
    for give, kept in ((give_a, keep_a), (give_b, keep_b)):
        total = (kept + swap(give, 1).astype(F32)).astype(BF16)
        bit = 2
        while 2 * bit < freq_size:
            total = (total.astype(F32) + swap(total, bit).astype(F32)).astype(BF16)
            bit *= 2
        pairs += [total, swap(total, bit)]
    mine, stats = power_of(keep, pairs, ma_size * freq_size)
    other = swap(mine, 1)
    stats = lax.all_to_all(stats, ("ma", "freq"), 0, 0, tiled=True)
    return tuple(back(keep, freq_size, stats, mine, other, e_vmem))


def solution(mesh):
    return jax.shard_map(
        per_device,
        mesh=mesh,
        in_specs=(P("ma", None, "freq", None, None), P("ma", "freq", None, None, None), P("ma")),
        out_specs=(P("ma", None, None, None), P("ma", None, "freq", None, None)),
        check_vma=False,
    )
```

time: 30.7 us -> 30.4 us (level)
  waiting for transfers between devices: 6.2 us -> 4.94 us
  starting transfers between devices: 3.57 us -> 4.26 us
    ppermute x3 -> x5, waiting for transfers between devices: 6.2 us -> 4.94 us  [swap(): return lax.ppermute(x, 'freq', [(i, i ^ bit) for i in range(freq_size)])]
    ppermute x3 -> x5, starting transfers between devices: 3.57 us -> 4.26 us  [swap(): return lax.ppermute(x, 'freq', [(i, i ^ bit) for i in range(freq_size)])]
    pallas_call x3 -> x4, Pallas kernels: 6.62 us -> 6.83 us  [the longest x1 3.47 us: project(): pl.pallas_call(project_kernel, in_specs=[HBM, HBM], out_specs=[VMEM] * 5,...]
  transfers between devices with their start and end apart: 3 -> 5, of which waited for: 2 -> 3; matrix products, arithmetic and copies ran while one was open for 0% -> 0% of each run, Pallas kernels for 0% -> 1%
where the time goes in v5:
time: 30.4 us; the launch traced here: 30.2 us
  blocking collectives  13.4 us (44%)
  Pallas kernels  6.83 us (22%)
  waiting for transfers between devices  4.94 us (16%)
  starting transfers between devices  4.26 us (14%)
  between operations  0.68 us (2%)
    all_to_all x1, blocking collectives, per_device(): stats = lax.all_to_all(stats, ('ma', 'freq'), 0, 0, tiled=True)  13.4 us
    ppermute x5, waiting for transfers between devices, swap(): return lax.ppermute(x, 'freq', [(i, i ^ bit) for i in range(freq_size)])  4.94 us
    ppermute x5, starting transfers between devices, swap(): return lax.ppermute(x, 'freq', [(i, i ^ bit) for i in range(freq_size)])  4.26 us
    pallas_call x1, Pallas kernels, project(): pl.pallas_call(project_kernel, in_specs=[HBM, HBM], out_specs=[VMEM] * 5,...  3.47 us
    pallas_call x1, Pallas kernels, back(): pl.pallas_call(functools.partial(back_kernel, freq_size), in_specs=[VMEM]...  2.84 us
  transfers between devices with their start and end apart: 5, of which 3 were waited for; matrix products, arithmetic and copies ran while one was open for 0% of the time, Pallas kernels for 1%

profile of v5, /device:TPU:0, one launch (start us, length us, event | category | flops | bytes accessed | tf_op | source)
XLA Modules:
  0.0 30.2 jit_solution(9594015592815965854)
XLA Ops:
  0.6 3.5 %project.1 = (bf16[1,192,256]{2,1,0:T(8,128)(2,1)S(1)}, f32[1,192,256]{2,1,0:T(8,128)S(1)}, f32[1,2,384,256]{3,2,1,0:T(8,128)S(1)}, bf16[1,192,2,512]{3,2,1,0:T(2,128)(2,1)S(1)}, bf16[2,4,2,512,256]{4,3,2,1,0:T(8,128)(2,1)S(1)}) custom-call(bf16[2,192,4,2,512]{4,3,2,1,0:T(2,128)(2,1)} %v_hbm.1, bf16[2,4,2,512,256]{4,3,2,1,0:T(8,128)(2,1)} %e_hbm.1), custom_call_target="tpu_custom_call" | custom-call | flops 1610612736 | bytes 7340032 | tf_op jit(solution)/shard_map/project/pallas_call | solution.py:83
  4.1 0.0 copy-start
  4.1 0.5 %collective-permute-start = (bf16[1,192,256]{2,1,0:T(8,128)(2,1)S(1)}, bf16[1,192,256]{2,1,0:T(8,128)(2,1)S(1)}, u32[]{:S(2)}, u32[]{:S(2)}) collective-permute-start(bf16[1,192,256]{2,1,0:T(8,128)(2,1)S(1)} %get-tuple-element.12), channel_id=1, source_target_pairs={{0,1},{1,0},{2,3},{3,2},{4,5},{5,4},{6,7},{7,6},{8,9},{9,8},{10,11... | collective-permute-start | bytes 294920 | tf_op jit(solution)/shard_map/ppermute | solution.py:233
  4.7 0.4 %rest.1 = (bf16[1,192,256]{2,1,0:T(8,128)(2,1)S(1)}, f32[1,192,256]{2,1,0:T(8,128)S(1)}) custom-call(f32[1,2,384,256]{3,2,1,0:T(8,128)S(1)} %get-tuple-element.13.part_ref, bf16[1,192,2,512]{3,2,1,0:T(2,128)(2,1)S(1)} %get-tuple-element.14.v_ref, bf16[2,4,2,512,256]{4,3,2,1,0:T(8,128)(2,1)S(1)} %get-tuple-element.15.e_ref), custom_call_target="tpu_custom_call" | custom-call | flops 201326592 | bytes 393216 | tf_op jit(solution)/shard_map/rest/pallas_call | solution.py:119
  5.1 0.1 collective-permute-start.2
  5.2 0.4 %collective-permute-done = bf16[1,192,256]{2,1,0:T(8,128)(2,1)S(1)} collective-permute-done((bf16[1,192,256]{2,1,0:T(8,128)(2,1)S(1)}, bf16[1,192,256]{2,1,0:T(8,128)(2,1)S(1)}, u32[]{:S(2)}, u32[]{:S(2)}) %collective-permute-start) | collective-permute-done | bytes 98336 | tf_op jit(solution)/shard_map/ppermute | solution.py:233
  5.6 2.9 %collective-permute-start.1 = (bf16[1,192,256]{2,1,0:T(8,128)(2,1)S(1)}, bf16[1,192,256]{2,1,0:T(8,128)(2,1)S(1)}, u32[]{:S(2)}, u32[]{:S(2)}) collective-permute-start(bf16[1,192,256]{2,1,0:T(8,128)(2,1)S(1)} %add_convert_fusion.1.a_ref), channel_id=1, source_target_pairs={{0,2},{1,3},{2,0},{3,1},{4,6},{5,7},{6,4},{7,5},{8,10},{9,11},{10,... | collective-permute-start | bytes 294920 | tf_op jit(solution)/shard_map/ppermute | solution.py:233
  8.6 0.0 collective-permute-done.2
  8.6 0.6 %collective-permute-start.3 = (bf16[1,192,256]{2,1,0:T(8,128)(2,1)S(1)}, bf16[1,192,256]{2,1,0:T(8,128)(2,1)S(1)}, u32[]{:S(2)}, u32[]{:S(2)}) collective-permute-start(bf16[1,192,256]{2,1,0:T(8,128)(2,1)S(1)} %add_convert_fusion.b_ref), channel_id=1, source_target_pairs={{0,2},{1,3},{2,0},{3,1},{4,6},{5,7},{6,4},{7,5},{8,10},{9,11},{10,... | collective-permute-start | bytes 294920 | tf_op jit(solution)/shard_map/ppermute | solution.py:233
  9.2 0.0 copy-done
  9.2 0.1 compare_convert_fusion.keep_ref
  9.3 2.9 %collective-permute-done.1.a_their_ref = bf16[1,192,256]{2,1,0:T(8,128)(2,1)S(1)} collective-permute-done((bf16[1,192,256]{2,1,0:T(8,128)(2,1)S(1)}, bf16[1,192,256]{2,1,0:T(8,128)(2,1)S(1)}, u32[]{:S(2)}, u32[]{:S(2)}) %collective-permute-start.1) | collective-permute-done | bytes 98336 | tf_op jit(solution)/shard_map/ppermute | solution.py:233
  12.2 1.6 %collective-permute-done.3.b_their_ref = bf16[1,192,256]{2,1,0:T(8,128)(2,1)S(1)} collective-permute-done((bf16[1,192,256]{2,1,0:T(8,128)(2,1)S(1)}, bf16[1,192,256]{2,1,0:T(8,128)(2,1)S(1)}, u32[]{:S(2)}, u32[]{:S(2)}) %collective-permute-start.3) | collective-permute-done | bytes 98336 | tf_op jit(solution)/shard_map/ppermute | solution.py:233
  13.8 0.1 power.1
  13.9 0.1 collective-permute-start.4
  14.0 13.4 %all_to_all.5.stats_ref = f32[32,2,256]{2,1,0:T(2,128)S(1)} all-to-all(f32[32,2,256]{2,1,0:T(2,128)S(1)} %get-tuple-element.18), channel_id=1, replica_groups=mesh['ma'=8,'freq'=4] {'ma','freq'}, dimensions={0} | all-to-all | bytes 131072 | tf_op jit(solution)/shard_map/all_to_all | solution.py:247
  27.3 0.0 collective-permute-done.4.other_ref
  27.4 2.8 %back.1 = (bf16[2,2,192,256]{3,2,1,0:T(8,128)(2,1)}, bf16[2,192,4,2,512]{4,3,2,1,0:T(2,128)(2,1)}) custom-call(f32[2,256]{1,0:T(2,128)S(1)} %compare_convert_fusion.keep_ref, f32[32,2,256]{2,1,0:T(2,128)S(1)} %all_to_all.5.stats_ref, f32[2,192,256]{2,1,0:T(8,128)S(1)} %get-tuple-element.19.mine_ref, f32[2,192,256]{2,1,0:T(8,128)S(1)} %collective-permute-done.4.other_ref, ...), custom_call_target="tpu_custom_call" | custom-call | tf_op jit(solution)/shard_map/back/pallas_call | solution.py:206
  (2 shorter events, 0.0 us)
Async XLA Ops:
  4.1 5.1 %copy-start = (s32[2]{0:T(128)S(1)}, s32[2]{0:T(128)}, u32[]{:S(2)}) copy-start(s32[2]{0:T(128)} %param.5) | copy-start | bytes 28
  4.1 1.5 %collective-permute-start = (bf16[1,192,256]{2,1,0:T(8,128)(2,1)S(1)}, bf16[1,192,256]{2,1,0:T(8,128)(2,1)S(1)}, u32[]{:S(2)}, u32[]{:S(2)}) collective-permute-start(bf16[1,192,256]{2,1,0:T(8,128)(2,1)S(1)} %get-tuple-element.12), channel_id=1, source_target_pairs={{0,1},{1,0},{2,3},{3,2},{4,5},{5,4},{6,7},{7,6},{8,9},{9,8},{10,11... | collective-permute-start | bytes 294920 | tf_op jit(solution)/shard_map/ppermute | solution.py:233
  5.1 3.5 %collective-permute-start.2 = (bf16[1,192,256]{2,1,0:T(8,128)(2,1)S(1)}, bf16[1,192,256]{2,1,0:T(8,128)(2,1)S(1)}, u32[]{:S(2)}, u32[]{:S(2)}) collective-permute-start(bf16[1,192,256]{2,1,0:T(8,128)(2,1)S(1)} %get-tuple-element.17), channel_id=1, source_target_pairs={{0,1},{1,0},{2,3},{3,2},{4,5},{5,4},{6,7},{7,6},{8,9},{9,8},{10,11... | collective-permute-start | bytes 294920 | tf_op jit(solution)/shard_map/ppermute | solution.py:233
  5.6 6.6 %collective-permute-start.1 = (bf16[1,192,256]{2,1,0:T(8,128)(2,1)S(1)}, bf16[1,192,256]{2,1,0:T(8,128)(2,1)S(1)}, u32[]{:S(2)}, u32[]{:S(2)}) collective-permute-start(bf16[1,192,256]{2,1,0:T(8,128)(2,1)S(1)} %add_convert_fusion.1.a_ref), channel_id=1, source_target_pairs={{0,2},{1,3},{2,0},{3,1},{4,6},{5,7},{6,4},{7,5},{8,10},{9,11},{10,... | collective-permute-start | bytes 294920 | tf_op jit(solution)/shard_map/ppermute | solution.py:233
  8.6 5.2 %collective-permute-start.3 = (bf16[1,192,256]{2,1,0:T(8,128)(2,1)S(1)}, bf16[1,192,256]{2,1,0:T(8,128)(2,1)S(1)}, u32[]{:S(2)}, u32[]{:S(2)}) collective-permute-start(bf16[1,192,256]{2,1,0:T(8,128)(2,1)S(1)} %add_convert_fusion.b_ref), channel_id=1, source_target_pairs={{0,2},{1,3},{2,0},{3,1},{4,6},{5,7},{6,4},{7,5},{8,10},{9,11},{10,... | collective-permute-start | bytes 294920 | tf_op jit(solution)/shard_map/ppermute | solution.py:233
  13.9 13.5 %collective-permute-start.4 = (f32[2,192,256]{2,1,0:T(8,128)S(1)}, f32[2,192,256]{2,1,0:T(8,128)S(1)}, u32[]{:S(2)}, u32[]{:S(2)}) collective-permute-start(f32[2,192,256]{2,1,0:T(8,128)S(1)} %get-tuple-element.19.mine_ref), channel_id=1, source_target_pairs={{0,1},{1,0},{2,3},{3,2},{4,5},{5,4},{6,7},{7,6},{8,9},{9,8},{10,11... | collective-permute-start | bytes 1179656 | tf_op jit(solution)/shard_map/ppermute | solution.py:233

commit v6 on v5

--- a/solution.py
+++ b/solution.py
@@ -7,6 +7,7 @@
 from jax.experimental.pallas import tpu as pltpu
 from jax.sharding import PartitionSpec as P
 
+
 F32 = jnp.float32
 BF16 = jnp.bfloat16
 VMEM = pl.BlockSpec(memory_space=pltpu.VMEM)
@@ -23,8 +24,8 @@
     return pl.CostEstimate(flops=flops, bytes_accessed=moved, transcendentals=0)
 
 
-def side():
-    return (lax.axis_index("freq") & 1).astype(jnp.int32)
+def side(bit=0):
+    return ((lax.axis_index("freq") >> bit) & 1).astype(jnp.int32)
 
 
 def times_i(x):
@@ -104,7 +105,7 @@
 
 
 def rest_kernel(part_ref, v_ref, e_ref, give_ref, keep_ref):
-    modes, freqs = e_ref.shape[:2]
+    _, freqs = e_ref.shape[:2]
     half, samples, _, base = v_ref.shape
     for j in range(half):
         x = v_ref[j].reshape(2 * samples, base)
@@ -130,43 +131,98 @@
     )(part, v, e)
 
 
-def power_kernel(keep_ref, a_ref, a_their_ref, b_ref, b_their_ref, total_ref, stats_ref):
-    half, _, kmax = a_ref.shape
+def split_kernel(mine_ref, theirs_ref, give_ref, keep_ref):
+    half, rows, _ = give_ref.shape
+    for j in range(half):
+        total = mine_ref[j] + theirs_ref[j].astype(F32)
+        low, high = total[:rows], total[rows:]
+        give_ref[j] = jnp.where(side(1) == 0, high, low).astype(give_ref.dtype)
+        keep_ref[j] = jnp.where(side(1) == 0, low, high)
+
+
+def split(mine, theirs):
+    half, rows, kmax = mine.shape
+    return pl.pallas_call(
+        split_kernel,
+        in_specs=[VMEM] * 2,
+        out_specs=[VMEM] * 2,
+        out_shape=[
+            jax.ShapeDtypeStruct((half, rows // 2, kmax), BF16),
+            jax.ShapeDtypeStruct((half, rows // 2, kmax), F32),
+        ],
+        name="split",
+        compiler_params=limit(MIB * 2),
+    )(mine, theirs)
+
+
+def power_kernel(freq_size, keep_ref, quarter_ref, b_ref, b_their_ref, total_ref, stats_ref):
+    half, _, kmax = b_ref.shape
     stats = jnp.zeros((2, kmax), F32)
     for m in range(2 * half):
-        mine, theirs = (a_ref, a_their_ref) if m < half else (b_ref, b_their_ref)
-        total = mine[m % half].astype(F32) + theirs[m % half].astype(F32)
-        total_ref[m] = total
+        if m < half:
+            total, copies = quarter_ref[m].astype(F32), freq_size // 4
+        else:
+            total, copies = b_ref[m - half].astype(F32) + b_their_ref[m - half].astype(F32), freq_size // 2
+            total_ref[m - half] = total
         keep = keep_ref[m : m + 1]
-        power = keep * jnp.sum(total * total, axis=0, keepdims=True)
-        stats += jnp.concatenate([power, keep], axis=0)
+        power = keep * jnp.sum(total * total, axis=0, keepdims=True) * F32(1.0 / copies)
+        stats += jnp.concatenate([power, keep * F32(1.0 / freq_size)], axis=0)
     stats_ref[...] = jnp.broadcast_to(stats[None], stats_ref.shape)
 
 
-def power_of(keep, pairs, peers):
-    half, rows, kmax = pairs[0].shape
-    return pl.pallas_call(
-        power_kernel,
-        in_specs=[VMEM] * 5,
+def power_of(keep, freq_size, quarter, mine, theirs, peers):
+    kmax = mine.shape[-1]
+    return pl.pallas_call(
+        functools.partial(power_kernel, freq_size),
+        in_specs=[VMEM] * 4,
         out_specs=[VMEM] * 2,
         out_shape=[
-            jax.ShapeDtypeStruct((2 * half, rows, kmax), F32),
+            jax.ShapeDtypeStruct(mine.shape, F32),
             jax.ShapeDtypeStruct((peers, 2, kmax), F32),
         ],
         name="power",
         compiler_params=limit(MIB * 4),
-    )(keep, *pairs)
+    )(keep, quarter, mine, theirs)
+
+
+def pool_kernel(samples, stats_ref, scale_ref):
+    stats = jnp.sum(stats_ref[...], axis=0)
+    power, count = stats[0:1], F32(samples) * stats[1:2]
+    scale_ref[...] = 1.0 / jnp.sqrt(power / jnp.maximum(count, 1.0) + 1e-06)
+
+
+def pool(stats, samples):
+    return pl.pallas_call(
+        functools.partial(pool_kernel, samples),
+        in_specs=[VMEM],
+        out_specs=VMEM,
+        out_shape=jax.ShapeDtypeStruct((1, stats.shape[-1]), F32),
+        name="pool",
+        compiler_params=limit(MIB),
+    )(stats)
+
+
+def pieces(m, c, y, quarters, mine_ref, other_ref):
+    half = mine_ref.shape[0]
+    if m < half:
+        own, core, chip, both = [q[m].astype(F32) for q in quarters]
+        rows = own.shape[0]
+        for c_of in range(2):
+            near, far = jnp.where(c == c_of, own, core), jnp.where(c == c_of, chip, both)
+            for y_of in range(2):
+                yield (2 * c_of + y_of) * rows, jnp.where(y == y_of, near, far)
+    else:
+        mine, other = mine_ref[m - half], other_ref[m - half]
+        for c_of in range(2):
+            yield c_of * mine.shape[0], jnp.where(c == c_of, mine, other)
 
 
 def back_kernel(
-    freq_size, keep_ref, stats_ref, mine_ref, other_ref, e_ref, coef_hbm, out_hbm, pair, flat, coef_buf, out_buf, coef_sem, out_sem
+    keep_ref, scale_ref, q0_ref, q1_ref, q2_ref, q3_ref, mine_ref, other_ref, e_ref, coef_hbm, out_hbm, pair, flat, coef_buf, out_buf, coef_sem, out_sem
 ):
     modes, freqs, samples, _, base = out_buf.shape
     kmax = mine_ref.shape[-1]
     lanes = flat.shape[2]
-    stats = jnp.sum(stats_ref[...], axis=0)
-    power, count = stats[0:1] * F32(2 / freq_size), F32(samples) * (stats[1:2] * F32(1 / freq_size))
-    scale = 1.0 / jnp.sqrt(power / jnp.maximum(count, 1.0) + 1e-06)
     contract = (((1,), (1,)), ((), ()))
     pending = []
 
@@ -176,11 +232,10 @@
         pending.append(copy)
 
     for m in range(modes):
-        gain = keep_ref[m : m + 1] * scale
-        mine, other = mine_ref[m] * gain, other_ref[m] * gain
-        for h in range(2):
-            coef = jnp.where(side() == h, mine, other)
-            at = slice(h * samples, (h + 1) * samples)
+        gain = keep_ref[m : m + 1] * scale_ref[...]
+        for start, proj in pieces(m, side(), side(1), (q0_ref, q1_ref, q2_ref, q3_ref), mine_ref, other_ref):
+            coef = proj * gain
+            at = slice(start, start + coef.shape[0])
             pair[at, :kmax] = coef.astype(BF16)
             pair[at, kmax:] = times_i(coef).astype(BF16)
             for i in range(kmax // lanes):
@@ -200,12 +255,12 @@
         copy.wait()
 
 
-def back(keep, freq_size, stats, mine, other, e):
+def back(keep, scale, quarters, mine, other, e):
     modes, freqs, _, base, kmax = e.shape
     samples = mine.shape[1]
     return pl.pallas_call(
-        functools.partial(back_kernel, freq_size),
-        in_specs=[VMEM] * 5,
+        back_kernel,
+        in_specs=[VMEM] * 9,
         out_specs=[HBM, HBM],
         out_shape=[
             jax.ShapeDtypeStruct((modes, 2, samples, kmax), BF16),
@@ -221,10 +276,10 @@
         ],
         name="back",
         compiler_params=limit(MIB * 16),
-    )(keep, stats, mine, other, e)
-
-
-def per_device(visibilities, eigenmodes, retained):
+    )(keep, scale, *quarters, mine, other, e)
+
+
+def filter_modes(visibilities, eigenmodes, retained):
     freq_size, ma_size = lax.axis_size("freq"), lax.axis_size("ma")
     ranks = jnp.arange(eigenmodes.shape[-1], dtype=jnp.int32)
     keep = (ranks[None, :] < retained[:, None]).astype(F32)
@@ -232,25 +287,35 @@
     def swap(x, bit):
         return lax.ppermute(x, "freq", [(i, i ^ bit) for i in range(freq_size)])
 
-    give_a, keep_a, part, v_last, e_vmem = project(visibilities, eigenmodes)
-    give_b, keep_b = rest(part, v_last, e_vmem)
-    pairs = []
-    for give, kept in ((give_a, keep_a), (give_b, keep_b)):
-        total = (kept + swap(give, 1).astype(F32)).astype(BF16)
+    def over_chips(total):
         bit = 2
         while 2 * bit < freq_size:
             total = (total.astype(F32) + swap(total, bit).astype(F32)).astype(BF16)
             bit *= 2
-        pairs += [total, swap(total, bit)]
-    mine, stats = power_of(keep, pairs, ma_size * freq_size)
+        return total, swap(total, bit)
+
+    give_a, keep_a, part, v_last, e_vmem = project(visibilities, eigenmodes)
+    give_b, keep_b = rest(part, v_last, e_vmem)
+    give_a, keep_a = split(keep_a, swap(give_a, 1))
+    quarter = keep_a + swap(give_a, 2).astype(F32)
+    bit = 4
+    while bit < freq_size:
+        quarter = quarter + swap(quarter.astype(BF16), bit).astype(F32)
+        bit *= 2
+    quarter = quarter.astype(BF16)
+    total, theirs = over_chips((keep_b + swap(give_b, 1).astype(F32)).astype(BF16))
+    quarters = [quarter]
+    for bits in (1, 2, 3):
+        quarters.append(swap(quarter, bits))
+    mine, stats = power_of(keep, freq_size, quarter, total, theirs, ma_size * freq_size)
     other = swap(mine, 1)
-    stats = lax.all_to_all(stats, ("ma", "freq"), 0, 0, tiled=True)
-    return tuple(back(keep, freq_size, stats, mine, other, e_vmem))
+    scale = pool(lax.all_to_all(stats, ("ma", "freq"), 0, 0, tiled=True), visibilities.shape[1])
+    return tuple(back(keep, scale, quarters, mine, other, e_vmem))
 
 
 def solution(mesh):
     return jax.shard_map(
-        per_device,
+        filter_modes,
         mesh=mesh,
         in_specs=(P("ma", None, "freq", None, None), P("ma", "freq", None, None, None), P("ma")),
         out_specs=(P("ma", None, None, None), P("ma", None, "freq", None, None)),

time: 30.4 us -> 34.3 us (1.13)
  blocking collectives: 13.4 us -> 0 us
  starting transfers between devices: 4.26 us -> 12.3 us
  waiting for transfers between devices: 4.94 us -> 9.31 us
  local copies, waits for them, and re-layouts: 0.01 us -> 4.15 us
  Pallas kernels: 6.83 us -> 7.44 us
    all_to_all x1 -> x0, blocking collectives: 13.4 us -> none  [per_device(): stats = lax.all_to_all(stats, ('ma', 'freq'), 0, 0, tiled=True)]
    all_to_all x0 -> x1, starting transfers between devices: none -> 5.93 us  [filter_modes(): lax.all_to_all(stats, ('ma', 'freq'), 0, 0, tiled=True)]
    all_to_all x0 -> x1, waiting for transfers between devices: none -> 5.46 us  [filter_modes(): lax.all_to_all(stats, ('ma', 'freq'), 0, 0, tiled=True)]
    unnamed x2 -> x6, local copies, waits for them, and re-layouts: 0.01 us -> 4.15 us
    ppermute x5 -> x8, starting transfers between devices: 4.26 us -> 6.42 us  [swap(): return lax.ppermute(x, 'freq', [(i, i ^ bit) for i in range(freq_size)])]
    ppermute x5 -> x8, waiting for transfers between devices: 4.94 us -> 3.85 us  [swap(): return lax.ppermute(x, 'freq', [(i, i ^ bit) for i in range(freq_size)])]
    pallas_call x2 -> x4, Pallas kernels: 2.94 us -> 3.58 us  [the longest x1 2.78 us: back(): pl.pallas_call(back_kernel, in_specs=[VMEM] * 9, out_specs=[HBM, HBM], ou...]
  transfers between devices with their start and end apart: 5 -> 9, of which waited for: 3 -> 3; matrix products, arithmetic and copies ran while one was open for 0% -> 0% of each run, Pallas kernels for 1% -> 1%
where the time goes in v6:
time: 34.3 us; the launch traced here: 34.1 us
  starting transfers between devices  12.3 us (36%)
  waiting for transfers between devices  9.31 us (27%)
  Pallas kernels  7.44 us (22%)
  local copies, waits for them, and re-layouts  4.15 us (12%)
  between operations  0.73 us (2%)
    ppermute x8, starting transfers between devices, swap(): return lax.ppermute(x, 'freq', [(i, i ^ bit) for i in range(freq_size)])  6.42 us
    all_to_all x1, starting transfers between devices, filter_modes(): lax.all_to_all(stats, ('ma', 'freq'), 0, 0, tiled=True)  5.93 us
    all_to_all x1, waiting for transfers between devices, filter_modes(): lax.all_to_all(stats, ('ma', 'freq'), 0, 0, tiled=True)  5.46 us
    unnamed x6, local copies, waits for them, and re-layouts  4.15 us
    ppermute x8, waiting for transfers between devices, swap(): return lax.ppermute(x, 'freq', [(i, i ^ bit) for i in range(freq_size)])  3.85 us
    pallas_call x1, Pallas kernels, project(): pl.pallas_call(project_kernel, in_specs=[HBM, HBM], out_specs=[VMEM] * 5,...  3.45 us
    pallas_call x1, Pallas kernels, back(): pl.pallas_call(back_kernel, in_specs=[VMEM] * 9, out_specs=[HBM, HBM], ou...  2.78 us
    pallas_call x1, Pallas kernels, power_of(): pl.pallas_call(functools.partial(power_kernel, freq_size), in_specs=[VMEM...  0.71 us
  transfers between devices with their start and end apart: 9, of which 3 were waited for; matrix products, arithmetic and copies ran while one was open for 0% of the time, Pallas kernels for 1%

profile of v6, /device:TPU:0, one launch (start us, length us, event | category | flops | bytes accessed | tf_op | source)
XLA Modules:
  0.0 34.1 jit_solution(6716425124296553066)
XLA Ops:
  0.6 3.4 %project.1 = (bf16[1,192,256]{2,1,0:T(8,128)(2,1)S(1)}, f32[1,192,256]{2,1,0:T(8,128)S(1)}, f32[1,2,384,256]{3,2,1,0:T(8,128)S(1)}, bf16[1,192,2,512]{3,2,1,0:T(2,128)(2,1)S(1)}, bf16[2,4,2,512,256]{4,3,2,1,0:T(8,128)(2,1)S(1)}) custom-call(bf16[2,192,4,2,512]{4,3,2,1,0:T(2,128)(2,1)} %v_hbm.1, bf16[2,4,2,512,256]{4,3,2,1,0:T(8,128)(2,1)} %e_hbm.1), custom_call_target="tpu_custom_call" | custom-call | flops 1610612736 | bytes 7340032 | tf_op jit(solution)/shard_map/project/pallas_call | solution.py:84
  4.1 0.0 copy-start.2
  4.1 0.6 %collective-permute-start = (bf16[1,192,256]{2,1,0:T(8,128)(2,1)S(1)}, bf16[1,192,256]{2,1,0:T(8,128)(2,1)S(1)}, u32[]{:S(2)}, u32[]{:S(2)}) collective-permute-start(bf16[1,192,256]{2,1,0:T(8,128)(2,1)S(1)} %get-tuple-element.14), channel_id=1, source_target_pairs={{0,1},{1,0},{2,3},{3,2},{4,5},{5,4},{6,7},{7,6},{8,9},{9,8},{10,11... | collective-permute-start | bytes 294920 | tf_op jit(solution)/shard_map/ppermute | solution.py:288
  4.7 0.4 %rest.1 = (bf16[1,192,256]{2,1,0:T(8,128)(2,1)S(1)}, f32[1,192,256]{2,1,0:T(8,128)S(1)}) custom-call(f32[1,2,384,256]{3,2,1,0:T(8,128)S(1)} %get-tuple-element.17.part_ref, bf16[1,192,2,512]{3,2,1,0:T(2,128)(2,1)S(1)} %get-tuple-element.18.v_ref, bf16[2,4,2,512,256]{4,3,2,1,0:T(8,128)(2,1)S(1)} %get-tuple-element.19.e_ref), custom_call_target="tpu_custom_call" | custom-call | flops 201326592 | bytes 393216 | tf_op jit(solution)/shard_map/rest/pallas_call | solution.py:120
  5.1 0.0 copy-start
  5.1 2.0 %copy-done = bf16[2,4,2,512,256]{4,3,2,1,0:T(8,128)(2,1)} copy-done((bf16[2,4,2,512,256]{4,3,2,1,0:T(8,128)(2,1)}, bf16[2,4,2,512,256]{4,3,2,1,0:T(8,128)(2,1)S(1)}, u32[]{:S(2)}) %copy-start) | copy-done | bytes 4194328
  7.0 0.0 collective-permute-start.2
  7.1 0.0 copy-done.2
  7.1 0.1 compare_convert_fusion.keep_ref
  7.1 0.0 collective-permute-done.theirs_ref
  7.2 3.1 %collective-permute-start.1 = (bf16[1,96,256]{2,1,0:T(8,128)(2,1)S(1)}, bf16[1,96,256]{2,1,0:T(8,128)(2,1)S(1)}, u32[]{:S(2)}, u32[]{:S(2)}) collective-permute-start(bf16[1,96,256]{2,1,0:T(8,128)(2,1)S(1)} %get-tuple-element.16), channel_id=1, source_target_pairs={{0,2},{1,3},{2,0},{3,1},{4,6},{5,7},{6,4},{7,5},{8,10},{9,11},{10,... | collective-permute-start | bytes 147464 | tf_op jit(solution)/shard_map/ppermute | solution.py:288
  10.2 0.0 collective-permute-done.2
  10.3 0.8 %collective-permute-start.3 = (bf16[1,192,256]{2,1,0:T(8,128)(2,1)S(1)}, bf16[1,192,256]{2,1,0:T(8,128)(2,1)S(1)}, u32[]{:S(2)}, u32[]{:S(2)}) collective-permute-start(bf16[1,192,256]{2,1,0:T(8,128)(2,1)S(1)} %add_convert_fusion.b_ref), channel_id=1, source_target_pairs={{0,2},{1,3},{2,0},{3,1},{4,6},{5,7},{6,4},{7,5},{8,10},{9,11},{10,... | collective-permute-start | bytes 294920 | tf_op jit(solution)/shard_map/ppermute | solution.py:288
  11.1 1.2 %collective-permute-done.1 = bf16[1,96,256]{2,1,0:T(8,128)(2,1)S(1)} collective-permute-done((bf16[1,96,256]{2,1,0:T(8,128)(2,1)S(1)}, bf16[1,96,256]{2,1,0:T(8,128)(2,1)S(1)}, u32[]{:S(2)}, u32[]{:S(2)}) %collective-permute-start.1) | collective-permute-done | bytes 49184 | tf_op jit(solution)/shard_map/ppermute | solution.py:288
  12.3 2.6 %collective-permute-done.3.b_their_ref = bf16[1,192,256]{2,1,0:T(8,128)(2,1)S(1)} collective-permute-done((bf16[1,192,256]{2,1,0:T(8,128)(2,1)S(1)}, bf16[1,192,256]{2,1,0:T(8,128)(2,1)S(1)}, u32[]{:S(2)}, u32[]{:S(2)}) %collective-permute-start.3) | collective-permute-done | bytes 98336 | tf_op jit(solution)/shard_map/ppermute | solution.py:288
  15.0 0.7 %power.1 = (f32[1,192,256]{2,1,0:T(8,128)S(1)}, f32[32,2,256]{2,1,0:T(2,128)}) custom-call(f32[2,256]{1,0:T(2,128)S(1)} %compare_convert_fusion.keep_ref, bf16[1,96,256]{2,1,0:T(8,128)(2,1)S(1)} %add_convert_fusion.1.quarter_ref.q0_ref, bf16[1,192,256]{2,1,0:T(8,128)(2,1)S(1)} %add_convert_fusion.b_ref, ...), custom_call_target="tpu_custom_call" | custom-call | tf_op jit(solution)/shard_map/power/pallas_call | solution.py:175
  15.7 0.0 collective-permute-start.7
  15.7 5.9 %all-to-all-start = ((f32[32,2,256]{2,1,0:T(2,128)}), f32[32,2,256]{2,1,0:T(2,128)S(1)}, u32[]{:S(2)}, u32[]{:S(2)}) async-start(f32[32,2,256]{2,1,0:T(2,128)} %get-tuple-element.22), calls=%async_computation | async-start | bytes 131072 | tf_op jit(solution)/shard_map/all_to_all | solution.py:312
  21.6 1.6 %collective-permute-start.6 = (bf16[1,96,256]{2,1,0:T(8,128)(2,1)S(1)}, bf16[1,96,256]{2,1,0:T(8,128)(2,1)S(1)}, u32[]{:S(2)}, u32[]{:S(2)}) collective-permute-start(bf16[1,96,256]{2,1,0:T(8,128)(2,1)S(1)} %add_convert_fusion.1.quarter_ref.q0_ref), channel_id=1, source_target_pairs={{0,3},{1,2},{2,1},{3,0},{4,7},{5,6},{6,5},{7,4},{8,11},{9,10},{10,... | collective-permute-start | bytes 147464 | tf_op jit(solution)/shard_map/ppermute | solution.py:288
  23.2 0.4 %collective-permute-start.5 = (bf16[1,96,256]{2,1,0:T(8,128)(2,1)S(1)}, bf16[1,96,256]{2,1,0:T(8,128)(2,1)S(1)}, u32[]{:S(2)}, u32[]{:S(2)}) collective-permute-start(bf16[1,96,256]{2,1,0:T(8,128)(2,1)S(1)} %add_convert_fusion.1.quarter_ref.q0_ref), channel_id=1, source_target_pairs={{0,2},{1,3},{2,0},{3,1},{4,6},{5,7},{6,4},{7,5},{8,10},{9,11},{10,... | collective-permute-start | bytes 147464 | tf_op jit(solution)/shard_map/ppermute | solution.py:288
  23.6 0.0 collective-permute-start.4
  23.6 5.5 %all-to-all-done.stats_ref = f32[32,2,256]{2,1,0:T(2,128)S(1)} async-done(((f32[32,2,256]{2,1,0:T(2,128)}), f32[32,2,256]{2,1,0:T(2,128)S(1)}, u32[]{:S(2)}, u32[]{:S(2)}) %all-to-all-start) | async-done | bytes 65568 | tf_op jit(solution)/shard_map/all_to_all | solution.py:312
  29.0 0.1 pool.1.scale_ref
  29.1 0.0 collective-permute-done.6.q3_ref
  29.1 0.0 collective-permute-done.5.q2_ref
  29.1 0.0 collective-permute-done.4.q1_ref
  29.1 0.0 collective-permute-done.7.other_ref
  29.1 0.0 copy-start.1
  29.1 2.2 %copy-done.1 = bf16[2,4,2,512,256]{4,3,2,1,0:T(8,128)(2,1)S(1)} copy-done((bf16[2,4,2,512,256]{4,3,2,1,0:T(8,128)(2,1)S(1)}, bf16[2,4,2,512,256]{4,3,2,1,0:T(8,128)(2,1)}, u32[]{:S(2)}) %copy-start.1) | copy-done | bytes 4194328
  31.3 2.8 %back.1 = (bf16[2,2,192,256]{3,2,1,0:T(8,128)(2,1)}, bf16[2,192,4,2,512]{4,3,2,1,0:T(2,128)(2,1)}) custom-call(f32[2,256]{1,0:T(2,128)S(1)} %compare_convert_fusion.keep_ref, f32[1,256]{1,0:T(1,128)S(1)} %pool.1.scale_ref, bf16[1,96,256]{2,1,0:T(8,128)(2,1)S(1)} %add_convert_fusion.1.quarter_ref.q0_ref, ...), custom_call_target="tpu_custom_call" | custom-call | tf_op jit(solution)/shard_map/back/pallas_call | solution.py:261
  (3 shorter events, 0.1 us)
Async XLA Ops:
  4.1 3.0 %copy-start.2 = (s32[2]{0:T(128)S(1)}, s32[2]{0:T(128)}, u32[]{:S(2)}) copy-start(s32[2]{0:T(128)} %param.5) | copy-start | bytes 28
  4.1 3.0 %collective-permute-start = (bf16[1,192,256]{2,1,0:T(8,128)(2,1)S(1)}, bf16[1,192,256]{2,1,0:T(8,128)(2,1)S(1)}, u32[]{:S(2)}, u32[]{:S(2)}) collective-permute-start(bf16[1,192,256]{2,1,0:T(8,128)(2,1)S(1)} %get-tuple-element.14), channel_id=1, source_target_pairs={{0,1},{1,0},{2,3},{3,2},{4,5},{5,4},{6,7},{7,6},{8,9},{9,8},{10,11... | collective-permute-start | bytes 294920 | tf_op jit(solution)/shard_map/ppermute | solution.py:288
  5.1 2.0 %copy-start = (bf16[2,4,2,512,256]{4,3,2,1,0:T(8,128)(2,1)}, bf16[2,4,2,512,256]{4,3,2,1,0:T(8,128)(2,1)S(1)}, u32[]{:S(2)}) copy-start(bf16[2,4,2,512,256]{4,3,2,1,0:T(8,128)(2,1)S(1)} %get-tuple-element.19.e_ref) | copy-start | bytes 12582916
  7.0 3.2 %collective-permute-start.2 = (bf16[1,192,256]{2,1,0:T(8,128)(2,1)S(1)}, bf16[1,192,256]{2,1,0:T(8,128)(2,1)S(1)}, u32[]{:S(2)}, u32[]{:S(2)}) collective-permute-start(bf16[1,192,256]{2,1,0:T(8,128)(2,1)S(1)} %get-tuple-element.21), channel_id=1, source_target_pairs={{0,1},{1,0},{2,3},{3,2},{4,5},{5,4},{6,7},{7,6},{8,9},{9,8},{10,11... | collective-permute-start | bytes 294920 | tf_op jit(solution)/shard_map/ppermute | solution.py:288
  7.2 5.1 %collective-permute-start.1 = (bf16[1,96,256]{2,1,0:T(8,128)(2,1)S(1)}, bf16[1,96,256]{2,1,0:T(8,128)(2,1)S(1)}, u32[]{:S(2)}, u32[]{:S(2)}) collective-permute-start(bf16[1,96,256]{2,1,0:T(8,128)(2,1)S(1)} %get-tuple-element.16), channel_id=1, source_target_pairs={{0,2},{1,3},{2,0},{3,1},{4,6},{5,7},{6,4},{7,5},{8,10},{9,11},{10,... | collective-permute-start | bytes 147464 | tf_op jit(solution)/shard_map/ppermute | solution.py:288
  10.3 4.7 %collective-permute-start.3 = (bf16[1,192,256]{2,1,0:T(8,128)(2,1)S(1)}, bf16[1,192,256]{2,1,0:T(8,128)(2,1)S(1)}, u32[]{:S(2)}, u32[]{:S(2)}) collective-permute-start(bf16[1,192,256]{2,1,0:T(8,128)(2,1)S(1)} %add_convert_fusion.b_ref), channel_id=1, source_target_pairs={{0,2},{1,3},{2,0},{3,1},{4,6},{5,7},{6,4},{7,5},{8,10},{9,11},{10,... | collective-permute-start | bytes 294920 | tf_op jit(solution)/shard_map/ppermute | solution.py:288
  15.7 13.4 %collective-permute-start.7 = (f32[1,192,256]{2,1,0:T(8,128)S(1)}, f32[1,192,256]{2,1,0:T(8,128)S(1)}, u32[]{:S(2)}, u32[]{:S(2)}) collective-permute-start(f32[1,192,256]{2,1,0:T(8,128)S(1)} %get-tuple-element.23.mine_ref), channel_id=1, source_target_pairs={{0,1},{1,0},{2,3},{3,2},{4,5},{5,4},{6,7},{7,6},{8,9},{9,8},{10,11... | collective-permute-start | bytes 589832 | tf_op jit(solution)/shard_map/ppermute | solution.py:288
  15.7 13.3 %all-to-all-start = ((f32[32,2,256]{2,1,0:T(2,128)}), f32[32,2,256]{2,1,0:T(2,128)S(1)}, u32[]{:S(2)}, u32[]{:S(2)}) async-start(f32[32,2,256]{2,1,0:T(2,128)} %get-tuple-element.22), calls=%async_computation | async-start | bytes 131072 | tf_op jit(solution)/shard_map/all_to_all | solution.py:312
  21.6 7.5 %collective-permute-start.6 = (bf16[1,96,256]{2,1,0:T(8,128)(2,1)S(1)}, bf16[1,96,256]{2,1,0:T(8,128)(2,1)S(1)}, u32[]{:S(2)}, u32[]{:S(2)}) collective-permute-start(bf16[1,96,256]{2,1,0:T(8,128)(2,1)S(1)} %add_convert_fusion.1.quarter_ref.q0_ref), channel_id=1, source_target_pairs={{0,3},{1,2},{2,1},{3,0},{4,7},{5,6},{6,5},{7,4},{8,11},{9,10},{10,... | collective-permute-start | bytes 147464 | tf_op jit(solution)/shard_map/ppermute | solution.py:288
  23.2 5.9 %collective-permute-start.5 = (bf16[1,96,256]{2,1,0:T(8,128)(2,1)S(1)}, bf16[1,96,256]{2,1,0:T(8,128)(2,1)S(1)}, u32[]{:S(2)}, u32[]{:S(2)}) collective-permute-start(bf16[1,96,256]{2,1,0:T(8,128)(2,1)S(1)} %add_convert_fusion.1.quarter_ref.q0_ref), channel_id=1, source_target_pairs={{0,2},{1,3},{2,0},{3,1},{4,6},{5,7},{6,4},{7,5},{8,10},{9,11},{10,... | collective-permute-start | bytes 147464 | tf_op jit(solution)/shard_map/ppermute | solution.py:288
  23.6 5.5 %collective-permute-start.4 = (bf16[1,96,256]{2,1,0:T(8,128)(2,1)S(1)}, bf16[1,96,256]{2,1,0:T(8,128)(2,1)S(1)}, u32[]{:S(2)}, u32[]{:S(2)}) collective-permute-start(bf16[1,96,256]{2,1,0:T(8,128)(2,1)S(1)} %add_convert_fusion.1.quarter_ref.q0_ref), channel_id=1, source_target_pairs={{0,1},{1,0},{2,3},{3,2},{4,5},{5,4},{6,7},{7,6},{8,9},{9,8},{10,11... | collective-permute-start | bytes 147464 | tf_op jit(solution)/shard_map/ppermute | solution.py:288
  29.1 2.2 %copy-start.1 = (bf16[2,4,2,512,256]{4,3,2,1,0:T(8,128)(2,1)S(1)}, bf16[2,4,2,512,256]{4,3,2,1,0:T(8,128)(2,1)}, u32[]{:S(2)}) copy-start(bf16[2,4,2,512,256]{4,3,2,1,0:T(8,128)(2,1)} %copy-done) | copy-start | bytes 12582916

commit v7 on v5

--- a/solution.py
+++ b/solution.py
@@ -36,10 +36,8 @@
 
 def finish(j, by_re, by_im, give_ref, keep_ref):
     out = by_re - times_i(by_im)
-    half = out.shape[0] // 2
-    low, high = out[:half], out[half:]
-    give_ref[j] = jnp.where(side() == 0, high, low).astype(give_ref.dtype)
-    keep_ref[j] = jnp.where(side() == 0, low, high).astype(keep_ref.dtype)
+    give_ref[j] = out.astype(give_ref.dtype)
+    keep_ref[j] = out.astype(keep_ref.dtype)
 
 
 def project_kernel(v_hbm, e_hbm, give_ref, keep_ref, part_ref, v_last, e_ref, v_buf, acc, v_sem, e_sem):
@@ -85,8 +83,8 @@
         in_specs=[HBM, HBM],
         out_specs=[VMEM] * 5,
         out_shape=[
-            jax.ShapeDtypeStruct((half, samples, kmax), BF16),
-            jax.ShapeDtypeStruct((half, samples, kmax), F32),
+            jax.ShapeDtypeStruct((half, 2 * samples, kmax), BF16),
+            jax.ShapeDtypeStruct((half, 2 * samples, kmax), F32),
             jax.ShapeDtypeStruct((half, 2, 2 * samples, kmax), F32),
             jax.ShapeDtypeStruct((half, samples, 2, base), v.dtype),
             jax.ShapeDtypeStruct(e.shape, e.dtype),
@@ -121,8 +119,8 @@
         in_specs=[VMEM] * 3,
         out_specs=[VMEM] * 2,
         out_shape=[
-            jax.ShapeDtypeStruct((half, samples, kmax), BF16),
-            jax.ShapeDtypeStruct((half, samples, kmax), F32),
+            jax.ShapeDtypeStruct((half, 2 * samples, kmax), BF16),
+            jax.ShapeDtypeStruct((half, 2 * samples, kmax), F32),
         ],
         name="rest",
         compiler_params=limit(MIB * 4),
@@ -139,7 +137,7 @@
         total_ref[m] = total
         keep = keep_ref[m : m + 1]
         power = keep * jnp.sum(total * total, axis=0, keepdims=True)
-        stats += jnp.concatenate([power, keep], axis=0)
+        stats += jnp.where(side() == 1, jnp.concatenate([power, keep], axis=0), 0.0)
     stats_ref[...] = jnp.broadcast_to(stats[None], stats_ref.shape)
 
 
@@ -165,7 +163,7 @@
     kmax = mine_ref.shape[-1]
     lanes = flat.shape[2]
     stats = jnp.sum(stats_ref[...], axis=0)
-    power, count = stats[0:1] * F32(2 / freq_size), F32(samples) * (stats[1:2] * F32(1 / freq_size))
+    power, count = stats[0:1] * F32(2 / freq_size), F32(samples) * (stats[1:2] * F32(2 / freq_size))
     scale = 1.0 / jnp.sqrt(power / jnp.maximum(count, 1.0) + 1e-06)
     contract = (((1,), (1,)), ((), ()))
     pending = []
@@ -177,14 +175,11 @@
 
     for m in range(modes):
         gain = keep_ref[m : m + 1] * scale
-        mine, other = mine_ref[m] * gain, other_ref[m] * gain
-        for h in range(2):
-            coef = jnp.where(side() == h, mine, other)
-            at = slice(h * samples, (h + 1) * samples)
-            pair[at, :kmax] = coef.astype(BF16)
-            pair[at, kmax:] = times_i(coef).astype(BF16)
-            for i in range(kmax // lanes):
-                flat[i, at, :] = coef[:, i * lanes : (i + 1) * lanes]
+        coef = jnp.where(side() == 1, mine_ref[m], other_ref[m]) * gain
+        pair[:, :kmax] = coef.astype(BF16)
+        pair[:, kmax:] = times_i(coef).astype(BF16)
+        for i in range(kmax // lanes):
+            flat[i] = coef[:, i * lanes : (i + 1) * lanes]
         for f in range(freqs):
             out = lax.dot_general(pair[:, :kmax], e_ref[m, f, 0], contract, preferred_element_type=F32)
             out += lax.dot_general(pair[:, kmax:], e_ref[m, f, 1], contract, preferred_element_type=F32)
@@ -202,7 +197,7 @@
 
 def back(keep, freq_size, stats, mine, other, e):
     modes, freqs, _, base, kmax = e.shape
-    samples = mine.shape[1]
+    samples = mine.shape[1] // 2
     return pl.pallas_call(
         functools.partial(back_kernel, freq_size),
         in_specs=[VMEM] * 5,
@@ -229,21 +224,29 @@
     ranks = jnp.arange(eigenmodes.shape[-1], dtype=jnp.int32)
     keep = (ranks[None, :] < retained[:, None]).astype(F32)
 
+    summing = range(1, freq_size, 2)
+
+    def collect(x):
+        return lax.ppermute(x, "freq", [(i - 1, i) for i in summing])
+
+    def hand_back(x):
+        return lax.ppermute(x, "freq", [(i, i - 1) for i in summing])
+
     def swap(x, bit):
-        return lax.ppermute(x, "freq", [(i, i ^ bit) for i in range(freq_size)])
+        return lax.ppermute(x, "freq", [(i, i ^ bit) for i in summing])
 
     give_a, keep_a, part, v_last, e_vmem = project(visibilities, eigenmodes)
     give_b, keep_b = rest(part, v_last, e_vmem)
     pairs = []
     for give, kept in ((give_a, keep_a), (give_b, keep_b)):
-        total = (kept + swap(give, 1).astype(F32)).astype(BF16)
+        total = (kept + collect(give).astype(F32)).astype(BF16)
         bit = 2
         while 2 * bit < freq_size:
             total = (total.astype(F32) + swap(total, bit).astype(F32)).astype(BF16)
             bit *= 2
         pairs += [total, swap(total, bit)]
     mine, stats = power_of(keep, pairs, ma_size * freq_size)
-    other = swap(mine, 1)
+    other = hand_back(mine)
     stats = lax.all_to_all(stats, ("ma", "freq"), 0, 0, tiled=True)
     return tuple(back(keep, freq_size, stats, mine, other, e_vmem))
 

time: 30.4 us -> 34.7 us (1.14)
  blocking collectives: 13.4 us -> 20.1 us
  waiting for transfers between devices: 4.94 us -> 0.31 us
  starting transfers between devices: 4.26 us -> 6.34 us
    all_to_all x1, blocking collectives: 13.4 us -> 20.1 us  [per_device(): stats = lax.all_to_all(stats, ('ma', 'freq'), 0, 0, tiled=True)]
    ppermute x5, waiting for transfers between devices: 4.94 us -> 0.31 us  [the longest x2 0.3 us: collect(): return lax.ppermute(x, 'freq', [(i - 1, i) for i in summing])]
    ppermute x5, starting transfers between devices: 4.26 us -> 6.34 us  [the longest x2 3.7 us: collect(): return lax.ppermute(x, 'freq', [(i - 1, i) for i in summing])]
  transfers between devices with their start and end apart: 5 -> 5, of which waited for: 3 -> 1; matrix products, arithmetic and copies ran while one was open for 0% -> 0% of each run, Pallas kernels for 1% -> 1%
where the time goes in v7:
time: 34.7 us; the launch traced here: 34.5 us
  blocking collectives  20.1 us (58%)
  Pallas kernels  6.86 us (20%)
  starting transfers between devices  6.34 us (18%)
  between operations  0.72 us (2%)
    all_to_all x1, blocking collectives, per_device(): stats = lax.all_to_all(stats, ('ma', 'freq'), 0, 0, tiled=True)  20.1 us
    ppermute x2, starting transfers between devices, collect(): return lax.ppermute(x, 'freq', [(i - 1, i) for i in summing])  3.7 us
    pallas_call x1, Pallas kernels, project(): pl.pallas_call(project_kernel, in_specs=[HBM, HBM], out_specs=[VMEM] * 5,...  3.46 us
    pallas_call x1, Pallas kernels, back(): pl.pallas_call(functools.partial(back_kernel, freq_size), in_specs=[VMEM]...  2.83 us
    ppermute x2, starting transfers between devices, swap(): return lax.ppermute(x, 'freq', [(i, i ^ bit) for i in summing])  1.35 us
    ppermute x1, starting transfers between devices, hand_back(): return lax.ppermute(x, 'freq', [(i, i - 1) for i in summing])  1.29 us
  transfers between devices with their start and end apart: 5, of which 1 were waited for; matrix products, arithmetic and copies ran while one was open for 0% of the time, Pallas kernels for 1%

profile of v7, /device:TPU:0, one launch (start us, length us, event | category | flops | bytes accessed | tf_op | source)
XLA Modules:
  0.0 34.5 jit_solution(18174037526262326359)
XLA Ops:
  0.6 3.5 %project.1 = (bf16[1,384,256]{2,1,0:T(8,128)(2,1)S(1)}, f32[1,384,256]{2,1,0:T(8,128)S(1)}, f32[1,2,384,256]{3,2,1,0:T(8,128)S(1)}, bf16[1,192,2,512]{3,2,1,0:T(2,128)(2,1)S(1)}, bf16[2,4,2,512,256]{4,3,2,1,0:T(8,128)(2,1)S(1)}) custom-call(bf16[2,192,4,2,512]{4,3,2,1,0:T(2,128)(2,1)} %v_hbm.1, bf16[2,4,2,512,256]{4,3,2,1,0:T(8,128)(2,1)} %e_hbm.1), custom_call_target="tpu_custom_call" | custom-call | flops 1610612736 | bytes 7340032 | tf_op jit(solution)/shard_map/project/pallas_call | solution.py:81
  4.1 0.0 copy-start
  4.1 2.4 %collective-permute-start = (bf16[1,384,256]{2,1,0:T(8,128)(2,1)S(1)}, bf16[1,384,256]{2,1,0:T(8,128)(2,1)S(1)}, u32[]{:S(2)}, u32[]{:S(2)}) collective-permute-start(bf16[1,384,256]{2,1,0:T(8,128)(2,1)S(1)} %get-tuple-element.12), channel_id=1, source_target_pairs={{0,1},{2,3},{4,5},{6,7},{8,9},{10,11},{12,13},{14,15},{16,17},{18,... | collective-permute-start | bytes 589832 | tf_op jit(solution)/shard_map/ppermute | solution.py:230
  6.5 0.4 %rest.1 = (bf16[1,384,256]{2,1,0:T(8,128)(2,1)S(1)}, f32[1,384,256]{2,1,0:T(8,128)S(1)}) custom-call(f32[1,2,384,256]{3,2,1,0:T(8,128)S(1)} %get-tuple-element.13.part_ref, bf16[1,192,2,512]{3,2,1,0:T(2,128)(2,1)S(1)} %get-tuple-element.14.v_ref, bf16[2,4,2,512,256]{4,3,2,1,0:T(8,128)(2,1)S(1)} %get-tuple-element.15.e_ref), custom_call_target="tpu_custom_call" | custom-call | flops 201326592 | bytes 393216 | tf_op jit(solution)/shard_map/rest/pallas_call | solution.py:117
  6.9 1.3 %collective-permute-start.2 = (bf16[1,384,256]{2,1,0:T(8,128)(2,1)S(1)}, bf16[1,384,256]{2,1,0:T(8,128)(2,1)S(1)}, u32[]{:S(2)}, u32[]{:S(2)}) collective-permute-start(bf16[1,384,256]{2,1,0:T(8,128)(2,1)S(1)} %get-tuple-element.17), channel_id=1, source_target_pairs={{0,1},{2,3},{4,5},{6,7},{8,9},{10,11},{12,13},{14,15},{16,17},{18,... | collective-permute-start | bytes 589832 | tf_op jit(solution)/shard_map/ppermute | solution.py:230
  8.2 0.0 collective-permute-done
  8.3 0.1 add_convert_fusion.1.a_ref
  8.3 0.7 %collective-permute-start.1 = (bf16[1,384,256]{2,1,0:T(8,128)(2,1)S(1)}, bf16[1,384,256]{2,1,0:T(8,128)(2,1)S(1)}, u32[]{:S(2)}, u32[]{:S(2)}) collective-permute-start(bf16[1,384,256]{2,1,0:T(8,128)(2,1)S(1)} %add_convert_fusion.1.a_ref), channel_id=1, source_target_pairs={{1,3},{3,1},{5,7},{7,5},{9,11},{11,9},{13,15},{15,13},{17,19},{19,... | collective-permute-start | bytes 589832 | tf_op jit(solution)/shard_map/ppermute | solution.py:236
  9.0 0.3 collective-permute-done.2
  9.3 0.7 %collective-permute-start.3 = (bf16[1,384,256]{2,1,0:T(8,128)(2,1)S(1)}, bf16[1,384,256]{2,1,0:T(8,128)(2,1)S(1)}, u32[]{:S(2)}, u32[]{:S(2)}) collective-permute-start(bf16[1,384,256]{2,1,0:T(8,128)(2,1)S(1)} %add_convert_fusion.b_ref), channel_id=1, source_target_pairs={{1,3},{3,1},{5,7},{7,5},{9,11},{11,9},{13,15},{15,13},{17,19},{19,... | collective-permute-start | bytes 589832 | tf_op jit(solution)/shard_map/ppermute | solution.py:236
  10.0 0.0 copy-done
  10.0 0.1 compare_convert_fusion.keep_ref
  10.1 0.0 collective-permute-done.1.a_their_ref
  10.1 0.0 collective-permute-done.3.b_their_ref
  10.1 0.2 power.1
  10.3 1.3 %collective-permute-start.4 = (f32[2,384,256]{2,1,0:T(8,128)S(1)}, f32[2,384,256]{2,1,0:T(8,128)S(1)}, u32[]{:S(2)}, u32[]{:S(2)}) collective-permute-start(f32[2,384,256]{2,1,0:T(8,128)S(1)} %get-tuple-element.19.mine_ref), channel_id=1, source_target_pairs={{1,0},{3,2},{5,4},{7,6},{9,8},{11,10},{13,12},{15,14},{17,16},{19,... | collective-permute-start | bytes 2359304 | tf_op jit(solution)/shard_map/ppermute | solution.py:233
  11.6 20.1 %all_to_all.5.stats_ref = f32[32,2,256]{2,1,0:T(2,128)S(1)} all-to-all(f32[32,2,256]{2,1,0:T(2,128)S(1)} %get-tuple-element.18), channel_id=1, replica_groups=mesh['ma'=8,'freq'=4] {'ma','freq'}, dimensions={0} | all-to-all | bytes 131072 | tf_op jit(solution)/shard_map/all_to_all | solution.py:250
  31.7 0.0 collective-permute-done.4.other_ref
  31.7 2.8 %back.1 = (bf16[2,2,192,256]{3,2,1,0:T(8,128)(2,1)}, bf16[2,192,4,2,512]{4,3,2,1,0:T(2,128)(2,1)}) custom-call(f32[2,256]{1,0:T(2,128)S(1)} %compare_convert_fusion.keep_ref, f32[32,2,256]{2,1,0:T(2,128)S(1)} %all_to_all.5.stats_ref, f32[2,384,256]{2,1,0:T(8,128)S(1)} %get-tuple-element.19.mine_ref, f32[2,384,256]{2,1,0:T(8,128)S(1)} %collective-permute-done.4.other_ref, ...), custom_call_target="tpu_custom_call" | custom-call | tf_op jit(solution)/shard_map/back/pallas_call | solution.py:201
  (1 shorter events, 0.0 us)
Async XLA Ops:
  4.1 5.9 %copy-start = (s32[2]{0:T(128)S(1)}, s32[2]{0:T(128)}, u32[]{:S(2)}) copy-start(s32[2]{0:T(128)} %param.5) | copy-start | bytes 28
  4.1 4.1 %collective-permute-start = (bf16[1,384,256]{2,1,0:T(8,128)(2,1)S(1)}, bf16[1,384,256]{2,1,0:T(8,128)(2,1)S(1)}, u32[]{:S(2)}, u32[]{:S(2)}) collective-permute-start(bf16[1,384,256]{2,1,0:T(8,128)(2,1)S(1)} %get-tuple-element.12), channel_id=1, source_target_pairs={{0,1},{2,3},{4,5},{6,7},{8,9},{10,11},{12,13},{14,15},{16,17},{18,... | collective-permute-start | bytes 589832 | tf_op jit(solution)/shard_map/ppermute | solution.py:230
  6.9 2.4 %collective-permute-start.2 = (bf16[1,384,256]{2,1,0:T(8,128)(2,1)S(1)}, bf16[1,384,256]{2,1,0:T(8,128)(2,1)S(1)}, u32[]{:S(2)}, u32[]{:S(2)}) collective-permute-start(bf16[1,384,256]{2,1,0:T(8,128)(2,1)S(1)} %get-tuple-element.17), channel_id=1, source_target_pairs={{0,1},{2,3},{4,5},{6,7},{8,9},{10,11},{12,13},{14,15},{16,17},{18,... | collective-permute-start | bytes 589832 | tf_op jit(solution)/shard_map/ppermute | solution.py:230
  8.3 1.8 %collective-permute-start.1 = (bf16[1,384,256]{2,1,0:T(8,128)(2,1)S(1)}, bf16[1,384,256]{2,1,0:T(8,128)(2,1)S(1)}, u32[]{:S(2)}, u32[]{:S(2)}) collective-permute-start(bf16[1,384,256]{2,1,0:T(8,128)(2,1)S(1)} %add_convert_fusion.1.a_ref), channel_id=1, source_target_pairs={{1,3},{3,1},{5,7},{7,5},{9,11},{11,9},{13,15},{15,13},{17,19},{19,... | collective-permute-start | bytes 589832 | tf_op jit(solution)/shard_map/ppermute | solution.py:236
  9.3 0.8 %collective-permute-start.3 = (bf16[1,384,256]{2,1,0:T(8,128)(2,1)S(1)}, bf16[1,384,256]{2,1,0:T(8,128)(2,1)S(1)}, u32[]{:S(2)}, u32[]{:S(2)}) collective-permute-start(bf16[1,384,256]{2,1,0:T(8,128)(2,1)S(1)} %add_convert_fusion.b_ref), channel_id=1, source_target_pairs={{1,3},{3,1},{5,7},{7,5},{9,11},{11,9},{13,15},{15,13},{17,19},{19,... | collective-permute-start | bytes 589832 | tf_op jit(solution)/shard_map/ppermute | solution.py:236
  10.3 21.4 %collective-permute-start.4 = (f32[2,384,256]{2,1,0:T(8,128)S(1)}, f32[2,384,256]{2,1,0:T(8,128)S(1)}, u32[]{:S(2)}, u32[]{:S(2)}) collective-permute-start(f32[2,384,256]{2,1,0:T(8,128)S(1)} %get-tuple-element.19.mine_ref), channel_id=1, source_target_pairs={{1,0},{3,2},{5,4},{7,6},{9,8},{11,10},{13,12},{15,14},{17,16},{19,... | collective-permute-start | bytes 2359304 | tf_op jit(solution)/shard_map/ppermute | solution.py:233

commit v8 on v6

--- a/solution.py
+++ b/solution.py
@@ -202,28 +202,60 @@
     )(stats)
 
 
-def pieces(m, c, y, quarters, mine_ref, other_ref):
-    half = mine_ref.shape[0]
-    if m < half:
-        own, core, chip, both = [q[m].astype(F32) for q in quarters]
-        rows = own.shape[0]
-        for c_of in range(2):
-            near, far = jnp.where(c == c_of, own, core), jnp.where(c == c_of, chip, both)
-            for y_of in range(2):
-                yield (2 * c_of + y_of) * rows, jnp.where(y == y_of, near, far)
-    else:
-        mine, other = mine_ref[m - half], other_ref[m - half]
-        for c_of in range(2):
-            yield c_of * mine.shape[0], jnp.where(c == c_of, mine, other)
-
-
-def back_kernel(
-    keep_ref, scale_ref, q0_ref, q1_ref, q2_ref, q3_ref, mine_ref, other_ref, e_ref, coef_hbm, out_hbm, pair, flat, coef_buf, out_buf, coef_sem, out_sem
-):
-    modes, freqs, samples, _, base = out_buf.shape
-    kmax = mine_ref.shape[-1]
+def half_pieces(j, mine_ref, other_ref):
+    for c in range(2):
+        yield c * mine_ref.shape[1], jnp.where(side() == c, mine_ref[j], other_ref[j])
+
+
+def quarter_pieces(j, own_ref, chip_ref, core_ref):
+    own, chip, core, both = [q.astype(F32) for q in (own_ref[j], chip_ref[j], core_ref[0, j], core_ref[1, j])]
+    for c in range(2):
+        near, far = jnp.where(side() == c, own, core), jnp.where(side() == c, chip, both)
+        for y in range(2):
+            yield (2 * c + y) * own.shape[0], jnp.where(side(1) == y, near, far)
+
+
+def filter_mode(m, pieces, keep_ref, scale_ref, e_ref, pair, flat, coef_ref, out_ref, after_coef, after_out):
+    freqs, samples, _, base = out_ref.shape
+    kmax = pair.shape[1] // 2
     lanes = flat.shape[2]
     contract = (((1,), (1,)), ((), ()))
+    gain = keep_ref[m : m + 1] * scale_ref[...]
+    for start, proj in pieces:
+        coef = proj * gain
+        at = slice(start, start + coef.shape[0])
+        pair[at, :kmax] = coef.astype(BF16)
+        pair[at, kmax:] = times_i(coef).astype(BF16)
+        for i in range(kmax // lanes):
+            flat[i, at, :] = coef[:, i * lanes : (i + 1) * lanes]
+    for f in range(freqs):
+        out = lax.dot_general(pair[:, :kmax], e_ref[m, f, 0], contract, preferred_element_type=F32)
+        out += lax.dot_general(pair[:, kmax:], e_ref[m, f, 1], contract, preferred_element_type=F32)
+        out_ref[f] = out.astype(BF16).reshape(samples, 2, base)
+        if f == 0:
+            for i in range(kmax // lanes):
+                for part in range(2):
+                    every = flat[i, pl.ds(part, samples, stride=2), :]
+                    coef_ref[part, :, i * lanes : (i + 1) * lanes] = every.astype(BF16)
+            after_coef()
+        after_out(f)
+
+
+def nothing(*_):
+    pass
+
+
+def back_b_kernel(keep_ref, scale_ref, mine_ref, other_ref, e_ref, coef_ref, out_ref, pair, flat):
+    half = mine_ref.shape[0]
+    for j in range(half):
+        rows = half_pieces(j, mine_ref, other_ref)
+        filter_mode(half + j, rows, keep_ref, scale_ref, e_ref, pair, flat, coef_ref.at[j], out_ref.at[j], nothing, nothing)
+
+
+def back_a_kernel(
+    keep_ref, scale_ref, own_ref, chip_ref, core_ref, coef_b, out_b, e_ref, coef_hbm, out_hbm, pair, flat, coef_buf, out_buf, coef_sem, out_sem
+):
+    half, freqs = out_buf.shape[:2]
     pending = []
 
     def send(src, dst, sem):
@@ -231,36 +263,44 @@
         copy.start()
         pending.append(copy)
 
-    for m in range(modes):
-        gain = keep_ref[m : m + 1] * scale_ref[...]
-        for start, proj in pieces(m, side(), side(1), (q0_ref, q1_ref, q2_ref, q3_ref), mine_ref, other_ref):
-            coef = proj * gain
-            at = slice(start, start + coef.shape[0])
-            pair[at, :kmax] = coef.astype(BF16)
-            pair[at, kmax:] = times_i(coef).astype(BF16)
-            for i in range(kmax // lanes):
-                flat[i, at, :] = coef[:, i * lanes : (i + 1) * lanes]
+    for j in range(half):
+        send(coef_b.at[j], coef_hbm.at[half + j], coef_sem.at[half + j])
         for f in range(freqs):
-            out = lax.dot_general(pair[:, :kmax], e_ref[m, f, 0], contract, preferred_element_type=F32)
-            out += lax.dot_general(pair[:, kmax:], e_ref[m, f, 1], contract, preferred_element_type=F32)
-            out_buf[m, f] = out.astype(BF16).reshape(samples, 2, base)
-            if f == 0:
-                for i in range(kmax // lanes):
-                    for part in range(2):
-                        every = flat[i, pl.ds(part, samples, stride=2), :]
-                        coef_buf[m, part, :, i * lanes : (i + 1) * lanes] = every.astype(BF16)
-                send(coef_buf.at[m], coef_hbm.at[m], coef_sem.at[m])
-            send(out_buf.at[m, f], out_hbm.at[m, :, f], out_sem.at[m, f])
+            send(out_b.at[j, f], out_hbm.at[half + j, :, f], out_sem.at[half + j, f])
+    for j in range(half):
+        filter_mode(
+            j, quarter_pieces(j, own_ref, chip_ref, core_ref), keep_ref, scale_ref, e_ref, pair, flat, coef_buf.at[j], out_buf.at[j],
+            lambda j=j: send(coef_buf.at[j], coef_hbm.at[j], coef_sem.at[j]),
+            lambda f, j=j: send(out_buf.at[j, f], out_hbm.at[j, :, f], out_sem.at[j, f]),
+        )
     for copy in pending:
         copy.wait()
 
 
-def back(keep, scale, quarters, mine, other, e):
+def back_b(keep, scale, mine, other, e):
+    _, freqs, _, base, kmax = e.shape
+    half, samples = mine.shape[:2]
+    return pl.pallas_call(
+        back_b_kernel,
+        in_specs=[VMEM] * 5,
+        out_specs=[VMEM] * 2,
+        out_shape=[
+            jax.ShapeDtypeStruct((half, 2, samples, kmax), BF16),
+            jax.ShapeDtypeStruct((half, freqs, samples, 2, base), BF16),
+        ],
+        scratch_shapes=[pltpu.VMEM((2 * samples, 2 * kmax), BF16), pltpu.VMEM((kmax // 128, 2 * samples, 128), F32)],
+        name="back_b",
+        compiler_params=limit(MIB * 16),
+        cost_estimate=cost(8 * half * samples * freqs * base * kmax, mine, other),
+    )(keep, scale, mine, other, e)
+
+
+def back_a(keep, scale, quarters, done, e):
     modes, freqs, _, base, kmax = e.shape
-    samples = mine.shape[1]
-    return pl.pallas_call(
-        back_kernel,
-        in_specs=[VMEM] * 9,
+    half, _, samples, _ = done[0].shape
+    return pl.pallas_call(
+        back_a_kernel,
+        in_specs=[VMEM] * 8,
         out_specs=[HBM, HBM],
         out_shape=[
             jax.ShapeDtypeStruct((modes, 2, samples, kmax), BF16),
@@ -269,14 +309,14 @@
         scratch_shapes=[
             pltpu.VMEM((2 * samples, 2 * kmax), BF16),
             pltpu.VMEM((kmax // 128, 2 * samples, 128), F32),
-            pltpu.VMEM((modes, 2, samples, kmax), BF16),
-            pltpu.VMEM((modes, freqs, samples, 2, base), BF16),
+            pltpu.VMEM((half, 2, samples, kmax), BF16),
+            pltpu.VMEM((half, freqs, samples, 2, base), BF16),
             pltpu.SemaphoreType.DMA((modes,)),
             pltpu.SemaphoreType.DMA((modes, freqs)),
         ],
-        name="back",
+        name="back_a",
         compiler_params=limit(MIB * 16),
-    )(keep, scale, *quarters, mine, other, e)
+    )(keep, scale, *quarters, *done, e)
 
 
 def filter_modes(visibilities, eigenmodes, retained):
@@ -304,13 +344,14 @@
         bit *= 2
     quarter = quarter.astype(BF16)
     total, theirs = over_chips((keep_b + swap(give_b, 1).astype(F32)).astype(BF16))
-    quarters = [quarter]
-    for bits in (1, 2, 3):
-        quarters.append(swap(quarter, bits))
+    chip = swap(quarter, 2)
     mine, stats = power_of(keep, freq_size, quarter, total, theirs, ma_size * freq_size)
     other = swap(mine, 1)
-    scale = pool(lax.all_to_all(stats, ("ma", "freq"), 0, 0, tiled=True), visibilities.shape[1])
-    return tuple(back(keep, scale, quarters, mine, other, e_vmem))
+    stats = lax.all_to_all(stats, ("ma", "freq"), 0, 0, tiled=True)
+    scale = pool(stats, visibilities.shape[1])
+    core = swap(jnp.stack([quarter, chip]), 1)
+    done = back_b(keep, scale, mine, other, e_vmem)
+    return tuple(back_a(keep, scale, (quarter, chip, core), done, e_vmem))
 
 
 def solution(mesh):

time: 34.3 us -> 33.3 us (0.971)
  waiting for transfers between devices: 9.31 us -> 11.5 us
  local copies, waits for them, and re-layouts: 4.15 us -> 2.19 us
  starting transfers between devices: 12.3 us -> 10.9 us
    unnamed x6, local copies, waits for them, and re-layouts: 4.15 us -> 2.19 us
    all_to_all x1, waiting for transfers between devices: 5.46 us -> 7.06 us  [filter_modes(): stats = lax.all_to_all(stats, ('ma', 'freq'), 0, 0, tiled=True)]
    all_to_all x1, starting transfers between devices: 5.93 us -> 4.89 us  [filter_modes(): stats = lax.all_to_all(stats, ('ma', 'freq'), 0, 0, tiled=True)]
    ppermute x8 -> x7, waiting for transfers between devices: 3.85 us -> 4.43 us  [swap(): return lax.ppermute(x, 'freq', [(i, i ^ bit) for i in range(freq_size)])]
    ppermute x8 -> x7, starting transfers between devices: 6.42 us -> 5.98 us  [swap(): return lax.ppermute(x, 'freq', [(i, i ^ bit) for i in range(freq_size)])]
    pallas_call x1 -> x2, Pallas kernels: 2.78 us -> 3.01 us  [the longest x1 1.95 us: back_a(): pl.pallas_call(back_a_kernel, in_specs=[VMEM] * 8, out_specs=[HBM, HBM],...]
  transfers between devices with their start and end apart: 9 -> 8, of which waited for: 3 -> 4; matrix products, arithmetic and copies ran while one was open for 0% -> 0% of each run, Pallas kernels for 1% -> 5%
where the time goes in v8:
time: 33.3 us; the launch traced here: 33.1 us
  waiting for transfers between devices  11.5 us (35%)
  starting transfers between devices  10.9 us (33%)
  Pallas kernels  7.68 us (23%)
  local copies, waits for them, and re-layouts  2.19 us (7%)
  between operations  0.74 us (2%)
    all_to_all x1, waiting for transfers between devices, filter_modes(): stats = lax.all_to_all(stats, ('ma', 'freq'), 0, 0, tiled=True)  7.06 us
    ppermute x7, starting transfers between devices, swap(): return lax.ppermute(x, 'freq', [(i, i ^ bit) for i in range(freq_size)])  5.98 us
    all_to_all x1, starting transfers between devices, filter_modes(): stats = lax.all_to_all(stats, ('ma', 'freq'), 0, 0, tiled=True)  4.89 us
    ppermute x7, waiting for transfers between devices, swap(): return lax.ppermute(x, 'freq', [(i, i ^ bit) for i in range(freq_size)])  4.43 us
    pallas_call x1, Pallas kernels, project(): pl.pallas_call(project_kernel, in_specs=[HBM, HBM], out_specs=[VMEM] * 5,...  3.45 us
    unnamed x6, local copies, waits for them, and re-layouts  2.19 us
    pallas_call x1, Pallas kernels, back_a(): pl.pallas_call(back_a_kernel, in_specs=[VMEM] * 8, out_specs=[HBM, HBM],...  1.95 us
    pallas_call x1, Pallas kernels, back_b(): pl.pallas_call(back_b_kernel, in_specs=[VMEM] * 5, out_specs=[VMEM] * 2,...  1.06 us
  transfers between devices with their start and end apart: 8, of which 4 were waited for; matrix products, arithmetic and copies ran while one was open for 0% of the time, Pallas kernels for 5%

profile of v8, /device:TPU:0, one launch (start us, length us, event | category | flops | bytes accessed | tf_op | source)
XLA Modules:
  0.0 33.1 jit_solution(5329597852091645496)
XLA Ops:
  0.6 3.4 %project.1 = (bf16[1,192,256]{2,1,0:T(8,128)(2,1)S(1)}, f32[1,192,256]{2,1,0:T(8,128)S(1)}, f32[1,2,384,256]{3,2,1,0:T(8,128)S(1)}, bf16[1,192,2,512]{3,2,1,0:T(2,128)(2,1)S(1)}, bf16[2,4,2,512,256]{4,3,2,1,0:T(8,128)(2,1)S(1)}) custom-call(bf16[2,192,4,2,512]{4,3,2,1,0:T(2,128)(2,1)} %v_hbm.1, bf16[2,4,2,512,256]{4,3,2,1,0:T(8,128)(2,1)} %e_hbm.1), custom_call_target="tpu_custom_call" | custom-call | flops 1610612736 | bytes 7340032 | tf_op jit(solution)/shard_map/project/pallas_call | solution.py:84
  4.1 0.0 copy-start
  4.1 0.0 copy-start.2
  4.1 0.6 %collective-permute-start = (bf16[1,192,256]{2,1,0:T(8,128)(2,1)S(1)}, bf16[1,192,256]{2,1,0:T(8,128)(2,1)S(1)}, u32[]{:S(2)}, u32[]{:S(2)}) collective-permute-start(bf16[1,192,256]{2,1,0:T(8,128)(2,1)S(1)} %get-tuple-element.16), channel_id=1, source_target_pairs={{0,1},{1,0},{2,3},{3,2},{4,5},{5,4},{6,7},{7,6},{8,9},{9,8},{10,11... | collective-permute-start | bytes 294920 | tf_op jit(solution)/shard_map/ppermute | solution.py:328
  4.7 0.4 %rest.1 = (bf16[1,192,256]{2,1,0:T(8,128)(2,1)S(1)}, f32[1,192,256]{2,1,0:T(8,128)S(1)}) custom-call(f32[1,2,384,256]{3,2,1,0:T(8,128)S(1)} %get-tuple-element.19.part_ref, bf16[1,192,2,512]{3,2,1,0:T(2,128)(2,1)S(1)} %get-tuple-element.20.v_ref, bf16[2,4,2,512,256]{4,3,2,1,0:T(8,128)(2,1)S(1)} %get-tuple-element.21.e_ref), custom_call_target="tpu_custom_call" | custom-call | flops 201326592 | bytes 393216 | tf_op jit(solution)/shard_map/rest/pallas_call | solution.py:120
  5.1 0.1 collective-permute-start.2
  5.2 0.0 copy-done.2
  5.2 0.1 compare_convert_fusion.keep_ref
  5.3 0.4 %collective-permute-done.theirs_ref = bf16[1,192,256]{2,1,0:T(8,128)(2,1)S(1)} collective-permute-done((bf16[1,192,256]{2,1,0:T(8,128)(2,1)S(1)}, bf16[1,192,256]{2,1,0:T(8,128)(2,1)S(1)}, u32[]{:S(2)}, u32[]{:S(2)}) %collective-permute-start) | collective-permute-done | bytes 98336 | tf_op jit(solution)/shard_map/ppermute | solution.py:328
  5.6 2.9 %collective-permute-start.1 = (bf16[1,96,256]{2,1,0:T(8,128)(2,1)S(1)}, bf16[1,96,256]{2,1,0:T(8,128)(2,1)S(1)}, u32[]{:S(2)}, u32[]{:S(2)}) collective-permute-start(bf16[1,96,256]{2,1,0:T(8,128)(2,1)S(1)} %get-tuple-element.18), channel_id=1, source_target_pairs={{0,2},{1,3},{2,0},{3,1},{4,6},{5,7},{6,4},{7,5},{8,10},{9,11},{10,... | collective-permute-start | bytes 147464 | tf_op jit(solution)/shard_map/ppermute | solution.py:328
  8.6 0.0 collective-permute-done.2
  8.6 0.6 %collective-permute-start.3 = (bf16[1,192,256]{2,1,0:T(8,128)(2,1)S(1)}, bf16[1,192,256]{2,1,0:T(8,128)(2,1)S(1)}, u32[]{:S(2)}, u32[]{:S(2)}) collective-permute-start(bf16[1,192,256]{2,1,0:T(8,128)(2,1)S(1)} %add_convert_fusion.b_ref), channel_id=1, source_target_pairs={{0,2},{1,3},{2,0},{3,1},{4,6},{5,7},{6,4},{7,5},{8,10},{9,11},{10,... | collective-permute-start | bytes 294920 | tf_op jit(solution)/shard_map/ppermute | solution.py:328
  9.2 1.5 %collective-permute-done.1 = bf16[1,96,256]{2,1,0:T(8,128)(2,1)S(1)} collective-permute-done((bf16[1,96,256]{2,1,0:T(8,128)(2,1)S(1)}, bf16[1,96,256]{2,1,0:T(8,128)(2,1)S(1)}, u32[]{:S(2)}, u32[]{:S(2)}) %collective-permute-start.1) | collective-permute-done | bytes 49184 | tf_op jit(solution)/shard_map/ppermute | solution.py:328
  10.7 2.6 %collective-permute-done.3.b_their_ref = bf16[1,192,256]{2,1,0:T(8,128)(2,1)S(1)} collective-permute-done((bf16[1,192,256]{2,1,0:T(8,128)(2,1)S(1)}, bf16[1,192,256]{2,1,0:T(8,128)(2,1)S(1)}, u32[]{:S(2)}, u32[]{:S(2)}) %collective-permute-start.3) | collective-permute-done | bytes 98336 | tf_op jit(solution)/shard_map/ppermute | solution.py:328
  13.3 0.7 %power.1 = (f32[1,192,256]{2,1,0:T(8,128)S(1)}, f32[32,2,256]{2,1,0:T(2,128)}) custom-call(f32[2,256]{1,0:T(2,128)S(1)} %compare_convert_fusion.keep_ref, bf16[1,96,256]{2,1,0:T(8,128)(2,1)S(1)} %add_convert_fusion.1.quarter_ref.own_ref, bf16[1,192,256]{2,1,0:T(8,128)(2,1)S(1)} %add_convert_fusion.b_ref, ...), custom_call_target="tpu_custom_call" | custom-call | tf_op jit(solution)/shard_map/power/pallas_call | solution.py:175
  14.0 0.0 copy-done
  14.0 0.0 collective-permute-start.6
  14.0 1.5 %collective-permute-start.4 = (bf16[1,96,256]{2,1,0:T(8,128)(2,1)S(1)}, bf16[1,96,256]{2,1,0:T(8,128)(2,1)S(1)}, u32[]{:S(2)}, u32[]{:S(2)}) collective-permute-start(bf16[1,96,256]{2,1,0:T(8,128)(2,1)S(1)} %add_convert_fusion.1.quarter_ref.own_ref), channel_id=1, source_target_pairs={{0,2},{1,3},{2,0},{3,1},{4,6},{5,7},{6,4},{7,5},{8,10},{9,11},{10,... | collective-permute-start | bytes 147464 | tf_op jit(solution)/shard_map/ppermute | solution.py:328
  15.5 4.9 %all-to-all-start = ((f32[32,2,256]{2,1,0:T(2,128)}), f32[32,2,256]{2,1,0:T(2,128)S(1)}, u32[]{:S(2)}, u32[]{:S(2)}) async-start(f32[32,2,256]{2,1,0:T(2,128)} %get-tuple-element.24), calls=%async_computation | async-start | bytes 131072 | tf_op jit(solution)/shard_map/all_to_all | solution.py:350
  20.4 0.0 collective-permute-done.4.chip_ref
  20.4 0.3 collective-permute-start.5
  20.7 7.1 %all-to-all-done.stats_ref = f32[32,2,256]{2,1,0:T(2,128)S(1)} async-done(((f32[32,2,256]{2,1,0:T(2,128)}), f32[32,2,256]{2,1,0:T(2,128)S(1)}, u32[]{:S(2)}, u32[]{:S(2)}) %all-to-all-start) | async-done | bytes 65568 | tf_op jit(solution)/shard_map/all_to_all | solution.py:350
  27.8 0.1 pool.1.scale_ref
  27.9 0.0 collective-permute-done.6.other_ref
  27.9 0.0 copy-start.1
  27.9 2.2 %copy-done.1 = bf16[2,4,2,512,256]{4,3,2,1,0:T(8,128)(2,1)S(1)} copy-done((bf16[2,4,2,512,256]{4,3,2,1,0:T(8,128)(2,1)S(1)}, bf16[2,4,2,512,256]{4,3,2,1,0:T(8,128)(2,1)}, u32[]{:S(2)}) %copy-start.1) | copy-done | bytes 4194328
  30.1 1.1 %back_b.1 = (bf16[1,2,192,256]{3,2,1,0:T(8,128)(2,1)S(1)}, bf16[1,4,192,2,512]{4,3,2,1,0:T(2,128)(2,1)S(1)}) custom-call(f32[2,256]{1,0:T(2,128)S(1)} %compare_convert_fusion.keep_ref, f32[1,256]{1,0:T(1,128)S(1)} %pool.1.scale_ref, f32[1,192,256]{2,1,0:T(8,128)S(1)} %get-tuple-element.25.mine_ref, f32[1,192,256]{2,1,0:T(8,128)S(1)} %collective-permute-done.6.other_ref, ...), custom_call_target="tpu_custom_call" | custom-call | flops 805306368 | bytes 393216 | tf_op jit(solution)/shard_map/back_b/pallas_call | solution.py:283
  31.1 0.0 collective-permute-done.5.core_ref
  31.1 1.9 %back_a.1 = (bf16[2,2,192,256]{3,2,1,0:T(8,128)(2,1)}, bf16[2,192,4,2,512]{4,3,2,1,0:T(2,128)(2,1)}) custom-call(f32[2,256]{1,0:T(2,128)S(1)} %compare_convert_fusion.keep_ref, f32[1,256]{1,0:T(1,128)S(1)} %pool.1.scale_ref, bf16[1,96,256]{2,1,0:T(8,128)(2,1)S(1)} %add_convert_fusion.1.quarter_ref.own_ref, ...), custom_call_target="tpu_custom_call" | custom-call | tf_op jit(solution)/shard_map/back_a/pallas_call | solution.py:301
  (4 shorter events, 0.1 us)
Async XLA Ops:
  4.1 9.9 %copy-start = (bf16[2,4,2,512,256]{4,3,2,1,0:T(8,128)(2,1)}, bf16[2,4,2,512,256]{4,3,2,1,0:T(8,128)(2,1)S(1)}, u32[]{:S(2)}) copy-start(bf16[2,4,2,512,256]{4,3,2,1,0:T(8,128)(2,1)S(1)} %get-tuple-element.21.e_ref) | copy-start | bytes 12582916
  4.1 1.1 %copy-start.2 = (s32[2]{0:T(128)S(1)}, s32[2]{0:T(128)}, u32[]{:S(2)}) copy-start(s32[2]{0:T(128)} %param.5) | copy-start | bytes 28
  4.1 1.5 %collective-permute-start = (bf16[1,192,256]{2,1,0:T(8,128)(2,1)S(1)}, bf16[1,192,256]{2,1,0:T(8,128)(2,1)S(1)}, u32[]{:S(2)}, u32[]{:S(2)}) collective-permute-start(bf16[1,192,256]{2,1,0:T(8,128)(2,1)S(1)} %get-tuple-element.16), channel_id=1, source_target_pairs={{0,1},{1,0},{2,3},{3,2},{4,5},{5,4},{6,7},{7,6},{8,9},{9,8},{10,11... | collective-permute-start | bytes 294920 | tf_op jit(solution)/shard_map/ppermute | solution.py:328
  5.1 3.5 %collective-permute-start.2 = (bf16[1,192,256]{2,1,0:T(8,128)(2,1)S(1)}, bf16[1,192,256]{2,1,0:T(8,128)(2,1)S(1)}, u32[]{:S(2)}, u32[]{:S(2)}) collective-permute-start(bf16[1,192,256]{2,1,0:T(8,128)(2,1)S(1)} %get-tuple-element.23), channel_id=1, source_target_pairs={{0,1},{1,0},{2,3},{3,2},{4,5},{5,4},{6,7},{7,6},{8,9},{9,8},{10,11... | collective-permute-start | bytes 294920 | tf_op jit(solution)/shard_map/ppermute | solution.py:328
  5.6 5.0 %collective-permute-start.1 = (bf16[1,96,256]{2,1,0:T(8,128)(2,1)S(1)}, bf16[1,96,256]{2,1,0:T(8,128)(2,1)S(1)}, u32[]{:S(2)}, u32[]{:S(2)}) collective-permute-start(bf16[1,96,256]{2,1,0:T(8,128)(2,1)S(1)} %get-tuple-element.18), channel_id=1, source_target_pairs={{0,2},{1,3},{2,0},{3,1},{4,6},{5,7},{6,4},{7,5},{8,10},{9,11},{10,... | collective-permute-start | bytes 147464 | tf_op jit(solution)/shard_map/ppermute | solution.py:328
  8.6 4.7 %collective-permute-start.3 = (bf16[1,192,256]{2,1,0:T(8,128)(2,1)S(1)}, bf16[1,192,256]{2,1,0:T(8,128)(2,1)S(1)}, u32[]{:S(2)}, u32[]{:S(2)}) collective-permute-start(bf16[1,192,256]{2,1,0:T(8,128)(2,1)S(1)} %add_convert_fusion.b_ref), channel_id=1, source_target_pairs={{0,2},{1,3},{2,0},{3,1},{4,6},{5,7},{6,4},{7,5},{8,10},{9,11},{10,... | collective-permute-start | bytes 294920 | tf_op jit(solution)/shard_map/ppermute | solution.py:328
  14.0 13.9 %collective-permute-start.6 = (f32[1,192,256]{2,1,0:T(8,128)S(1)}, f32[1,192,256]{2,1,0:T(8,128)S(1)}, u32[]{:S(2)}, u32[]{:S(2)}) collective-permute-start(f32[1,192,256]{2,1,0:T(8,128)S(1)} %get-tuple-element.25.mine_ref), channel_id=1, source_target_pairs={{0,1},{1,0},{2,3},{3,2},{4,5},{5,4},{6,7},{7,6},{8,9},{9,8},{10,11... | collective-permute-start | bytes 589832 | tf_op jit(solution)/shard_map/ppermute | solution.py:328
  14.0 6.4 %collective-permute-start.4 = (bf16[1,96,256]{2,1,0:T(8,128)(2,1)S(1)}, bf16[1,96,256]{2,1,0:T(8,128)(2,1)S(1)}, u32[]{:S(2)}, u32[]{:S(2)}) collective-permute-start(bf16[1,96,256]{2,1,0:T(8,128)(2,1)S(1)} %add_convert_fusion.1.quarter_ref.own_ref), channel_id=1, source_target_pairs={{0,2},{1,3},{2,0},{3,1},{4,6},{5,7},{6,4},{7,5},{8,10},{9,11},{10,... | collective-permute-start | bytes 147464 | tf_op jit(solution)/shard_map/ppermute | solution.py:328
  15.5 12.3 %all-to-all-start = ((f32[32,2,256]{2,1,0:T(2,128)}), f32[32,2,256]{2,1,0:T(2,128)S(1)}, u32[]{:S(2)}, u32[]{:S(2)}) async-start(f32[32,2,256]{2,1,0:T(2,128)} %get-tuple-element.24), calls=%async_computation | async-start | bytes 131072 | tf_op jit(solution)/shard_map/all_to_all | solution.py:350
  20.4 10.7 %collective-permute-start.5 = (bf16[2,1,96,256]{3,2,1,0:T(8,128)(2,1)S(1)}, bf16[2,1,96,256]{3,2,1,0:T(8,128)(2,1)S(1)}, u32[]{:S(2)}, u32[]{:S(2)}) collective-permute-start(bf16[2,1,96,256]{3,2,1,0:T(8,128)(2,1)S(1)} %pad_maximum_fusion), channel_id=1, source_target_pairs={{0,1},{1,0},{2,3},{3,2},{4,5},{5,4},{6,7},{7,6},{8,9},{9,8},{10,11... | collective-permute-start | bytes 294920 | tf_op jit(solution)/shard_map/ppermute | solution.py:328
  27.9 2.2 %copy-start.1 = (bf16[2,4,2,512,256]{4,3,2,1,0:T(8,128)(2,1)S(1)}, bf16[2,4,2,512,256]{4,3,2,1,0:T(8,128)(2,1)}, u32[]{:S(2)}) copy-start(bf16[2,4,2,512,256]{4,3,2,1,0:T(8,128)(2,1)} %copy-done) | copy-start | bytes 12582916

commit v9 on v6

--- a/solution.py
+++ b/solution.py
@@ -161,9 +161,10 @@
     for m in range(2 * half):
         if m < half:
             total, copies = quarter_ref[m].astype(F32), freq_size // 4
+            total_ref[m, b_ref.shape[1] :] = total
         else:
             total, copies = b_ref[m - half].astype(F32) + b_their_ref[m - half].astype(F32), freq_size // 2
-            total_ref[m - half] = total
+            total_ref[m - half, : b_ref.shape[1]] = total
         keep = keep_ref[m : m + 1]
         power = keep * jnp.sum(total * total, axis=0, keepdims=True) * F32(1.0 / copies)
         stats += jnp.concatenate([power, keep * F32(1.0 / freq_size)], axis=0)
@@ -177,7 +178,7 @@
         in_specs=[VMEM] * 4,
         out_specs=[VMEM] * 2,
         out_shape=[
-            jax.ShapeDtypeStruct(mine.shape, F32),
+            jax.ShapeDtypeStruct((mine.shape[0], mine.shape[1] + quarter.shape[1], kmax), F32),
             jax.ShapeDtypeStruct((peers, 2, kmax), F32),
         ],
         name="power",
@@ -205,20 +206,22 @@
 def pieces(m, c, y, quarters, mine_ref, other_ref):
     half = mine_ref.shape[0]
     if m < half:
-        own, core, chip, both = [q[m].astype(F32) for q in quarters]
+        own, chip, both = [q[m].astype(F32) for q in quarters]
         rows = own.shape[0]
+        core = other_ref[m, 2 * rows :]
         for c_of in range(2):
             near, far = jnp.where(c == c_of, own, core), jnp.where(c == c_of, chip, both)
             for y_of in range(2):
                 yield (2 * c_of + y_of) * rows, jnp.where(y == y_of, near, far)
     else:
-        mine, other = mine_ref[m - half], other_ref[m - half]
+        rows = 2 * quarters[0].shape[1]
+        mine, other = mine_ref[m - half, :rows], other_ref[m - half, :rows]
         for c_of in range(2):
             yield c_of * mine.shape[0], jnp.where(c == c_of, mine, other)
 
 
 def back_kernel(
-    keep_ref, scale_ref, q0_ref, q1_ref, q2_ref, q3_ref, mine_ref, other_ref, e_ref, coef_hbm, out_hbm, pair, flat, coef_buf, out_buf, coef_sem, out_sem
+    keep_ref, scale_ref, q0_ref, q2_ref, q3_ref, mine_ref, other_ref, e_ref, coef_hbm, out_hbm, pair, flat, coef_buf, out_buf, coef_sem, out_sem
 ):
     modes, freqs, samples, _, base = out_buf.shape
     kmax = mine_ref.shape[-1]
@@ -233,7 +236,7 @@
 
     for m in range(modes):
         gain = keep_ref[m : m + 1] * scale_ref[...]
-        for start, proj in pieces(m, side(), side(1), (q0_ref, q1_ref, q2_ref, q3_ref), mine_ref, other_ref):
+        for start, proj in pieces(m, side(), side(1), (q0_ref, q2_ref, q3_ref), mine_ref, other_ref):
             coef = proj * gain
             at = slice(start, start + coef.shape[0])
             pair[at, :kmax] = coef.astype(BF16)
@@ -257,10 +260,10 @@
 
 def back(keep, scale, quarters, mine, other, e):
     modes, freqs, _, base, kmax = e.shape
-    samples = mine.shape[1]
+    samples = 2 * quarters[0].shape[1]
     return pl.pallas_call(
         back_kernel,
-        in_specs=[VMEM] * 9,
+        in_specs=[VMEM] * 8,
         out_specs=[HBM, HBM],
         out_shape=[
             jax.ShapeDtypeStruct((modes, 2, samples, kmax), BF16),
@@ -305,7 +308,7 @@
     quarter = quarter.astype(BF16)
     total, theirs = over_chips((keep_b + swap(give_b, 1).astype(F32)).astype(BF16))
     quarters = [quarter]
-    for bits in (1, 2, 3):
+    for bits in (2, 3):
         quarters.append(swap(quarter, bits))
     mine, stats = power_of(keep, freq_size, quarter, total, theirs, ma_size * freq_size)
     other = swap(mine, 1)

time: 34.3 us -> 34.3 us (level)
    ppermute x8 -> x7, starting transfers between devices: 6.42 us -> 6.42 us  [swap(): return lax.ppermute(x, 'freq', [(i, i ^ bit) for i in range(freq_size)])]
    ppermute x8 -> x7, waiting for transfers between devices: 3.85 us -> 3.85 us  [swap(): return lax.ppermute(x, 'freq', [(i, i ^ bit) for i in range(freq_size)])]
  transfers between devices with their start and end apart: 9 -> 8, of which waited for: 3 -> 3; matrix products, arithmetic and copies ran while one was open for 0% -> 0% of each run, Pallas kernels for 1% -> 1%
where the time goes in v9:
time: 34.3 us; the launch traced here: 34.1 us
  starting transfers between devices  12.3 us (36%)
  waiting for transfers between devices  9.31 us (27%)
  Pallas kernels  7.44 us (22%)
  local copies, waits for them, and re-layouts  4.13 us (12%)
  between operations  0.73 us (2%)
    ppermute x7, starting transfers between devices, swap(): return lax.ppermute(x, 'freq', [(i, i ^ bit) for i in range(freq_size)])  6.42 us
    all_to_all x1, starting transfers between devices, filter_modes(): lax.all_to_all(stats, ('ma', 'freq'), 0, 0, tiled=True)  5.93 us
    all_to_all x1, waiting for transfers between devices, filter_modes(): lax.all_to_all(stats, ('ma', 'freq'), 0, 0, tiled=True)  5.46 us
    unnamed x6, local copies, waits for them, and re-layouts  4.13 us
    ppermute x7, waiting for transfers between devices, swap(): return lax.ppermute(x, 'freq', [(i, i ^ bit) for i in range(freq_size)])  3.85 us
    pallas_call x1, Pallas kernels, project(): pl.pallas_call(project_kernel, in_specs=[HBM, HBM], out_specs=[VMEM] * 5,...  3.45 us
    pallas_call x1, Pallas kernels, back(): pl.pallas_call(back_kernel, in_specs=[VMEM] * 8, out_specs=[HBM, HBM], ou...  2.78 us
    pallas_call x1, Pallas kernels, power_of(): pl.pallas_call(functools.partial(power_kernel, freq_size), in_specs=[VMEM...  0.72 us
  transfers between devices with their start and end apart: 8, of which 3 were waited for; matrix products, arithmetic and copies ran while one was open for 0% of the time, Pallas kernels for 1%

profile of v9, /device:TPU:0, one launch (start us, length us, event | category | flops | bytes accessed | tf_op | source)
XLA Modules:
  0.0 34.1 jit_solution(14327656853768506537)
XLA Ops:
  0.6 3.4 %project.1 = (bf16[1,192,256]{2,1,0:T(8,128)(2,1)S(1)}, f32[1,192,256]{2,1,0:T(8,128)S(1)}, f32[1,2,384,256]{3,2,1,0:T(8,128)S(1)}, bf16[1,192,2,512]{3,2,1,0:T(2,128)(2,1)S(1)}, bf16[2,4,2,512,256]{4,3,2,1,0:T(8,128)(2,1)S(1)}) custom-call(bf16[2,192,4,2,512]{4,3,2,1,0:T(2,128)(2,1)} %v_hbm.1, bf16[2,4,2,512,256]{4,3,2,1,0:T(8,128)(2,1)} %e_hbm.1), custom_call_target="tpu_custom_call" | custom-call | flops 1610612736 | bytes 7340032 | tf_op jit(solution)/shard_map/project/pallas_call | solution.py:84
  4.1 0.0 copy-start.2
  4.1 0.6 %collective-permute-start = (bf16[1,192,256]{2,1,0:T(8,128)(2,1)S(1)}, bf16[1,192,256]{2,1,0:T(8,128)(2,1)S(1)}, u32[]{:S(2)}, u32[]{:S(2)}) collective-permute-start(bf16[1,192,256]{2,1,0:T(8,128)(2,1)S(1)} %get-tuple-element.14), channel_id=1, source_target_pairs={{0,1},{1,0},{2,3},{3,2},{4,5},{5,4},{6,7},{7,6},{8,9},{9,8},{10,11... | collective-permute-start | bytes 294920 | tf_op jit(solution)/shard_map/ppermute | solution.py:291
  4.7 0.4 %rest.1 = (bf16[1,192,256]{2,1,0:T(8,128)(2,1)S(1)}, f32[1,192,256]{2,1,0:T(8,128)S(1)}) custom-call(f32[1,2,384,256]{3,2,1,0:T(8,128)S(1)} %get-tuple-element.17.part_ref, bf16[1,192,2,512]{3,2,1,0:T(2,128)(2,1)S(1)} %get-tuple-element.18.v_ref, bf16[2,4,2,512,256]{4,3,2,1,0:T(8,128)(2,1)S(1)} %get-tuple-element.19.e_ref), custom_call_target="tpu_custom_call" | custom-call | flops 201326592 | bytes 393216 | tf_op jit(solution)/shard_map/rest/pallas_call | solution.py:120
  5.1 0.0 copy-start
  5.1 1.9 %copy-done = bf16[2,4,2,512,256]{4,3,2,1,0:T(8,128)(2,1)} copy-done((bf16[2,4,2,512,256]{4,3,2,1,0:T(8,128)(2,1)}, bf16[2,4,2,512,256]{4,3,2,1,0:T(8,128)(2,1)S(1)}, u32[]{:S(2)}) %copy-start) | copy-done | bytes 4194328
  7.0 0.0 collective-permute-start.2
  7.1 0.0 copy-done.2
  7.1 0.1 compare_convert_fusion.keep_ref
  7.1 0.0 collective-permute-done.theirs_ref
  7.2 3.1 %collective-permute-start.1 = (bf16[1,96,256]{2,1,0:T(8,128)(2,1)S(1)}, bf16[1,96,256]{2,1,0:T(8,128)(2,1)S(1)}, u32[]{:S(2)}, u32[]{:S(2)}) collective-permute-start(bf16[1,96,256]{2,1,0:T(8,128)(2,1)S(1)} %get-tuple-element.16), channel_id=1, source_target_pairs={{0,2},{1,3},{2,0},{3,1},{4,6},{5,7},{6,4},{7,5},{8,10},{9,11},{10,... | collective-permute-start | bytes 147464 | tf_op jit(solution)/shard_map/ppermute | solution.py:291
  10.2 0.0 collective-permute-done.2
  10.3 0.8 %collective-permute-start.3 = (bf16[1,192,256]{2,1,0:T(8,128)(2,1)S(1)}, bf16[1,192,256]{2,1,0:T(8,128)(2,1)S(1)}, u32[]{:S(2)}, u32[]{:S(2)}) collective-permute-start(bf16[1,192,256]{2,1,0:T(8,128)(2,1)S(1)} %add_convert_fusion.b_ref), channel_id=1, source_target_pairs={{0,2},{1,3},{2,0},{3,1},{4,6},{5,7},{6,4},{7,5},{8,10},{9,11},{10,... | collective-permute-start | bytes 294920 | tf_op jit(solution)/shard_map/ppermute | solution.py:291
  11.1 1.2 %collective-permute-done.1 = bf16[1,96,256]{2,1,0:T(8,128)(2,1)S(1)} collective-permute-done((bf16[1,96,256]{2,1,0:T(8,128)(2,1)S(1)}, bf16[1,96,256]{2,1,0:T(8,128)(2,1)S(1)}, u32[]{:S(2)}, u32[]{:S(2)}) %collective-permute-start.1) | collective-permute-done | bytes 49184 | tf_op jit(solution)/shard_map/ppermute | solution.py:291
  12.3 2.6 %collective-permute-done.3.b_their_ref = bf16[1,192,256]{2,1,0:T(8,128)(2,1)S(1)} collective-permute-done((bf16[1,192,256]{2,1,0:T(8,128)(2,1)S(1)}, bf16[1,192,256]{2,1,0:T(8,128)(2,1)S(1)}, u32[]{:S(2)}, u32[]{:S(2)}) %collective-permute-start.3) | collective-permute-done | bytes 98336 | tf_op jit(solution)/shard_map/ppermute | solution.py:291
  14.9 0.7 %power.1 = (f32[1,288,256]{2,1,0:T(8,128)S(1)}, f32[32,2,256]{2,1,0:T(2,128)}) custom-call(f32[2,256]{1,0:T(2,128)S(1)} %compare_convert_fusion.keep_ref, bf16[1,96,256]{2,1,0:T(8,128)(2,1)S(1)} %add_convert_fusion.1.quarter_ref.q0_ref, bf16[1,192,256]{2,1,0:T(8,128)(2,1)S(1)} %add_convert_fusion.b_ref, ...), custom_call_target="tpu_custom_call" | custom-call | tf_op jit(solution)/shard_map/power/pallas_call | solution.py:176
  15.7 0.0 collective-permute-start.6
  15.7 5.9 %all-to-all-start = ((f32[32,2,256]{2,1,0:T(2,128)}), f32[32,2,256]{2,1,0:T(2,128)S(1)}, u32[]{:S(2)}, u32[]{:S(2)}) async-start(f32[32,2,256]{2,1,0:T(2,128)} %get-tuple-element.22), calls=%async_computation | async-start | bytes 131072 | tf_op jit(solution)/shard_map/all_to_all | solution.py:315
  21.6 1.6 %collective-permute-start.5 = (bf16[1,96,256]{2,1,0:T(8,128)(2,1)S(1)}, bf16[1,96,256]{2,1,0:T(8,128)(2,1)S(1)}, u32[]{:S(2)}, u32[]{:S(2)}) collective-permute-start(bf16[1,96,256]{2,1,0:T(8,128)(2,1)S(1)} %add_convert_fusion.1.quarter_ref.q0_ref), channel_id=1, source_target_pairs={{0,3},{1,2},{2,1},{3,0},{4,7},{5,6},{6,5},{7,4},{8,11},{9,10},{10,... | collective-permute-start | bytes 147464 | tf_op jit(solution)/shard_map/ppermute | solution.py:291
  23.1 0.4 %collective-permute-start.4 = (bf16[1,96,256]{2,1,0:T(8,128)(2,1)S(1)}, bf16[1,96,256]{2,1,0:T(8,128)(2,1)S(1)}, u32[]{:S(2)}, u32[]{:S(2)}) collective-permute-start(bf16[1,96,256]{2,1,0:T(8,128)(2,1)S(1)} %add_convert_fusion.1.quarter_ref.q0_ref), channel_id=1, source_target_pairs={{0,2},{1,3},{2,0},{3,1},{4,6},{5,7},{6,4},{7,5},{8,10},{9,11},{10,... | collective-permute-start | bytes 147464 | tf_op jit(solution)/shard_map/ppermute | solution.py:291
  23.5 5.5 %all-to-all-done.stats_ref = f32[32,2,256]{2,1,0:T(2,128)S(1)} async-done(((f32[32,2,256]{2,1,0:T(2,128)}), f32[32,2,256]{2,1,0:T(2,128)S(1)}, u32[]{:S(2)}, u32[]{:S(2)}) %all-to-all-start) | async-done | bytes 65568 | tf_op jit(solution)/shard_map/all_to_all | solution.py:315
  29.0 0.1 pool.1.scale_ref
  29.1 0.0 collective-permute-done.5.q3_ref
  29.1 0.0 collective-permute-done.4.q2_ref
  29.1 0.0 collective-permute-done.6.other_ref
  29.1 0.0 copy-start.1
  29.1 2.2 %copy-done.1 = bf16[2,4,2,512,256]{4,3,2,1,0:T(8,128)(2,1)S(1)} copy-done((bf16[2,4,2,512,256]{4,3,2,1,0:T(8,128)(2,1)S(1)}, bf16[2,4,2,512,256]{4,3,2,1,0:T(8,128)(2,1)}, u32[]{:S(2)}) %copy-start.1) | copy-done | bytes 4194328
  31.3 2.8 %back.1 = (bf16[2,2,192,256]{3,2,1,0:T(8,128)(2,1)}, bf16[2,192,4,2,512]{4,3,2,1,0:T(2,128)(2,1)}) custom-call(f32[2,256]{1,0:T(2,128)S(1)} %compare_convert_fusion.keep_ref, f32[1,256]{1,0:T(1,128)S(1)} %pool.1.scale_ref, bf16[1,96,256]{2,1,0:T(8,128)(2,1)S(1)} %add_convert_fusion.1.quarter_ref.q0_ref, ...), custom_call_target="tpu_custom_call" | custom-call | tf_op jit(solution)/shard_map/back/pallas_call | solution.py:264
  (3 shorter events, 0.1 us)
Async XLA Ops:
  4.1 3.0 %copy-start.2 = (s32[2]{0:T(128)S(1)}, s32[2]{0:T(128)}, u32[]{:S(2)}) copy-start(s32[2]{0:T(128)} %param.5) | copy-start | bytes 28
  4.1 3.0 %collective-permute-start = (bf16[1,192,256]{2,1,0:T(8,128)(2,1)S(1)}, bf16[1,192,256]{2,1,0:T(8,128)(2,1)S(1)}, u32[]{:S(2)}, u32[]{:S(2)}) collective-permute-start(bf16[1,192,256]{2,1,0:T(8,128)(2,1)S(1)} %get-tuple-element.14), channel_id=1, source_target_pairs={{0,1},{1,0},{2,3},{3,2},{4,5},{5,4},{6,7},{7,6},{8,9},{9,8},{10,11... | collective-permute-start | bytes 294920 | tf_op jit(solution)/shard_map/ppermute | solution.py:291
  5.1 2.0 %copy-start = (bf16[2,4,2,512,256]{4,3,2,1,0:T(8,128)(2,1)}, bf16[2,4,2,512,256]{4,3,2,1,0:T(8,128)(2,1)S(1)}, u32[]{:S(2)}) copy-start(bf16[2,4,2,512,256]{4,3,2,1,0:T(8,128)(2,1)S(1)} %get-tuple-element.19.e_ref) | copy-start | bytes 12582916
  7.0 3.2 %collective-permute-start.2 = (bf16[1,192,256]{2,1,0:T(8,128)(2,1)S(1)}, bf16[1,192,256]{2,1,0:T(8,128)(2,1)S(1)}, u32[]{:S(2)}, u32[]{:S(2)}) collective-permute-start(bf16[1,192,256]{2,1,0:T(8,128)(2,1)S(1)} %get-tuple-element.21), channel_id=1, source_target_pairs={{0,1},{1,0},{2,3},{3,2},{4,5},{5,4},{6,7},{7,6},{8,9},{9,8},{10,11... | collective-permute-start | bytes 294920 | tf_op jit(solution)/shard_map/ppermute | solution.py:291
  7.2 5.1 %collective-permute-start.1 = (bf16[1,96,256]{2,1,0:T(8,128)(2,1)S(1)}, bf16[1,96,256]{2,1,0:T(8,128)(2,1)S(1)}, u32[]{:S(2)}, u32[]{:S(2)}) collective-permute-start(bf16[1,96,256]{2,1,0:T(8,128)(2,1)S(1)} %get-tuple-element.16), channel_id=1, source_target_pairs={{0,2},{1,3},{2,0},{3,1},{4,6},{5,7},{6,4},{7,5},{8,10},{9,11},{10,... | collective-permute-start | bytes 147464 | tf_op jit(solution)/shard_map/ppermute | solution.py:291
  10.3 4.7 %collective-permute-start.3 = (bf16[1,192,256]{2,1,0:T(8,128)(2,1)S(1)}, bf16[1,192,256]{2,1,0:T(8,128)(2,1)S(1)}, u32[]{:S(2)}, u32[]{:S(2)}) collective-permute-start(bf16[1,192,256]{2,1,0:T(8,128)(2,1)S(1)} %add_convert_fusion.b_ref), channel_id=1, source_target_pairs={{0,2},{1,3},{2,0},{3,1},{4,6},{5,7},{6,4},{7,5},{8,10},{9,11},{10,... | collective-permute-start | bytes 294920 | tf_op jit(solution)/shard_map/ppermute | solution.py:291
  15.7 13.4 %collective-permute-start.6 = (f32[1,288,256]{2,1,0:T(8,128)S(1)}, f32[1,288,256]{2,1,0:T(8,128)S(1)}, u32[]{:S(2)}, u32[]{:S(2)}) collective-permute-start(f32[1,288,256]{2,1,0:T(8,128)S(1)} %get-tuple-element.23.mine_ref), channel_id=1, source_target_pairs={{0,1},{1,0},{2,3},{3,2},{4,5},{5,4},{6,7},{7,6},{8,9},{9,8},{10,11... | collective-permute-start | bytes 884744 | tf_op jit(solution)/shard_map/ppermute | solution.py:291
  15.7 13.3 %all-to-all-start = ((f32[32,2,256]{2,1,0:T(2,128)}), f32[32,2,256]{2,1,0:T(2,128)S(1)}, u32[]{:S(2)}, u32[]{:S(2)}) async-start(f32[32,2,256]{2,1,0:T(2,128)} %get-tuple-element.22), calls=%async_computation | async-start | bytes 131072 | tf_op jit(solution)/shard_map/all_to_all | solution.py:315
  21.6 7.5 %collective-permute-start.5 = (bf16[1,96,256]{2,1,0:T(8,128)(2,1)S(1)}, bf16[1,96,256]{2,1,0:T(8,128)(2,1)S(1)}, u32[]{:S(2)}, u32[]{:S(2)}) collective-permute-start(bf16[1,96,256]{2,1,0:T(8,128)(2,1)S(1)} %add_convert_fusion.1.quarter_ref.q0_ref), channel_id=1, source_target_pairs={{0,3},{1,2},{2,1},{3,0},{4,7},{5,6},{6,5},{7,4},{8,11},{9,10},{10,... | collective-permute-start | bytes 147464 | tf_op jit(solution)/shard_map/ppermute | solution.py:291
  23.1 5.9 %collective-permute-start.4 = (bf16[1,96,256]{2,1,0:T(8,128)(2,1)S(1)}, bf16[1,96,256]{2,1,0:T(8,128)(2,1)S(1)}, u32[]{:S(2)}, u32[]{:S(2)}) collective-permute-start(bf16[1,96,256]{2,1,0:T(8,128)(2,1)S(1)} %add_convert_fusion.1.quarter_ref.q0_ref), channel_id=1, source_target_pairs={{0,2},{1,3},{2,0},{3,1},{4,6},{5,7},{6,4},{7,5},{8,10},{9,11},{10,... | collective-permute-start | bytes 147464 | tf_op jit(solution)/shard_map/ppermute | solution.py:291
  29.1 2.2 %copy-start.1 = (bf16[2,4,2,512,256]{4,3,2,1,0:T(8,128)(2,1)S(1)}, bf16[2,4,2,512,256]{4,3,2,1,0:T(8,128)(2,1)}, u32[]{:S(2)}) copy-start(bf16[2,4,2,512,256]{4,3,2,1,0:T(8,128)(2,1)} %copy-done) | copy-start | bytes 12582916
